TPU v7x, 256 devices: a whole 4x4x8 slice. The times are simulated.
256 devices in a mesh: blk: 16 (over x_lo, y, core), walk: 16 (over x_hi, z).
Axes of the slice: x: 4 (x_hi: 2, x_lo: 2; x = x_hi * 2 + x_lo), y: 4, z: 8, core: 2. Of those that a mesh axis runs over, the one named last changes fastest.
Arguments:
- walkers: bfloat16 [512, 200, 2048], P(('blk', 'walk')), may hold values from -6 to 6
- inv_intersection: bfloat16 [512, 2, 100, 100], P(('blk', 'walk')), may hold values from -0.625 to 0.625
- rotated_chol: bfloat16 [32, 100, 2048], P('blk'), may hold values from -0.013671875 to 0.013671875
- full_chol: bfloat16 [32, 2048, 2048], P('walk', 'blk'), may hold values from -0.125 to 0.125
- field_noise: float32 [32], replicated, may hold values from -4 to 4
Outputs:
- propagated: bfloat16 [512, 200, 2048], P(('blk', 'walk'))
- force_bias: float32 [512, 32], P(('blk', 'walk'))
- bias_shift: float32 [32], replicated
All inputs are finite; a program needn't handle non-finite values.
Results may differ from a plain program's by a relative error of at most 0.0065.
Values may be sent and summed in bfloat16 or wider, within the bound.
No kernel may reach another device: no remote copies, remote signals or barrier semaphores. Data moves between devices by JAX's collectives and lax.ppermute only.
A program may use at most 128 MiB of HBM per device.

v0:
```python
import functools
import math

import jax
import jax.numpy as jnp
from jax import lax
from jax.sharding import Mesh
from jax.sharding import PartitionSpec as P

BLK = ("blk_0", "blk_1", "blk_2")
WALK = ("walk_0", "walk_1")
BLK_WALK = ("blk_0", "blk_1", "blk_2", "walk_0", "walk_1")


time_root = 0.1


def by_axis(array, axes):
    return functools.reduce(lax.psum, axes, array)


def in_blocks(array, dim, count):
    before, after = (array.shape[:dim], array.shape[dim + 1 :])
    return jnp.moveaxis(array.reshape(*before, count, -1, *after), dim, 0)


def sent_and_summed(array, axis, dim):
    blocks = in_blocks(array, dim, lax.axis_size(axis))
    arrived = lax.all_to_all(blocks, axis, split_axis=0, concat_axis=0, tiled=True)
    return arrived.sum(axis=0)


def sent_to_all(array, axis):
    count = lax.axis_size(axis)
    return lax.all_to_all(
        jnp.broadcast_to(array[None], (count, *array.shape)), axis, 0, 0, tiled=True
    )


def in_order(blocks, dim):
    blocks = jnp.moveaxis(blocks, 0, dim)
    shape = blocks.shape
    return blocks.reshape(*shape[:dim], shape[dim] * shape[dim + 1], *shape[dim + 2 :])


def gather_directly(array, axis, dim):
    blocks = sent_to_all(array, axis)
    return in_order(blocks, dim)


def local(walkers, inv_intersection, rotated_chol, full_chol, field_noise):
    wdev_count, double_rows, orbitals = walkers.shape
    occupied = double_rows // 2
    spins = walkers.reshape(wdev_count, 2, occupied, orbitals)
    theta = jnp.einsum(
        "wsij,wsjp->wip", inv_intersection, spins, preferred_element_type=jnp.float32
    ).astype(jnp.bfloat16)
    flat_theta = theta.reshape(wdev_count, occupied * orbitals)
    piece = lax.all_gather(rotated_chol, BLK, axis=0, tiled=True)
    flat_piece = piece.reshape(piece.shape[0], occupied * orbitals)
    part_bias = lax.dot_general(
        flat_theta, flat_piece, (((1,), (1,)), ((), ())), preferred_element_type=jnp.float32
    )
    total_walkers = wdev_count * lax.axis_size(BLK) * lax.axis_size(WALK)
    bias_shift = by_axis(jnp.sum(part_bias, axis=0), BLK_WALK) / math.sqrt(total_walkers)
    shifted = field_noise - bias_shift
    local_count = full_chol.shape[0]
    local_shift = lax.dynamic_slice_in_dim(shifted, lax.axis_index(WALK) * local_count, local_count)
    partial_value = time_root * jnp.tensordot(
        local_shift, full_chol.astype(jnp.float32), axes=1, precision=lax.Precision.HIGHEST
    )
    narrow = sent_and_summed(partial_value, WALK, 1).astype(jnp.bfloat16)
    row_block = gather_directly(narrow, WALK, 1)
    field = lax.all_gather(row_block, BLK, axis=0, tiled=True)
    current = walkers.reshape(wdev_count * double_rows, orbitals)
    total = current.astype(jnp.float32)
    for order in range(1, 5):
        current = (jnp.dot(current, field, preferred_element_type=jnp.float32) / order).astype(
            jnp.bfloat16
        )
        total = total + current.astype(jnp.float32)
    propagated = total.astype(jnp.bfloat16).reshape(wdev_count, double_rows, orbitals)
    return (propagated, part_bias, bias_shift)


def solution(mesh):
    torus = Mesh(
        mesh.devices.reshape(2, 4, 2, 2, 8), ("blk_0", "blk_1", "blk_2", "walk_0", "walk_1")
    )
    in_specs = (
        P(BLK_WALK, None, None),
        P(BLK_WALK, None, None, None),
        P(BLK, None, None),
        P(WALK, BLK, None),
        P(),
    )
    out_specs = (P(BLK_WALK, None, None), P(BLK_WALK, None), P())
    return jax.shard_map(local, mesh=torus, in_specs=in_specs, out_specs=out_specs, check_vma=False)
```

profile of v0, /device:TPU:1, one launch (start us, length us, event | category | flops | bytes accessed | tf_op | source)
XLA Modules:
  0.0 296.6 jit_solution(11933287155726860161)
XLA Ops:
  7.2 2.4 copy.18
  9.7 1.6 reshape.27
  11.3 1.4 fusion.6
  12.7 81.3 %all-gather.3.cloned.1.call-done = bf16[32,100,2048]{2,1,0:T(8,128)(2,1)} async-done(((bf16[2,100,2048]{2,1,0:T(8,128)(2,1)}), bf16[32,100,2048]{2,1,0:T(8,128)(2,1)}) %all-gather.3.cloned.1.call-update) | async-done | bytes 13107216 | tf_op jit(solution)/shard_map/all_gather | solution.py:59
  93.9 22.6 %fusion.15 = (f32[32]{0:T(128)S(1)}, f32[2,32]{1,0:T(2,128)}) fusion(bf16[32,100,2048]{2,1,0:T(8,128)(2,1)} %all-gather.3.cloned.1.call-done, bf16[2,100,2048]{2,1,0:T(8,128)(2,1)} %fusion.6), kind=kOutput, calls=%fused_computation.22 | convolution fusion | flops 26214432 | bytes 13926784 | tf_op jit(solution)/shard_map/dot_general | solution.py:61
  116.5 3.8 %psum.35 = f32[32]{0:T(128)S(1)} all-reduce(f32[32]{0:T(128)S(1)} %get-tuple-element.5), channel_id=1, replica_groups=mesh['blk_0'=2,'blk_1'=4,'blk_2'=2,'walk_0'=2,'walk_1'=8] {'blk_0'}, use_global_device_ids=true, to_apply=%region_1.0 | all-reduce | flops 32 | bytes 256 | tf_op jit(solution)/shard_map/psum | solution.py:19
  120.3 8.4 %psum.36 = f32[32]{0:T(128)S(1)} all-reduce(f32[32]{0:T(128)S(1)} %psum.35), channel_id=1, replica_groups=mesh['blk_0'=2,'blk_1'=4,'blk_2'=2,'walk_0'=2,'walk_1'=8] {'blk_1'}, use_global_device_ids=true, to_apply=%region_2.0 | all-reduce | flops 32 | bytes 256 | tf_op jit(solution)/shard_map/psum | solution.py:19
  128.7 5.5 %psum.37 = f32[32]{0:T(128)S(1)} all-reduce(f32[32]{0:T(128)S(1)} %psum.36), channel_id=1, replica_groups=mesh['blk_0'=2,'blk_1'=4,'blk_2'=2,'walk_0'=2,'walk_1'=8] {'blk_2'}, use_global_device_ids=true, to_apply=%region_3.0 | all-reduce | flops 32 | bytes 256 | tf_op jit(solution)/shard_map/psum | solution.py:19
  134.2 5.3 %psum.38 = f32[32]{0:T(128)S(1)} all-reduce(f32[32]{0:T(128)S(1)} %psum.37), channel_id=1, replica_groups=mesh['blk_0'=2,'blk_1'=4,'blk_2'=2,'walk_0'=2,'walk_1'=8] {'walk_0'}, use_global_device_ids=true, to_apply=%region_4.0 | all-reduce | flops 32 | bytes 256 | tf_op jit(solution)/shard_map/psum | solution.py:19
  139.5 13.7 %psum.39 = f32[32]{0:T(128)S(1)} all-reduce(f32[32]{0:T(128)S(1)} %psum.38), channel_id=1, replica_groups=mesh['blk_0'=2,'blk_1'=4,'blk_2'=2,'walk_0'=2,'walk_1'=8] {'walk_1'}, use_global_device_ids=true, to_apply=%region_5.0 | all-reduce | flops 32 | bytes 256 | tf_op jit(solution)/shard_map/psum | solution.py:19
  153.2 0.5 fusion.14
  153.7 3.7 %fusion.10 = f32[1,128,2048]{2,0,1:T(1,128)S(1)} fusion(bf16[2,128,2048]{2,1,0:T(8,128)(2,1)S(1)} %copy-done, f32[32]{0:T(128)S(1)} %get-tuple-element.3, s32[]{:T(128)S(6)} %select_n.3), kind=kOutput, calls=%fused_computation.15 | convolution fusion | flops 6291456 | bytes 2097284 | tf_op jit(solution)/shard_map/dot_general | solution.py:69
  157.4 0.7 copy.25
  158.2 0.1 bitcast_multiply_fusion
  158.3 0.3 copy.21
  158.6 27.7 %all_to_all.10 = f32[16,128,128]{2,1,0:T(8,128)S(1)} all-to-all(f32[16,128,128]{2,1,0:T(8,128)S(1)} %copy.21), channel_id=1, replica_groups=mesh['blk_0'=2,'blk_1'=4,'blk_2'=2,'walk_0'=2,'walk_1'=8] {'walk_0','wal..., dimensions={0} | all-to-all | bytes 2097152 | tf_op jit(solution)/shard_map/all_to_all | solution.py:29
  186.4 0.1 copy.22
  186.5 0.1 broadcast_in_dim.2
  186.6 19.3 %all_to_all.11 = bf16[16,128,128]{1,2,0:T(8,128)(2,1)} all-to-all(bf16[16,128,128]{1,2,0:T(8,128)(2,1)S(1)} %broadcast_in_dim.2), channel_id=1, replica_groups=mesh['blk_0'=2,'blk_1'=4,'blk_2'=2,'walk_0'=2,'walk_1'=8] {'walk_0','wal..., dimensions={0} | all-to-all | bytes 1048576 | tf_op jit(solution)/shard_map/all_to_all | solution.py:35
  206.0 63.8 %all-gather.5.cloned.1.call-done = bf16[2048,2048]{0,1:T(8,128)(2,1)} async-done(((bf16[128,2048]{0,1:T(8,128)(2,1)}), bf16[2048,2048]{0,1:T(8,128)(2,1)}) %all-gather.5.cloned.1.call-update) | async-done | bytes 8388624 | tf_op jit(solution)/shard_map/all_gather | solution.py:74
  269.8 7.5 %convolution_convert_fusion = bf16[2048,400]{0,1:T(8,128)(2,1)S(1)} fusion(bf16[2048,2048]{0,1:T(8,128)(2,1)} %all-gather.5.cloned.1.call-done, bf16[400,2048]{1,0:T(8,128)(2,1)} %bitcast.41), kind=kOutput, calls=%fused_computation.10 | convolution fusion | flops 3356262400 | bytes 11665408 | tf_op jit(solution)/shard_map/dot_general | solution.py:78
  277.3 3.6 %multiply_convert_fusion.2 = bf16[400,2048]{1,0:T(8,128)(2,1)S(1)} fusion(bf16[2048,400]{0,1:T(8,128)(2,1)S(1)} %convolution_convert_fusion, bf16[2048,2048]{0,1:T(8,128)(2,1)S(1)} %copy-done.4), kind=kOutput, calls=%fused_computation.9 | convolution fusion | flops 3357081600 | bytes 11665408 | tf_op jit(solution)/shard_map/dot_general | solution.py:78
  281.0 3.6 %multiply_convert_fusion.1 = bf16[400,2048]{1,0:T(8,128)(2,1)S(1)} fusion(bf16[400,2048]{1,0:T(8,128)(2,1)S(1)} %multiply_convert_fusion.2, bf16[2048,2048]{0,1:T(8,128)(2,1)S(1)} %copy-done.4), kind=kOutput, calls=%fused_computation.8 | convolution fusion | flops 3357081600 | bytes 11665408 | tf_op jit(solution)/shard_map/dot_general | solution.py:78
  284.6 5.2 %fusion.5 = bf16[400,2048]{1,0:T(8,128)(2,1)} fusion(bf16[2048,400]{0,1:T(8,128)(2,1)S(1)} %convolution_convert_fusion, bf16[400,2048]{1,0:T(8,128)(2,1)S(1)} %multiply_convert_fusion.1, bf16[400,2048]{1,0:T(8,128)(2,1)S(1)} %multiply_convert_fusion.2, bf16[400,2048]{1,0:T(8,128)(2,1)S(1)} %bitcast.42, bf16[2048,2048]{0,1:T(8,128)(2,1)S(1)} %copy-done.4), kind=kOutput, calls=%fused_computation.6 | convolution fusion | flops 3365273600 | bytes 16580608 | tf_op jit(solution)/shard_map/dot_general | solution.py:78
  (15 shorter events, 0.2 us)
Async XLA Ops:
  7.2 146.5 %copy-start = (bf16[2,128,2048]{2,1,0:T(8,128)(2,1)S(1)}, bf16[2,128,2048]{2,1,0:T(8,128)(2,1)}, u32[]{:S(2)}) copy-start(bf16[2,128,2048]{2,1,0:T(8,128)(2,1)} %param.8) | copy-start | bytes 3145732
  7.2 4.1 %copy-start.2 = (bf16[2,2,100,100]{3,1,2,0:T(2,128)(2,1)S(1)}, bf16[2,2,100,100]{3,1,2,0:T(2,128)(2,1)}, u32[]{:S(2)}) copy-start(bf16[2,2,100,100]{3,1,2,0:T(2,128)(2,1)} %param.6) | copy-start | bytes 240004
  7.2 86.7 %all-gather.3.cloned.1.call-start = ((), (), s32[]{:S(2)}) async-start(), calls=%async_computation.2 | async-start | bytes 14483456 | tf_op jit(solution)/shard_map/all_gather | solution.py:59
  9.7 260.1 %all-gather.5.cloned.1.call-start = ((), (), s32[]{:S(2)}) async-start(), calls=%async_computation.3 | async-start | bytes 8912896 | tf_op jit(solution)/shard_map/all_gather | solution.py:74
  12.7 140.5 %copy-start.3 = (f32[32]{0:T(128)S(1)}, f32[32]{0:T(128)}, u32[]{:S(2)}) copy-start(f32[32]{0:T(128)} %param.9) | copy-start | bytes 388
  269.8 7.6 %copy-start.4 = (bf16[2048,2048]{0,1:T(8,128)(2,1)S(1)}, bf16[2048,2048]{0,1:T(8,128)(2,1)}, u32[]{:S(2)}) copy-start(bf16[2048,2048]{0,1:T(8,128)(2,1)} %all-gather.5.cloned.1.call-done) | copy-start | bytes 25165828
  280.9 3.6 %copy-start.1 = (bf16[2,200,2048]{2,1,0:T(8,128)(2,1)S(1)}, bf16[2,200,2048]{2,1,0:T(8,128)(2,1)}, u32[]{:S(2)}) copy-start(bf16[2,200,2048]{2,1,0:T(8,128)(2,1)} %param.5) | copy-start | bytes 4915204
Sparse Core Ops, SparseCore 0:
  10.4 83.4 all-gather.2
  206.1 63.6 all-gather.4
where the time goes:
time: 297 us
  waiting for transfers between devices  145 us (49%)
  blocking collectives  83.7 us (28%)
  matrix products  47.6 us (16%)
  between operations  14.2 us (5%)
  local copies, waits for them, and re-layouts  5.29 us (2%)
    all_gather x1, waiting for transfers between devices, local(): piece = lax.all_gather(rotated_chol, BLK, axis=0, tiled=True)  81.3 us
    all_gather x1, waiting for transfers between devices, local(): field = lax.all_gather(row_block, BLK, axis=0, tiled=True)  63.8 us
    psum x5, blocking collectives, by_axis(): return functools.reduce(lax.psum, axes, array)  36.6 us
    all_to_all x1, blocking collectives, sent_and_summed(): lax.all_to_all(blocks, axis, split_axis=0, concat_axis=0, tiled=True)  27.7 us
    dot_general x1, matrix products, local(): lax.dot_general(flat_theta, flat_piece, (((1,), (1,)), ((), ())), preferr...  22.6 us
    dot_general x4, matrix products, local(): jnp.dot(current, field, preferred_element_type=jnp.float32) / order  19.9 us
    all_to_all x1, blocking collectives, sent_to_all(): lax.all_to_all(jnp.broadcast_to(array[None], (count, *array.shape)), axis...  19.3 us
  transfers between devices with their start and end apart: 2, of which 2 were waited for; matrix products, arithmetic and copies ran while one was open for 1% of the time, Pallas kernels for 0%

commit v1 on v0

v1 whole, which is shorter than its diff:
```python
import math

import jax
import jax.numpy as jnp
from jax import lax
from jax.experimental import pallas as pl
from jax.experimental.pallas import tpu as pltpu
from jax.sharding import Mesh
from jax.sharding import PartitionSpec as P

BLK = ("blk_0", "blk_1", "blk_2")
WALK = ("walk_0", "walk_1")
ALL = BLK + WALK
ROWS = 16


def bias_kernel(theta_ref, chol_ref, out_ref):
    walkers, padded, lanes = theta_ref.shape
    vectors = chol_ref.shape[0]
    m, n = walkers * ROWS, vectors * ROWS
    total = jnp.zeros((m, n), jnp.float32)
    for t in range(padded // ROWS):
        a = theta_ref[:, t * ROWS : (t + 1) * ROWS, :].reshape(m, lanes)
        b = chol_ref[:, t * ROWS : (t + 1) * ROWS, :].reshape(n, lanes)
        total = total + lax.dot_general(
            a, b, (((1,), (1,)), ((), ())), preferred_element_type=jnp.float32
        )
    row = lax.broadcasted_iota(jnp.int32, (m, n), 0) % ROWS
    col = lax.broadcasted_iota(jnp.int32, (m, n), 1) % ROWS
    kept = jnp.where(row == col, total, 0.0)
    by_walker = kept.reshape(walkers, ROWS, n).sum(axis=1)
    group = lax.broadcasted_iota(jnp.int32, (n, vectors), 0) // ROWS
    vector = lax.broadcasted_iota(jnp.int32, (n, vectors), 1)
    pick = (group == vector).astype(jnp.float32)
    out_ref[...] = jnp.dot(
        by_walker, pick, preferred_element_type=jnp.float32, precision=lax.Precision.HIGHEST
    )


def partial_bias(theta, chol):
    walkers, vectors = theta.shape[0], chol.shape[0]
    steps = theta.shape[1] // ROWS
    return pl.pallas_call(
        bias_kernel,
        out_shape=jax.ShapeDtypeStruct((walkers, vectors), jnp.float32),
        in_specs=[pl.BlockSpec(memory_space=pltpu.VMEM)] * 2,
        out_specs=pl.BlockSpec(memory_space=pltpu.VMEM),
        cost_estimate=pl.CostEstimate(
            flops=2 * steps * walkers * vectors * ROWS * ROWS * 128,
            bytes_accessed=2 * (theta.size + chol.size),
            transcendentals=0,
        ),
        compiler_params=pltpu.CompilerParams(vmem_limit_bytes=16 * 1024 * 1024),
    )(theta, chol)


def column_blocks(array, count):
    *lead, columns = array.shape
    return jnp.moveaxis(array.reshape(*lead, count, columns // count), -2, 0)


def exchanged(blocks, axes):
    return lax.all_to_all(blocks, axes, split_axis=0, concat_axis=0, tiled=True)


def part(walkers, inv_intersection, rotated_chol, full_chol, field_noise):
    wdev, double_rows, orbitals = walkers.shape
    occupied = double_rows // 2
    n_blk, n_walk = lax.axis_size(BLK), lax.axis_size(WALK)
    n_all = n_blk * n_walk
    padded = -(-occupied // ROWS) * ROWS
    pad = padded - occupied

    width = orbitals // n_blk
    chol = exchanged(column_blocks(rotated_chol, n_blk), BLK)
    chol_all = jnp.pad(chol, ((0, 0), (0, 0), (0, pad), (0, 0))).reshape(-1, padded, width)
    inv = jnp.moveaxis(inv_intersection, 1, 2).reshape(wdev, occupied, double_rows)
    inv = jnp.pad(inv, ((0, 0), (0, pad), (0, 0)))
    theta = jnp.einsum("wij,wjp->wip", inv, walkers, preferred_element_type=jnp.float32)
    theta = theta.astype(jnp.bfloat16)
    theta_all = exchanged(column_blocks(theta, n_blk), BLK)
    theta_all = theta_all.reshape(n_blk * wdev, padded, width)
    partial = partial_bias(theta_all, chol_all)
    vectors = partial.shape[1]

    row = jnp.pad(jnp.sum(partial, axis=0), (0, 128 - vectors))
    rows = exchanged(jnp.broadcast_to(row[None, None], (n_all, 1, 128)), ALL)
    bias_shift = jnp.sum(rows, axis=(0, 1))[:vectors] / math.sqrt(wdev * n_all)
    bias = jnp.sum(exchanged(partial.reshape(n_blk, wdev, vectors), BLK), axis=0)

    shifted = 0.1 * (field_noise - bias_shift)
    own = full_chol.shape[0]
    mine = lax.dynamic_slice_in_dim(shifted, lax.axis_index(WALK) * own, own)
    part_field = jnp.sum(mine[:, None, None] * full_chol.astype(jnp.float32), axis=0)
    part_field = part_field.astype(jnp.bfloat16).reshape(n_walk, -1, orbitals)
    parts = exchanged(part_field, WALK)
    piece = jnp.sum(parts.astype(jnp.float32), axis=0).astype(jnp.bfloat16)
    pieces = exchanged(jnp.broadcast_to(piece[None], (n_walk, *piece.shape)), WALK)
    row_block = pieces.reshape(-1, orbitals)
    field = lax.all_gather(row_block, BLK, axis=0, tiled=True)

    current = walkers.reshape(wdev * double_rows, orbitals)
    total = current.astype(jnp.float32)
    for order in range(1, 5):
        current = (jnp.dot(current, field, preferred_element_type=jnp.float32) / order).astype(
            jnp.bfloat16
        )
        total = total + current.astype(jnp.float32)
    propagated = total.astype(jnp.bfloat16).reshape(wdev, double_rows, orbitals)
    return propagated, bias, bias_shift


def solution(mesh):
    torus = Mesh(mesh.devices.reshape(2, 4, 2, 2, 8), ALL)
    in_specs = (
        P(ALL, None, None),
        P(ALL, None, None, None),
        P(BLK, None, None),
        P(WALK, BLK, None),
        P(),
    )
    out_specs = (P(ALL, None, None), P(ALL, None), P())
    return jax.shard_map(part, mesh=torus, in_specs=in_specs, out_specs=out_specs, check_vma=False)
```

time: 297 us -> 199 us (0.67)
  waiting for transfers between devices: 145 us -> 77 us
  blocking collectives: 83.7 us -> 51.2 us
  matrix products: 47.6 us -> 19.8 us
  starting transfers between devices: 0.08 us -> 24.3 us
    all_gather x2 -> x1, waiting for transfers between devices: 145 us -> 40.1 us  [part(): field = lax.all_gather(row_block, BLK, axis=0, tiled=True)]
    all_to_all x0 -> x3, waiting for transfers between devices: none -> 36.9 us  [exchanged(): return lax.all_to_all(blocks, axes, split_axis=0, concat_axis=0, tiled=True)]
    psum x5 -> x0, blocking collectives: 36.6 us -> none  [by_axis(): return functools.reduce(lax.psum, axes, array)]
    dot_general x7 -> x5, matrix products: 47.6 us -> 19.8 us  [the longest x4 19.4 us: part(): jnp.dot(current, field, preferred_element_type=jnp.float32) / order]
    all_to_all x0 -> x3, starting transfers between devices: none -> 24.3 us  [exchanged(): return lax.all_to_all(blocks, axes, split_axis=0, concat_axis=0, tiled=True)]
    all_to_all x2 -> x3, blocking collectives: 47 us -> 51.2 us  [exchanged(): return lax.all_to_all(blocks, axes, split_axis=0, concat_axis=0, tiled=True)]
    reshape x1 -> x4, local copies, waits for them, and re-layouts: 1.58 us -> 4.85 us  [the longest x2 3.7 us: column_blocks(): return jnp.moveaxis(array.reshape(*lead, count, columns // count), -2, 0)]
  transfers between devices with their start and end apart: 2 -> 4, of which waited for: 2 -> 4; matrix products, arithmetic and copies ran while one was open for 1% -> 2% of each run, Pallas kernels for 0% -> 0%
where the time goes in v1:
time: 199 us; the launch traced here: 198 us
  waiting for transfers between devices  77 us (39%)
  blocking collectives  51.2 us (26%)
  starting transfers between devices  24.3 us (12%)
  matrix products  19.8 us (10%)
  between operations  14.2 us (7%)
  local copies, waits for them, and re-layouts  7.42 us (4%)
  other arithmetic  2.76 us (1%)
    all_to_all x3, blocking collectives, exchanged(): return lax.all_to_all(blocks, axes, split_axis=0, concat_axis=0, tiled=True)  51.2 us
    all_gather x1, waiting for transfers between devices, part(): field = lax.all_gather(row_block, BLK, axis=0, tiled=True)  40.1 us
    all_to_all x3, waiting for transfers between devices, exchanged(): return lax.all_to_all(blocks, axes, split_axis=0, concat_axis=0, tiled=True)  36.9 us
    all_to_all x3, starting transfers between devices, exchanged(): return lax.all_to_all(blocks, axes, split_axis=0, concat_axis=0, tiled=True)  24.3 us
    dot_general x4, matrix products, part(): jnp.dot(current, field, preferred_element_type=jnp.float32) / order  19.4 us
  transfers between devices with their start and end apart: 4, of which 4 were waited for; matrix products, arithmetic and copies ran while one was open for 2% of the time, Pallas kernels for 0%

profile of v1, /device:TPU:1, one launch (start us, length us, event | category | flops | bytes accessed | tf_op | source)
XLA Modules:
  0.0 198.0 jit_solution(1480640423258314488)
XLA Ops:
  7.2 2.6 %reshape.51 = bf16[2,100,16,128]{3,2,0,1:T(8,128)(2,1)S(1)} reshape(bf16[2,100,2048]{2,0,1:T(2,128)(2,1)} %param.7) | data formatting | bytes 1638400 | tf_op jit(solution)/shard_map/reshape | solution.py:59
  9.8 1.5 copy.30
  11.3 6.9 %all-to-all-start.1 = ((bf16[16,2,100,128]{3,1,2,0:T(2,128)(2,1)}), bf16[16,2,100,128]{3,1,2,0:T(2,128)(2,1)S(1)}, u32[]{:S(2)}, u32[]{:S(2)}) async-start(bf16[16,2,100,128]{3,1,2,0:T(2,128)(2,1)} %copy.30), calls=%async_computation.1 | async-start | bytes 1638400 | tf_op jit(solution)/shard_map/all_to_all | solution.py:63
  18.2 1.0 reshape.50
  19.4 0.5 fusion.4
  19.8 1.1 copy.39
  20.9 10.2 %all-to-all-done.1 = bf16[16,2,100,128]{3,1,2,0:T(2,128)(2,1)S(1)} async-done(((bf16[16,2,100,128]{3,1,2,0:T(2,128)(2,1)}), bf16[16,2,100,128]{3,1,2,0:T(2,128)(2,1)S(1)}, u32[]{:S(2)}, u32[]{:S(2)}) %all-to-all-start.1) | async-done | bytes 819232 | tf_op jit(solution)/shard_map/all_to_all | solution.py:63
  31.1 4.7 %all-to-all-start = ((bf16[16,2,112,128]{3,2,1,0:T(8,128)(2,1)}), bf16[16,2,112,128]{3,2,1,0:T(8,128)(2,1)S(1)}, u32[]{:S(2)}, u32[]{:S(2)}) async-start(bf16[16,2,112,128]{3,2,1,0:T(8,128)(2,1)} %bitcast.41), calls=%async_computation | async-start | bytes 1835008 | tf_op jit(solution)/shard_map/all_to_all | solution.py:63
  36.0 14.1 %all-to-all-done = bf16[16,2,112,128]{3,2,1,0:T(8,128)(2,1)S(1)} async-done(((bf16[16,2,112,128]{3,2,1,0:T(8,128)(2,1)}), bf16[16,2,112,128]{3,2,1,0:T(8,128)(2,1)S(1)}, u32[]{:S(2)}, u32[]{:S(2)}) %all-to-all-start) | async-done | bytes 917536 | tf_op jit(solution)/shard_map/all_to_all | solution.py:63
  50.2 1.4 shard_map.76
  51.6 0.7 broadcast_in_dim.4
  52.4 12.7 %all-to-all-start.2 = ((f32[256,1,128]{2,1,0:T(1,128)}), f32[256,1,128]{2,1,0:T(1,128)S(1)}, u32[]{:S(2)}, u32[]{:S(2)}) async-start(f32[256,1,128]{2,1,0:T(1,128)} %broadcast_in_dim.4), calls=%async_computation.2 | async-start | bytes 262144 | tf_op jit(solution)/shard_map/all_to_all | solution.py:63
  65.1 12.5 %all-to-all-done.2 = f32[256,1,128]{2,1,0:T(1,128)S(1)} async-done(((f32[256,1,128]{2,1,0:T(1,128)}), f32[256,1,128]{2,1,0:T(1,128)S(1)}, u32[]{:S(2)}, u32[]{:S(2)}) %all-to-all-start.2) | async-done | bytes 131104 | tf_op jit(solution)/shard_map/all_to_all | solution.py:63
  77.7 0.5 subtract_multiply_fusion
  78.3 1.5 multiply_reduce_fusion
  79.8 18.4 %all_to_all.30 = bf16[16,8,2048]{2,1,0:T(8,128)(2,1)S(1)} all-to-all(bf16[16,8,2048]{2,1,0:T(8,128)(2,1)S(1)} %bitcast.47), channel_id=1, replica_groups=mesh['blk_0'=2,'blk_1'=4,'blk_2'=2,'walk_0'=2,'walk_1'=8] {'walk_0','wal..., dimensions={0} | all-to-all | bytes 1048576 | tf_op jit(solution)/shard_map/all_to_all | solution.py:63
  98.3 20.6 %all_to_all.31 = bf16[16,8,2048]{2,1,0:T(8,128)(2,1)} all-to-all(bf16[16,8,2048]{2,1,0:T(8,128)(2,1)S(1)} %broadcast_in_dim.5), channel_id=1, replica_groups=mesh['blk_0'=2,'blk_1'=4,'blk_2'=2,'walk_0'=2,'walk_1'=8] {'walk_0','wal..., dimensions={0} | all-to-all | bytes 1048576 | tf_op jit(solution)/shard_map/all_to_all | solution.py:63
  118.9 12.3 %all_to_all.32 = f32[16,2,32]{2,1,0:T(2,128)S(1)} all-to-all(f32[16,2,32]{2,1,0:T(2,128)S(1)} %bitcast.44), channel_id=1, replica_groups=mesh['blk_0'=2,'blk_1'=4,'blk_2'=2,'walk_0'=2,'walk_1'=8] {'blk_0','blk_..., dimensions={0} | all-to-all | bytes 8192 | tf_op jit(solution)/shard_map/all_to_all | solution.py:63
  131.1 0.6 reduce_sum.52
  131.7 40.1 %all-gather.2.cloned.1.call-done = bf16[2048,2048]{1,0:T(8,128)(2,1)} async-done(((bf16[128,2048]{1,0:T(8,128)(2,1)}), bf16[2048,2048]{1,0:T(8,128)(2,1)}) %all-gather.2.cloned.1.call-update) | async-done | bytes 8388624 | tf_op jit(solution)/shard_map/all_gather | solution.py:100
  171.8 7.1 %convolution_convert_fusion = bf16[2048,400]{0,1:T(8,128)(2,1)S(1)} fusion(bf16[400,2048]{1,0:T(8,128)(2,1)S(1)} %bitcast.48, bf16[2048,2048]{1,0:T(8,128)(2,1)} %all-gather.2.cloned.1.call-done), kind=kOutput, calls=%fused_computation.8 | convolution fusion | flops 3356262400 | bytes 11665408 | tf_op jit(solution)/shard_map/dot_general | solution.py:105
  178.9 3.6 %multiply_convert_fusion.2 = bf16[400,2048]{1,0:T(8,128)(2,1)S(1)} fusion(bf16[2048,400]{0,1:T(8,128)(2,1)S(1)} %convolution_convert_fusion, bf16[2048,2048]{1,0:T(8,128)(2,1)S(1)} %copy-done.2), kind=kOutput, calls=%fused_computation.7 | convolution fusion | flops 3357081600 | bytes 11665408 | tf_op jit(solution)/shard_map/dot_general | solution.py:105
  182.5 3.6 %multiply_convert_fusion.1 = bf16[400,2048]{1,0:T(8,128)(2,1)S(1)} fusion(bf16[400,2048]{1,0:T(8,128)(2,1)S(1)} %multiply_convert_fusion.2, bf16[2048,2048]{1,0:T(8,128)(2,1)S(1)} %copy-done.2), kind=kOutput, calls=%fused_computation.6 | convolution fusion | flops 3357081600 | bytes 11665408 | tf_op jit(solution)/shard_map/dot_general | solution.py:105
  186.1 5.1 %fusion.3 = bf16[400,2048]{1,0:T(8,128)(2,1)} fusion(bf16[2048,400]{0,1:T(8,128)(2,1)S(1)} %convolution_convert_fusion, bf16[400,2048]{1,0:T(8,128)(2,1)S(1)} %multiply_convert_fusion.1, bf16[400,2048]{1,0:T(8,128)(2,1)S(1)} %multiply_convert_fusion.2, bf16[400,2048]{1,0:T(8,128)(2,1)S(1)} %bitcast.49, bf16[2048,2048]{1,0:T(8,128)(2,1)S(1)} %copy-done.2), kind=kOutput, calls=%fused_computation.4 | convolution fusion | flops 3365273600 | bytes 16580608 | tf_op jit(solution)/shard_map/dot_general | solution.py:105
  (17 shorter events, 0.7 us)
Async XLA Ops:
  7.2 12.2 %copy-start = (bf16[2,200,2048]{2,1,0:T(8,128)(2,1)S(1)}, bf16[2,200,2048]{2,1,0:T(8,128)(2,1)}, u32[]{:S(2)}) copy-start(bf16[2,200,2048]{2,1,0:T(8,128)(2,1)} %param.5) | copy-start | bytes 4915204
  11.3 19.8 %all-to-all-start.1 = ((bf16[16,2,100,128]{3,1,2,0:T(2,128)(2,1)}), bf16[16,2,100,128]{3,1,2,0:T(2,128)(2,1)S(1)}, u32[]{:S(2)}, u32[]{:S(2)}) async-start(bf16[16,2,100,128]{3,1,2,0:T(2,128)(2,1)} %copy.30), calls=%async_computation.1 | async-start | bytes 1638400 | tf_op jit(solution)/shard_map/all_to_all | solution.py:63
  31.1 19.0 %all-to-all-start = ((bf16[16,2,112,128]{3,2,1,0:T(8,128)(2,1)}), bf16[16,2,112,128]{3,2,1,0:T(8,128)(2,1)S(1)}, u32[]{:S(2)}, u32[]{:S(2)}) async-start(bf16[16,2,112,128]{3,2,1,0:T(8,128)(2,1)} %bitcast.41), calls=%async_computation | async-start | bytes 1835008 | tf_op jit(solution)/shard_map/all_to_all | solution.py:63
  35.8 41.9 %copy-start.1 = (f32[32]{0:T(128)S(1)}, f32[32]{0:T(128)}, u32[]{:S(2)}) copy-start(f32[32]{0:T(128)} %param.9) | copy-start | bytes 388
  52.4 25.3 %all-to-all-start.2 = ((f32[256,1,128]{2,1,0:T(1,128)}), f32[256,1,128]{2,1,0:T(1,128)S(1)}, u32[]{:S(2)}, u32[]{:S(2)}) async-start(f32[256,1,128]{2,1,0:T(1,128)} %broadcast_in_dim.4), calls=%async_computation.2 | async-start | bytes 262144 | tf_op jit(solution)/shard_map/all_to_all | solution.py:63
  65.1 106.7 %all-gather.2.cloned.1.call-start = ((), (), s32[]{:S(2)}) async-start(), calls=%async_computation.6 | async-start | bytes 8912896 | tf_op jit(solution)/shard_map/all_gather | solution.py:100
  171.8 7.1 %copy-start.2 = (bf16[2048,2048]{1,0:T(8,128)(2,1)S(1)}, bf16[2048,2048]{1,0:T(8,128)(2,1)}, u32[]{:S(2)}) copy-start(bf16[2048,2048]{1,0:T(8,128)(2,1)} %all-gather.2.cloned.1.call-done) | copy-start | bytes 25165828
Sparse Core Ops, SparseCore 0:
  119.0 52.7 all-gather.1

commit v2 on v1

v2 whole, which is shorter than its diff:
```python
import functools
import math

import jax
import jax.numpy as jnp
from jax import lax
from jax.experimental import pallas as pl
from jax.experimental.pallas import tpu as pltpu
from jax.sharding import Mesh
from jax.sharding import PartitionSpec as P

BLK = ("blk_0", "blk_1", "blk_2")
WALK = ("walk_0", "walk_1")
ALL = BLK + WALK
ROWS = 16
TILE = 256


def theta_kernel(inv_ref, walkers_ref, chol_ref, out_ref):
    blocks, both, padded, width = out_ref.shape
    wdev = walkers_ref.shape[0]
    occupied = chol_ref.shape[1]
    for k in range(blocks):
        columns = slice(k * width, (k + 1) * width)
        for w in range(wdev):
            theta = jnp.dot(
                inv_ref[w], walkers_ref[w, :, columns], preferred_element_type=jnp.float32
            )
            out_ref[k, w] = theta.astype(out_ref.dtype)
        for g in range(both - wdev):
            rows = chol_ref[g, :, columns]
            rest = jnp.zeros((padded - occupied, width), rows.dtype)
            out_ref[k, wdev + g] = jnp.concatenate([rows, rest], axis=0)


def theta_and_chol(inv, walkers, chol, blocks):
    wdev, padded, double_rows = inv.shape
    orbitals = walkers.shape[2]
    shape = (blocks, wdev + chol.shape[0], padded, orbitals // blocks)
    return pl.pallas_call(
        theta_kernel,
        out_shape=jax.ShapeDtypeStruct(shape, jnp.bfloat16),
        in_specs=[pl.BlockSpec(memory_space=pltpu.VMEM)] * 3,
        out_specs=pl.BlockSpec(memory_space=pltpu.VMEM),
        cost_estimate=pl.CostEstimate(
            flops=2 * wdev * padded * double_rows * orbitals,
            bytes_accessed=2 * (walkers.size + chol.size + math.prod(shape)),
            transcendentals=0,
        ),
        compiler_params=pltpu.CompilerParams(vmem_limit_bytes=16 * 1024 * 1024),
    )(inv, walkers, chol)


def bias_kernel(wdev, both_ref, out_ref):
    blocks, both, padded, lanes = both_ref.shape
    vdev = both - wdev
    walkers, vectors = blocks * wdev, blocks * vdev
    m, n = walkers * ROWS, vectors * ROWS
    total = jnp.zeros((m, n), jnp.float32)
    for t in range(padded // ROWS):
        rows = slice(t * ROWS, (t + 1) * ROWS)
        a = both_ref[:, :wdev, rows, :].reshape(m, lanes)
        b = both_ref[:, wdev:, rows, :].reshape(n, lanes)
        total = total + lax.dot_general(
            a, b, (((1,), (1,)), ((), ())), preferred_element_type=jnp.float32
        )
    row = lax.broadcasted_iota(jnp.int32, (m, n), 0) % ROWS
    col = lax.broadcasted_iota(jnp.int32, (m, n), 1) % ROWS
    kept = jnp.where(row == col, total, 0.0)
    by_walker = kept.reshape(walkers, ROWS, n).sum(axis=1)
    group = lax.broadcasted_iota(jnp.int32, (n, vectors), 0) // ROWS
    vector = lax.broadcasted_iota(jnp.int32, (n, vectors), 1)
    pick = (group == vector).astype(jnp.float32)
    out_ref[...] = jnp.dot(
        by_walker, pick, preferred_element_type=jnp.float32, precision=lax.Precision.HIGHEST
    )


def partial_bias(both, wdev):
    blocks, held, padded, lanes = both.shape
    walkers, vectors = blocks * wdev, blocks * (held - wdev)
    return pl.pallas_call(
        functools.partial(bias_kernel, wdev),
        out_shape=jax.ShapeDtypeStruct((walkers, vectors), jnp.float32),
        in_specs=[pl.BlockSpec(memory_space=pltpu.VMEM)],
        out_specs=pl.BlockSpec(memory_space=pltpu.VMEM),
        cost_estimate=pl.CostEstimate(
            flops=2 * walkers * vectors * ROWS * padded * lanes,
            bytes_accessed=2 * both.size,
            transcendentals=0,
        ),
        compiler_params=pltpu.CompilerParams(vmem_limit_bytes=16 * 1024 * 1024),
    )(both)


AROUND = (0, -1, 1, 2)
SECOND = (0, -1, 1, -2, 2)


def places(colour):
    for other in (0, 1):
        for step, far in enumerate(SECOND):
            kept = AROUND if step < 3 else (AROUND[:2] if step == 3 else AROUND[2:])
            yield [((near, far) if colour == 0 else (far, near)) + (other,) for near in kept]


PLACES = [list(places(0)), list(places(1))]


def product_kernel(*refs):
    n_blocks = sum(len(p) for p in PLACES)
    walkers_ref, blocks = refs[0], refs[1 : 1 + n_blocks]
    out_ref, field, current, total, sems = refs[1 + n_blocks :]
    orbitals = field.shape[0]
    height, width = blocks[0].shape[1:]
    x = lax.axis_index("walk_0") * 2 + lax.axis_index("blk_0")
    y, core = lax.axis_index("blk_1"), lax.axis_index("blk_2")
    copies = []
    for colour, operands in enumerate(PLACES):
        for place in operands:
            block = blocks[sum(len(p) for p in PLACES[:colour]) + operands.index(place)]
            for k, (dx, dy, other) in enumerate(place):
                bx, by = (x + dx + 4) % 4, (y + dy + 4) % 4
                bc = core if other == 0 else 1 - core
                row = (((bx % 2) * 4 + by) * 2 + bc) * 2 * height + (bx // 2) * height
                row = pl.multiple_of(row, height)
                copies.append(
                    pltpu.make_async_copy(
                        block.at[k],
                        field.at[pl.ds(row, height), pl.ds(colour * width, width)],
                        sems.at[len(copies)],
                    )
                )
    for copy in copies:
        copy.start()
    for copy in copies:
        copy.wait()
    for order in range(1, 5):
        source = walkers_ref if order == 1 else current.at[order % 2]

        @pl.loop(0, orbitals // TILE)
        def _(n, order=order, source=source):
            columns = pl.ds(pl.multiple_of(n * TILE, TILE), TILE)
            term = jnp.dot(source[...], field[:, columns], preferred_element_type=jnp.float32)
            term = (term / order).astype(jnp.bfloat16)
            before = walkers_ref[:, columns].astype(jnp.float32) if order == 1 else total[:, columns]
            summed = before + term.astype(jnp.float32)
            if order < 4:
                current[(order + 1) % 2, :, columns] = term
                total[:, columns] = summed
            else:
                out_ref[:, columns] = summed.astype(out_ref.dtype)


def propagate(walkers, blocks):
    rows, orbitals = walkers.shape
    copies = sum(len(place) for p in PLACES for place in p)
    return pl.pallas_call(
        product_kernel,
        out_shape=jax.ShapeDtypeStruct((rows, orbitals), walkers.dtype),
        in_specs=[pl.BlockSpec(memory_space=pltpu.VMEM)]
        + [pl.BlockSpec(memory_space=pl.ANY)] * len(blocks),
        out_specs=pl.BlockSpec(memory_space=pltpu.VMEM),
        scratch_shapes=[
            pltpu.VMEM((orbitals, orbitals), jnp.bfloat16),
            pltpu.VMEM((2, rows, orbitals), jnp.bfloat16),
            pltpu.VMEM((rows, orbitals), jnp.float32),
            pltpu.SemaphoreType.DMA((copies,)),
        ],
        cost_estimate=pl.CostEstimate(
            flops=8 * rows * orbitals * orbitals,
            bytes_accessed=2 * (2 * walkers.size + orbitals * orbitals),
            transcendentals=0,
        ),
        compiler_params=pltpu.CompilerParams(vmem_limit_bytes=32 * 1024 * 1024),
    )(walkers, *blocks)


def along(axis):
    if axis == "y":
        names, index = ("blk_1",), lambda v: v % 4
    else:
        names, index = ("blk_0", "walk_0"), lambda v: (v % 2) * 2 + (v % 4) // 2
    return lambda array, steps: lax.ppermute(
        array, names, [(index(v), index(v + steps)) for v in range(4)]
    )


def gathered(own, first, second):
    near = jnp.stack([own] + [first(own, -step) for step in AROUND[1:]])
    below, above = second(near, 1), second(near, -1)
    half = len(AROUND) // 2
    return [near, below, above, second(below[:half], 1), second(above[half:], -1)]


def other_core(array):
    return lax.ppermute(array, "blk_2", [(0, 1), (1, 0)])


def exchanged(blocks, axes):
    return lax.all_to_all(blocks, axes, split_axis=0, concat_axis=0, tiled=True)


def part(walkers, inv_intersection, rotated_chol, full_chol, field_noise):
    wdev, double_rows, orbitals = walkers.shape
    occupied = double_rows // 2
    n_blk, n_walk = lax.axis_size(BLK), lax.axis_size(WALK)
    n_all = n_blk * n_walk
    padded = -(-occupied // ROWS) * ROWS

    inv = jnp.moveaxis(inv_intersection, 1, 2).reshape(wdev, occupied, double_rows)
    inv = jnp.pad(inv, ((0, 0), (0, padded - occupied), (0, 0)))
    both = exchanged(theta_and_chol(inv, walkers, rotated_chol, n_blk), BLK)
    partial = partial_bias(both, wdev)
    vectors = partial.shape[1]

    row = jnp.pad(jnp.sum(partial, axis=0), (0, 128 - vectors))
    rows = exchanged(jnp.broadcast_to(row[None, None], (n_all, 1, 128)), ALL)
    bias_shift = jnp.sum(rows, axis=(0, 1))[:vectors] / math.sqrt(wdev * n_all)
    bias = jnp.sum(exchanged(partial.reshape(n_blk, wdev, vectors), BLK), axis=0)

    shifted = 0.1 * (field_noise - bias_shift)
    own = full_chol.shape[0]
    mine = lax.dynamic_slice_in_dim(shifted, lax.axis_index(WALK) * own, own)
    part_field = jnp.sum(mine[:, None, None] * full_chol.astype(jnp.float32), axis=0)
    part_field = part_field.astype(jnp.bfloat16).reshape(n_walk, -1, orbitals)
    parts = exchanged(part_field, WALK)
    piece = sum(parts[k].astype(jnp.float32) for k in range(n_walk)).astype(jnp.bfloat16)
    n_z = lax.axis_size("walk_1")
    pieces = exchanged(jnp.broadcast_to(piece[None], (n_z, *piece.shape)), "walk_1")
    rows = pieces.reshape(-1, orbitals)
    left, right = rows[:, : orbitals // 2], rows[:, orbitals // 2 :]
    lefts = gathered(left, along("x"), along("y"))
    rights = gathered(right, along("y"), along("x"))
    blocks = []
    for held in (lefts, rights):
        blocks += held + [other_core(array) for array in held]
    propagated = propagate(walkers.reshape(wdev * double_rows, orbitals), blocks)
    propagated = propagated.reshape(walkers.shape)
    return propagated, bias, bias_shift


def solution(mesh):
    torus = Mesh(mesh.devices.reshape(2, 4, 2, 2, 8), ALL)
    in_specs = (
        P(ALL, None, None),
        P(ALL, None, None, None),
        P(BLK, None, None),
        P(WALK, BLK, None),
        P(),
    )
    out_specs = (P(ALL, None, None), P(ALL, None), P())
    return jax.shard_map(part, mesh=torus, in_specs=in_specs, out_specs=out_specs, check_vma=False)
```

time: 199 us -> 202 us (1.015)
  waiting for transfers between devices: 77 us -> 38.6 us
  Pallas kernels: 1.42 us -> 26.4 us
  blocking collectives: 51.2 us -> 72.9 us
  starting transfers between devices: 24.3 us -> 45.5 us
  matrix products: 19.8 us -> 0 us
  between operations: 14.2 us -> 1.06 us
  local copies, waits for them, and re-layouts: 7.42 us -> 15 us
    all_gather x1 -> x0, waiting for transfers between devices: 40.1 us -> none  [part(): field = lax.all_gather(row_block, BLK, axis=0, tiled=True)]
    ppermute x0 -> x24, starting transfers between devices: none -> 33 us  [the longest x10 16.8 us: other_core(): return lax.ppermute(array, 'blk_2', [(0, 1), (1, 0)])]
    ppermute x0 -> x24, waiting for transfers between devices: none -> 26 us  [the longest x14 26 us: along(): lax.ppermute(array, names, [(index(v), index(v + steps)) for v in range(4)])]
    pallas_call x1 -> x3, Pallas kernels: 1.42 us -> 26.4 us  [the longest x1 24.3 us: propagate(): pl.pallas_call(product_kernel, out_shape=jax.ShapeDtypeStruct((rows, orbi...]
    all_to_all x3 -> x1, waiting for transfers between devices: 36.9 us -> 12.6 us  [exchanged(): return lax.all_to_all(blocks, axes, split_axis=0, concat_axis=0, tiled=True)]
    all_to_all x3 -> x4, blocking collectives: 51.2 us -> 72.9 us  [exchanged(): return lax.all_to_all(blocks, axes, split_axis=0, concat_axis=0, tiled=True)]
    dot_general x5 -> x0, matrix products: 19.8 us -> none  [the longest x4 19.4 us: part(): jnp.dot(current, field, preferred_element_type=jnp.float32) / order]
    all_to_all x3 -> x1, starting transfers between devices: 24.3 us -> 12.5 us  [exchanged(): return lax.all_to_all(blocks, axes, split_axis=0, concat_axis=0, tiled=True)]
  transfers between devices with their start and end apart: 4 -> 25, of which waited for: 4 -> 7; matrix products, arithmetic and copies ran while one was open for 2% -> 1% of each run, Pallas kernels for 0% -> 0%
where the time goes in v2:
time: 202 us; the launch traced here: 201 us
  blocking collectives  72.9 us (36%)
  starting transfers between devices  45.5 us (23%)
  waiting for transfers between devices  38.6 us (19%)
  Pallas kernels  26.4 us (13%)
  local copies, waits for them, and re-layouts  15 us (7%)
    all_to_all x4, blocking collectives, exchanged(): return lax.all_to_all(blocks, axes, split_axis=0, concat_axis=0, tiled=True)  72.9 us
    ppermute x14, waiting for transfers between devices, along(): lax.ppermute(array, names, [(index(v), index(v + steps)) for v in range(4)])  26 us
    pallas_call x1, Pallas kernels, propagate(): pl.pallas_call(product_kernel, out_shape=jax.ShapeDtypeStruct((rows, orbi...  24.3 us
    ppermute x10, starting transfers between devices, other_core(): return lax.ppermute(array, 'blk_2', [(0, 1), (1, 0)])  16.8 us
    ppermute x14, starting transfers between devices, along(): lax.ppermute(array, names, [(index(v), index(v + steps)) for v in range(4)])  16.2 us
    all_to_all x1, waiting for transfers between devices, exchanged(): return lax.all_to_all(blocks, axes, split_axis=0, concat_axis=0, tiled=True)  12.6 us
    all_to_all x1, starting transfers between devices, exchanged(): return lax.all_to_all(blocks, axes, split_axis=0, concat_axis=0, tiled=True)  12.5 us
    unnamed x35, local copies, waits for them, and re-layouts  11.9 us
  transfers between devices with their start and end apart: 25, of which 7 were waited for; matrix products, arithmetic and copies ran while one was open for 1% of the time, Pallas kernels for 0%

profile of v2, /device:TPU:1, one launch (start us, length us, event | category | flops | bytes accessed | tf_op | source)
XLA Modules:
  0.0 201.1 jit_solution(15289770753200323534)
XLA Ops:
  1.8 1.4 copy.17.chol_ref
  3.9 30.7 %all_to_all.25.both_ref = bf16[16,4,112,128]{3,2,1,0:T(8,128)(2,1)S(1)} all-to-all(bf16[16,4,112,128]{3,2,1,0:T(8,128)(2,1)S(1)} %shard_map.76), channel_id=1, replica_groups=mesh['blk_0'=2,'blk_1'=4,'blk_2'=2,'walk_0'=2,'walk_1'=8] {'blk_0','blk_..., dimensions={0} | all-to-all | bytes 3670016 | tf_op jit(solution)/shard_map/all_to_all | solution.py:201
  34.7 1.4 shard_map.77
  36.9 12.5 %all-to-all-start.1 = ((f32[256,1,128]{2,1,0:T(1,128)}), f32[256,1,128]{2,1,0:T(1,128)S(1)}, u32[]{:S(2)}, u32[]{:S(2)}) async-start(f32[256,1,128]{2,1,0:T(1,128)} %broadcast_in_dim.6), calls=%async_computation.1 | async-start | bytes 262144 | tf_op jit(solution)/shard_map/all_to_all | solution.py:201
  49.4 12.6 %all-to-all-done.1 = f32[256,1,128]{2,1,0:T(1,128)S(1)} async-done(((f32[256,1,128]{2,1,0:T(1,128)}), f32[256,1,128]{2,1,0:T(1,128)S(1)}, u32[]{:S(2)}, u32[]{:S(2)}) %all-to-all-start.1) | async-done | bytes 131104 | tf_op jit(solution)/shard_map/all_to_all | solution.py:201
  62.9 18.4 %all_to_all.26 = bf16[16,8,2048]{2,1,0:T(8,128)(2,1)S(1)} all-to-all(bf16[16,8,2048]{2,1,0:T(8,128)(2,1)S(1)} %bitcast.23), channel_id=1, replica_groups=mesh['blk_0'=2,'blk_1'=4,'blk_2'=2,'walk_0'=2,'walk_1'=8] {'walk_0','wal..., dimensions={0} | all-to-all | bytes 1048576 | tf_op jit(solution)/shard_map/all_to_all | solution.py:201
  81.3 15.1 %all_to_all.27 = bf16[8,8,2048]{2,1,0:T(8,128)(2,1)S(1)} all-to-all(bf16[8,8,2048]{2,1,0:T(8,128)(2,1)S(1)} %broadcast_in_dim.8), channel_id=1, replica_groups=mesh['blk_0'=2,'blk_1'=4,'blk_2'=2,'walk_0'=2,'walk_1'=8] {'walk_1'}, dimensions={0} | all-to-all | bytes 524288 | tf_op jit(solution)/shard_map/all_to_all | solution.py:201
  96.5 1.7 collective-permute-start.1
  98.2 1.3 collective-permute-start.2
  100.4 4.3 %collective-permute-done = bf16[64,1024]{1,0:T(8,128)(2,1)S(1)} collective-permute-done((bf16[64,1024]{1,0:T(8,128)(2,1)S(1)}, bf16[64,1024]{1,0:T(8,128)(2,1)S(1)}, u32[]{:S(2)}, u32[]{:S(2)}) %collective-permute-start) | collective-permute-done | bytes 131104 | tf_op jit(solution)/shard_map/ppermute | solution.py:184
  106.3 2.4 %collective-permute-start.13 = (bf16[64,1024]{1,0:T(8,128)(2,1)S(1)}, bf16[64,1024]{1,0:T(8,128)(2,1)S(1)}, u32[]{:S(2)}, u32[]{:S(2)}) collective-permute-start(bf16[64,1024]{1,0:T(8,128)(2,1)S(1)} %get-tuple-element.7), channel_id=1, source_target_pairs={{0,96},{32,0},{64,32},{96,64},{1,97},{33,1},{65,33},{97,65},{2,98}... | collective-permute-start | bytes 393224 | tf_op jit(solution)/shard_map/ppermute | solution.py:184
  109.8 7.3 %collective-permute-done.13 = bf16[64,1024]{1,0:T(8,128)(2,1)S(1)} collective-permute-done((bf16[64,1024]{1,0:T(8,128)(2,1)S(1)}, bf16[64,1024]{1,0:T(8,128)(2,1)S(1)}, u32[]{:S(2)}, u32[]{:S(2)}) %collective-permute-start.13) | collective-permute-done | bytes 131104 | tf_op jit(solution)/shard_map/ppermute | solution.py:184
  117.2 3.7 %collective-permute-done.12 = bf16[64,1024]{1,0:T(8,128)(2,1)S(1)} collective-permute-done((bf16[64,1024]{1,0:T(8,128)(2,1)S(1)}, bf16[64,1024]{1,0:T(8,128)(2,1)S(1)}, u32[]{:S(2)}, u32[]{:S(2)}) %collective-permute-start.12) | collective-permute-done | bytes 131104 | tf_op jit(solution)/shard_map/ppermute | solution.py:184
  121.0 3.6 %collective-permute-start.16 = (bf16[4,64,1024]{2,1,0:T(8,128)(2,1)S(1)}, bf16[4,64,1024]{2,1,0:T(8,128)(2,1)S(1)}, u32[]{:S(2)}, u32[]{:S(2)}) collective-permute-start(bf16[4,64,1024]{2,1,0:T(8,128)(2,1)S(1)} %pad_maximum_fusion.1.refs_11_), channel_id=1, source_target_pairs={{0,136},{128,0},{8,128},{136,8},{1,137},{129,1},{9,129},{137,9},{2... | collective-permute-start | bytes 1572872 | tf_op jit(solution)/shard_map/ppermute | solution.py:184
  124.6 5.7 %collective-permute-start.7 = (bf16[4,64,1024]{2,1,0:T(8,128)(2,1)S(1)}, bf16[4,64,1024]{2,1,0:T(8,128)(2,1)S(1)}, u32[]{:S(2)}, u32[]{:S(2)}) collective-permute-start(bf16[4,64,1024]{2,1,0:T(8,128)(2,1)S(1)} %pad_maximum_fusion.refs_1_), channel_id=1, source_target_pairs={{0,16},{16,0},{1,17},{17,1},{2,18},{18,2},{3,19},{19,3},{4,20},{20... | collective-permute-start | bytes 1572872 | tf_op jit(solution)/shard_map/ppermute | solution.py:197
  130.7 1.3 collective-permute-start.5
  132.1 2.7 %collective-permute-start.18 = (bf16[2,64,1024]{2,1,0:T(8,128)(2,1)S(1)}, bf16[2,64,1024]{2,1,0:T(8,128)(2,1)}, u32[]{:S(2)}, u32[]{:S(2)}) collective-permute-start(bf16[2,64,1024]{2,1,0:T(8,128)(2,1)S(1)} %slice.113), channel_id=1, source_target_pairs={{0,136},{128,0},{8,128},{136,8},{1,137},{129,1},{9,129},{137,9},{2... | collective-permute-start | bytes 786440 | tf_op jit(solution)/shard_map/ppermute | solution.py:184
  135.6 7.3 %collective-permute-start.9 = (bf16[4,64,1024]{2,1,0:T(8,128)(2,1)S(1)}, bf16[4,64,1024]{2,1,0:T(8,128)(2,1)S(1)}, u32[]{:S(2)}, u32[]{:S(2)}) collective-permute-start(bf16[4,64,1024]{2,1,0:T(8,128)(2,1)S(1)} %collective-permute-done.4.refs_3_), channel_id=1, source_target_pairs={{0,16},{16,0},{1,17},{17,1},{2,18},{18,2},{3,19},{19,3},{4,20},{20... | collective-permute-start | bytes 1572872 | tf_op jit(solution)/shard_map/ppermute | solution.py:197
  142.9 1.7 collective-permute-done.15.refs_12_
  144.6 1.4 collective-permute-start.8
  147.6 8.1 %collective-permute-done.17.refs_14_ = bf16[2,64,1024]{2,1,0:T(8,128)(2,1)} collective-permute-done((bf16[2,64,1024]{2,1,0:T(8,128)(2,1)S(1)}, bf16[2,64,1024]{2,1,0:T(8,128)(2,1)}, u32[]{:S(2)}, u32[]{:S(2)}) %collective-permute-start.17) | collective-permute-done | bytes 262176 | tf_op jit(solution)/shard_map/ppermute | solution.py:184
  155.7 1.4 collective-permute-start.11
  160.0 8.7 %all_to_all.28 = f32[16,2,32]{2,1,0:T(2,128)S(1)} all-to-all(f32[16,2,32]{2,1,0:T(2,128)S(1)} %bitcast.22), channel_id=1, replica_groups=mesh['blk_0'=2,'blk_1'=4,'blk_2'=2,'walk_0'=2,'walk_1'=8] {'blk_0','blk_..., dimensions={0} | all-to-all | bytes 8192 | tf_op jit(solution)/shard_map/all_to_all | solution.py:201
  176.6 24.3 %shard_map.78 = bf16[400,2048]{1,0:T(8,128)(2,1)} custom-call(bf16[400,2048]{1,0:T(8,128)(2,1)S(1)} %bitcast.21, bf16[4,64,1024]{2,1,0:T(8,128)(2,1)S(1)} %pad_maximum_fusion.refs_1_, bf16[4,64,1024]{2,1,0:T(8,128)(2,1)S(1)} %copy-done.2, bf16[4,64,1024]{2,1,0:T(8,128)(2,1)S(1)} %collective-permute-done.4.refs_3_, ...), custom_call_target="tpu_custom_call" | custom-call | flops 13421772800 | bytes 11665408 | tf_op jit(solution)/shard_map/pallas_call | solution.py:158
  (87 shorter events, 21.1 us)
Async XLA Ops:
  36.9 25.1 %all-to-all-start.1 = ((f32[256,1,128]{2,1,0:T(1,128)}), f32[256,1,128]{2,1,0:T(1,128)S(1)}, u32[]{:S(2)}, u32[]{:S(2)}) async-start(f32[256,1,128]{2,1,0:T(1,128)} %broadcast_in_dim.6), calls=%async_computation.1 | async-start | bytes 262144 | tf_op jit(solution)/shard_map/all_to_all | solution.py:201
  98.2 6.4 %collective-permute-start = (bf16[64,1024]{1,0:T(8,128)(2,1)S(1)}, bf16[64,1024]{1,0:T(8,128)(2,1)S(1)}, u32[]{:S(2)}, u32[]{:S(2)}) collective-permute-start(bf16[64,1024]{1,0:T(8,128)(2,1)S(1)} %get-tuple-element.8), channel_id=1, source_target_pairs={{0,128},{128,8},{8,136},{136,0},{1,129},{129,9},{9,137},{137,1},{2... | collective-permute-start | bytes 393224 | tf_op jit(solution)/shard_map/ppermute | solution.py:184
  98.2 6.4 %collective-permute-start.2 = (bf16[64,1024]{1,0:T(8,128)(2,1)S(1)}, bf16[64,1024]{1,0:T(8,128)(2,1)S(1)}, u32[]{:S(2)}, u32[]{:S(2)}) collective-permute-start(bf16[64,1024]{1,0:T(8,128)(2,1)S(1)} %get-tuple-element.8), channel_id=1, source_target_pairs={{0,8},{128,136},{8,0},{136,128},{1,9},{129,137},{9,1},{137,129},{2... | collective-permute-start | bytes 393224 | tf_op jit(solution)/shard_map/ppermute | solution.py:184
  104.7 25.6 %collective-permute-start.4 = (bf16[4,64,1024]{2,1,0:T(8,128)(2,1)S(1)}, bf16[4,64,1024]{2,1,0:T(8,128)(2,1)S(1)}, u32[]{:S(2)}, u32[]{:S(2)}) collective-permute-start(bf16[4,64,1024]{2,1,0:T(8,128)(2,1)S(1)} %pad_maximum_fusion.refs_1_), channel_id=1, source_target_pairs={{0,96},{32,0},{64,32},{96,64},{1,97},{33,1},{65,33},{97,65},{2,98}... | collective-permute-start | bytes 1572872 | tf_op jit(solution)/shard_map/ppermute | solution.py:184
  106.0 24.4 %collective-permute-start.3 = (bf16[4,64,1024]{2,1,0:T(8,128)(2,1)S(1)}, bf16[4,64,1024]{2,1,0:T(8,128)(2,1)S(1)}, u32[]{:S(2)}, u32[]{:S(2)}) collective-permute-start(bf16[4,64,1024]{2,1,0:T(8,128)(2,1)S(1)} %pad_maximum_fusion.refs_1_), channel_id=1, source_target_pairs={{0,32},{32,64},{64,96},{96,0},{1,33},{33,65},{65,97},{97,1},{2,34}... | collective-permute-start | bytes 1572872 | tf_op jit(solution)/shard_map/ppermute | solution.py:184
  106.3 10.9 %collective-permute-start.13 = (bf16[64,1024]{1,0:T(8,128)(2,1)S(1)}, bf16[64,1024]{1,0:T(8,128)(2,1)S(1)}, u32[]{:S(2)}, u32[]{:S(2)}) collective-permute-start(bf16[64,1024]{1,0:T(8,128)(2,1)S(1)} %get-tuple-element.7), channel_id=1, source_target_pairs={{0,96},{32,0},{64,32},{96,64},{1,97},{33,1},{65,33},{97,65},{2,98}... | collective-permute-start | bytes 393224 | tf_op jit(solution)/shard_map/ppermute | solution.py:184
  108.6 12.2 %collective-permute-start.12 = (bf16[64,1024]{1,0:T(8,128)(2,1)S(1)}, bf16[64,1024]{1,0:T(8,128)(2,1)S(1)}, u32[]{:S(2)}, u32[]{:S(2)}) collective-permute-start(bf16[64,1024]{1,0:T(8,128)(2,1)S(1)} %get-tuple-element.7), channel_id=1, source_target_pairs={{0,32},{32,64},{64,96},{96,0},{1,33},{33,65},{65,97},{97,1},{2,34}... | collective-permute-start | bytes 393224 | tf_op jit(solution)/shard_map/ppermute | solution.py:184
  108.7 12.2 %collective-permute-start.14 = (bf16[64,1024]{1,0:T(8,128)(2,1)S(1)}, bf16[64,1024]{1,0:T(8,128)(2,1)S(1)}, u32[]{:S(2)}, u32[]{:S(2)}) collective-permute-start(bf16[64,1024]{1,0:T(8,128)(2,1)S(1)} %get-tuple-element.7), channel_id=1, source_target_pairs={{0,64},{32,96},{64,0},{96,32},{1,65},{33,97},{65,1},{97,33},{2,66}... | collective-permute-start | bytes 393224 | tf_op jit(solution)/shard_map/ppermute | solution.py:184
  121.0 9.8 %collective-permute-start.16 = (bf16[4,64,1024]{2,1,0:T(8,128)(2,1)S(1)}, bf16[4,64,1024]{2,1,0:T(8,128)(2,1)S(1)}, u32[]{:S(2)}, u32[]{:S(2)}) collective-permute-start(bf16[4,64,1024]{2,1,0:T(8,128)(2,1)S(1)} %pad_maximum_fusion.1.refs_11_), channel_id=1, source_target_pairs={{0,136},{128,0},{8,128},{136,8},{1,137},{129,1},{9,129},{137,9},{2... | collective-permute-start | bytes 1572872 | tf_op jit(solution)/shard_map/ppermute | solution.py:184
  124.6 7.4 %collective-permute-start.7 = (bf16[4,64,1024]{2,1,0:T(8,128)(2,1)S(1)}, bf16[4,64,1024]{2,1,0:T(8,128)(2,1)S(1)}, u32[]{:S(2)}, u32[]{:S(2)}) collective-permute-start(bf16[4,64,1024]{2,1,0:T(8,128)(2,1)S(1)} %pad_maximum_fusion.refs_1_), channel_id=1, source_target_pairs={{0,16},{16,0},{1,17},{17,1},{2,18},{18,2},{3,19},{19,3},{4,20},{20... | collective-permute-start | bytes 1572872 | tf_op jit(solution)/shard_map/ppermute | solution.py:197
  130.3 4.5 %collective-permute-start.19 = (bf16[4,64,1024]{2,1,0:T(8,128)(2,1)S(1)}, bf16[4,64,1024]{2,1,0:T(8,128)(2,1)S(1)}, u32[]{:S(2)}, u32[]{:S(2)}) collective-permute-start(bf16[4,64,1024]{2,1,0:T(8,128)(2,1)S(1)} %pad_maximum_fusion.1.refs_11_), channel_id=1, source_target_pairs={{0,16},{16,0},{1,17},{17,1},{2,18},{18,2},{3,19},{19,3},{4,20},{20... | collective-permute-start | bytes 1572872 | tf_op jit(solution)/shard_map/ppermute | solution.py:197
  130.3 14.3 %collective-permute-start.15 = (bf16[4,64,1024]{2,1,0:T(8,128)(2,1)S(1)}, bf16[4,64,1024]{2,1,0:T(8,128)(2,1)}, u32[]{:S(2)}, u32[]{:S(2)}) collective-permute-start(bf16[4,64,1024]{2,1,0:T(8,128)(2,1)S(1)} %pad_maximum_fusion.1.refs_11_), channel_id=1, source_target_pairs={{0,128},{128,8},{8,136},{136,0},{1,129},{129,9},{9,137},{137,1},{2... | collective-permute-start | bytes 1572872 | tf_op jit(solution)/shard_map/ppermute | solution.py:184
  130.4 15.6 %collective-permute-start.6 = (bf16[2,64,1024]{2,1,0:T(8,128)(2,1)S(1)}, bf16[2,64,1024]{2,1,0:T(8,128)(2,1)S(1)}, u32[]{:S(2)}, u32[]{:S(2)}) collective-permute-start(bf16[2,64,1024]{2,1,0:T(8,128)(2,1)S(1)} %slice.110), channel_id=1, source_target_pairs={{0,96},{32,0},{64,32},{96,64},{1,97},{33,1},{65,33},{97,65},{2,98}... | collective-permute-start | bytes 786440 | tf_op jit(solution)/shard_map/ppermute | solution.py:184
  130.7 16.2 %collective-permute-start.5 = (bf16[2,64,1024]{2,1,0:T(8,128)(2,1)S(1)}, bf16[2,64,1024]{2,1,0:T(8,128)(2,1)}, u32[]{:S(2)}, u32[]{:S(2)}) collective-permute-start(bf16[2,64,1024]{2,1,0:T(8,128)(2,1)S(1)} %slice.109), channel_id=1, source_target_pairs={{0,32},{32,64},{64,96},{96,0},{1,33},{33,65},{65,97},{97,1},{2,34}... | collective-permute-start | bytes 786440 | tf_op jit(solution)/shard_map/ppermute | solution.py:184
  132.1 15.0 %collective-permute-start.18 = (bf16[2,64,1024]{2,1,0:T(8,128)(2,1)S(1)}, bf16[2,64,1024]{2,1,0:T(8,128)(2,1)}, u32[]{:S(2)}, u32[]{:S(2)}) collective-permute-start(bf16[2,64,1024]{2,1,0:T(8,128)(2,1)S(1)} %slice.113), channel_id=1, source_target_pairs={{0,136},{128,0},{8,128},{136,8},{1,137},{129,1},{9,129},{137,9},{2... | collective-permute-start | bytes 786440 | tf_op jit(solution)/shard_map/ppermute | solution.py:184
  135.6 21.5 %collective-permute-start.9 = (bf16[4,64,1024]{2,1,0:T(8,128)(2,1)S(1)}, bf16[4,64,1024]{2,1,0:T(8,128)(2,1)S(1)}, u32[]{:S(2)}, u32[]{:S(2)}) collective-permute-start(bf16[4,64,1024]{2,1,0:T(8,128)(2,1)S(1)} %collective-permute-done.4.refs_3_), channel_id=1, source_target_pairs={{0,16},{16,0},{1,17},{17,1},{2,18},{18,2},{3,19},{19,3},{4,20},{20... | collective-permute-start | bytes 1572872 | tf_op jit(solution)/shard_map/ppermute | solution.py:197
  144.6 13.3 %collective-permute-start.8 = (bf16[4,64,1024]{2,1,0:T(8,128)(2,1)S(1)}, bf16[4,64,1024]{2,1,0:T(8,128)(2,1)S(1)}, u32[]{:S(2)}, u32[]{:S(2)}) collective-permute-start(bf16[4,64,1024]{2,1,0:T(8,128)(2,1)S(1)} %collective-permute-done.3.refs_2_), channel_id=1, source_target_pairs={{0,16},{16,0},{1,17},{17,1},{2,18},{18,2},{3,19},{19,3},{4,20},{20... | collective-permute-start | bytes 1572872 | tf_op jit(solution)/shard_map/ppermute | solution.py:197
  146.0 13.2 %collective-permute-start.21 = (bf16[4,64,1024]{2,1,0:T(8,128)(2,1)S(1)}, bf16[4,64,1024]{2,1,0:T(8,128)(2,1)S(1)}, u32[]{:S(2)}, u32[]{:S(2)}) collective-permute-start(bf16[4,64,1024]{2,1,0:T(8,128)(2,1)S(1)} %collective-permute-done.16.refs_13_), channel_id=1, source_target_pairs={{0,16},{16,0},{1,17},{17,1},{2,18},{18,2},{3,19},{19,3},{4,20},{20... | collective-permute-start | bytes 1572872 | tf_op jit(solution)/shard_map/ppermute | solution.py:197
  146.9 8.7 %collective-permute-start.17 = (bf16[2,64,1024]{2,1,0:T(8,128)(2,1)S(1)}, bf16[2,64,1024]{2,1,0:T(8,128)(2,1)}, u32[]{:S(2)}, u32[]{:S(2)}) collective-permute-start(bf16[2,64,1024]{2,1,0:T(8,128)(2,1)S(1)} %slice.112), channel_id=1, source_target_pairs={{0,128},{128,8},{8,136},{136,0},{1,129},{129,9},{9,137},{137,1},{2... | collective-permute-start | bytes 786440 | tf_op jit(solution)/shard_map/ppermute | solution.py:184
  147.0 22.3 %collective-permute-start.20 = (bf16[4,64,1024]{2,1,0:T(8,128)(2,1)}, bf16[4,64,1024]{2,1,0:T(8,128)(2,1)}, u32[]{:S(2)}, u32[]{:S(2)}) collective-permute-start(bf16[4,64,1024]{2,1,0:T(8,128)(2,1)} %collective-permute-done.15.refs_12_), channel_id=1, source_target_pairs={{0,16},{16,0},{1,17},{17,1},{2,18},{18,2},{3,19},{19,3},{4,20},{20... | collective-permute-start | bytes 1572872 | tf_op jit(solution)/shard_map/ppermute | solution.py:197
  155.7 13.6 %collective-permute-start.11 = (bf16[2,64,1024]{2,1,0:T(8,128)(2,1)S(1)}, bf16[2,64,1024]{2,1,0:T(8,128)(2,1)}, u32[]{:S(2)}, u32[]{:S(2)}) collective-permute-start(bf16[2,64,1024]{2,1,0:T(8,128)(2,1)S(1)} %collective-permute-done.6.refs_5_), channel_id=1, source_target_pairs={{0,16},{16,0},{1,17},{17,1},{2,18},{18,2},{3,19},{19,3},{4,20},{20... | collective-permute-start | bytes 786440 | tf_op jit(solution)/shard_map/ppermute | solution.py:197
  157.9 11.5 %collective-permute-start.10 = (bf16[2,64,1024]{2,1,0:T(8,128)(2,1)}, bf16[2,64,1024]{2,1,0:T(8,128)(2,1)}, u32[]{:S(2)}, u32[]{:S(2)}) collective-permute-start(bf16[2,64,1024]{2,1,0:T(8,128)(2,1)} %collective-permute-done.5.refs_4_), channel_id=1, source_target_pairs={{0,16},{16,0},{1,17},{17,1},{2,18},{18,2},{3,19},{19,3},{4,20},{20... | collective-permute-start | bytes 786440 | tf_op jit(solution)/shard_map/ppermute | solution.py:197
  158.7 10.7 %collective-permute-start.23 = (bf16[2,64,1024]{2,1,0:T(8,128)(2,1)}, bf16[2,64,1024]{2,1,0:T(8,128)(2,1)}, u32[]{:S(2)}, u32[]{:S(2)}) collective-permute-start(bf16[2,64,1024]{2,1,0:T(8,128)(2,1)} %collective-permute-done.18.refs_15_), channel_id=1, source_target_pairs={{0,16},{16,0},{1,17},{17,1},{2,18},{18,2},{3,19},{19,3},{4,20},{20... | collective-permute-start | bytes 786440 | tf_op jit(solution)/shard_map/ppermute | solution.py:197
  160.0 9.4 %collective-permute-start.22 = (bf16[2,64,1024]{2,1,0:T(8,128)(2,1)}, bf16[2,64,1024]{2,1,0:T(8,128)(2,1)}, u32[]{:S(2)}, u32[]{:S(2)}) collective-permute-start(bf16[2,64,1024]{2,1,0:T(8,128)(2,1)} %collective-permute-done.17.refs_14_), channel_id=1, source_target_pairs={{0,16},{16,0},{1,17},{17,1},{2,18},{18,2},{3,19},{19,3},{4,20},{20... | collective-permute-start | bytes 786440 | tf_op jit(solution)/shard_map/ppermute | solution.py:197
  (18 other events, 153.2 us)

commit v3 on v2

--- a/solution.py
+++ b/solution.py
@@ -14,6 +14,7 @@
 ALL = BLK + WALK
 ROWS = 16
 TILE = 256
+PART = 512
 
 
 def theta_kernel(inv_ref, walkers_ref, chol_ref, out_ref):
@@ -94,13 +95,13 @@
 
 
 AROUND = (0, -1, 1, 2)
-SECOND = (0, -1, 1, -2, 2)
+NEAR, NEXT = AROUND[:2], AROUND[2:]
+HELD = ((NEAR, 0), (NEXT, 0), (NEAR, -1), (NEXT, -1), (NEAR, 1), (NEXT, 1), (NEAR, 2), (NEXT, 2))
 
 
 def places(colour):
     for other in (0, 1):
-        for step, far in enumerate(SECOND):
-            kept = AROUND if step < 3 else (AROUND[:2] if step == 3 else AROUND[2:])
+        for kept, far in HELD:
             yield [((near, far) if colour == 0 else (far, near)) + (other,) for near in kept]
 
 
@@ -110,46 +111,66 @@
 def product_kernel(*refs):
     n_blocks = sum(len(p) for p in PLACES)
     walkers_ref, blocks = refs[0], refs[1 : 1 + n_blocks]
-    out_ref, field, current, total, sems = refs[1 + n_blocks :]
+    out_ref, field, terms, sems = refs[1 + n_blocks :]
     orbitals = field.shape[0]
     height, width = blocks[0].shape[1:]
     x = lax.axis_index("walk_0") * 2 + lax.axis_index("blk_0")
     y, core = lax.axis_index("blk_1"), lax.axis_index("blk_2")
-    copies = []
-    for colour, operands in enumerate(PLACES):
-        for place in operands:
-            block = blocks[sum(len(p) for p in PLACES[:colour]) + operands.index(place)]
-            for k, (dx, dy, other) in enumerate(place):
-                bx, by = (x + dx + 4) % 4, (y + dy + 4) % 4
-                bc = core if other == 0 else 1 - core
-                row = (((bx % 2) * 4 + by) * 2 + bc) * 2 * height + (bx // 2) * height
-                row = pl.multiple_of(row, height)
-                copies.append(
-                    pltpu.make_async_copy(
-                        block.at[k],
-                        field.at[pl.ds(row, height), pl.ds(colour * width, width)],
-                        sems.at[len(copies)],
+    parts = [[] for _ in range(2 * width // PART)]
+    count = 0
+    for first in range(0, width, PART):
+        index = 0
+        for colour, operands in enumerate(PLACES):
+            for place in operands:
+                block = blocks[index]
+                index += 1
+                for k, (dx, dy, other) in enumerate(place):
+                    bx, by = (x + dx + 4) % 4, (y + dy + 4) % 4
+                    bc = core if other == 0 else 1 - core
+                    row = (((bx % 2) * 4 + by) * 2 + bc) * 2 * height + (bx // 2) * height
+                    row = pl.multiple_of(row, height)
+                    at = colour * width + first
+                    copy = pltpu.make_async_copy(
+                        block.at[k, :, pl.ds(first, PART)],
+                        field.at[pl.ds(row, height), pl.ds(at, PART)],
+                        sems.at[count],
                     )
-                )
-    for copy in copies:
-        copy.start()
-    for copy in copies:
-        copy.wait()
-    for order in range(1, 5):
-        source = walkers_ref if order == 1 else current.at[order % 2]
-
-        @pl.loop(0, orbitals // TILE)
-        def _(n, order=order, source=source):
-            columns = pl.ds(pl.multiple_of(n * TILE, TILE), TILE)
-            term = jnp.dot(source[...], field[:, columns], preferred_element_type=jnp.float32)
-            term = (term / order).astype(jnp.bfloat16)
-            before = walkers_ref[:, columns].astype(jnp.float32) if order == 1 else total[:, columns]
-            summed = before + term.astype(jnp.float32)
-            if order < 4:
-                current[(order + 1) % 2, :, columns] = term
-                total[:, columns] = summed
-            else:
-                out_ref[:, columns] = summed.astype(out_ref.dtype)
+                    count += 1
+                    parts[at // PART].append(copy)
+    starts = [at for first in range(width // PART) for at in (first, first + width // PART)]
+    for at in starts:
+        for copy in parts[at]:
+            copy.start()
+
+    def term(order, n):
+        columns = pl.ds(pl.multiple_of(n * TILE, TILE), TILE)
+        source = walkers_ref if order == 1 else terms.at[order - 2]
+        product = jnp.dot(source[...], field[:, columns], preferred_element_type=jnp.float32)
+        value = (product * (1.0 / order)).astype(jnp.bfloat16)
+        if order < 4:
+            terms[order - 1, :, columns] = value
+        else:
+            total = walkers_ref[:, columns].astype(jnp.float32)
+            for k in range(3):
+                total = total + terms[k, :, columns].astype(jnp.float32)
+            out_ref[:, columns] = (total + value.astype(jnp.float32)).astype(out_ref.dtype)
+
+    per_part = PART // TILE
+    for at in starts:
+        for copy in parts[at]:
+            copy.wait()
+
+        @pl.loop(0, 1)
+        def _(n, at=at):
+            for k in range(per_part):
+                term(1, n + at * per_part + k)
+
+    for order in range(2, 5):
+
+        @pl.loop(0, orbitals // TILE // per_part)
+        def _(n, order=order):
+            for k in range(per_part):
+                term(order, n * per_part + k)
 
 
 def propagate(walkers, blocks):
@@ -163,9 +184,8 @@
         out_specs=pl.BlockSpec(memory_space=pltpu.VMEM),
         scratch_shapes=[
             pltpu.VMEM((orbitals, orbitals), jnp.bfloat16),
-            pltpu.VMEM((2, rows, orbitals), jnp.bfloat16),
-            pltpu.VMEM((rows, orbitals), jnp.float32),
-            pltpu.SemaphoreType.DMA((copies,)),
+            pltpu.VMEM((3, rows, orbitals), jnp.bfloat16),
+            pltpu.SemaphoreType.DMA((copies * blocks[0].shape[2] // PART,)),
         ],
         cost_estimate=pl.CostEstimate(
             flops=8 * rows * orbitals * orbitals,
@@ -187,10 +207,12 @@
 
 
 def gathered(own, first, second):
-    near = jnp.stack([own] + [first(own, -step) for step in AROUND[1:]])
-    below, above = second(near, 1), second(near, -1)
-    half = len(AROUND) // 2
-    return [near, below, above, second(below[:half], 1), second(above[half:], -1)]
+    came = [own] + [first(own, -step) for step in AROUND[1:]]
+    near, next_ = jnp.stack(came[:2]), jnp.stack(came[2:])
+    below, above = second(near, 1), second(next_, -1)
+    below_next, above_near = second(next_, 1), second(near, -1)
+    far = [second(below, 1), second(above, -1)]
+    return [near, next_, below, below_next, above_near, above] + far
 
 
 def other_core(array):
@@ -208,25 +230,45 @@
     n_all = n_blk * n_walk
     padded = -(-occupied // ROWS) * ROWS
 
+    half = lax.axis_index("walk_0")
+    rows = full_chol.shape[1] // 2
+    kept = lax.dynamic_slice_in_dim(full_chol, half * rows, rows, 1)
+    given = lax.dynamic_slice_in_dim(full_chol, (1 - half) * rows, rows, 1)
+    came = lax.ppermute(given, "walk_0", [(0, 1), (1, 0)])
     inv = jnp.moveaxis(inv_intersection, 1, 2).reshape(wdev, occupied, double_rows)
     inv = jnp.pad(inv, ((0, 0), (0, padded - occupied), (0, 0)))
-    both = exchanged(theta_and_chol(inv, walkers, rotated_chol, n_blk), BLK)
+    both = theta_and_chol(inv, walkers, rotated_chol, n_blk)
+    both = exchanged(both, BLK)
     partial = partial_bias(both, wdev)
     vectors = partial.shape[1]
 
-    row = jnp.pad(jnp.sum(partial, axis=0), (0, 128 - vectors))
-    rows = exchanged(jnp.broadcast_to(row[None, None], (n_all, 1, 128)), ALL)
+    summed = jnp.sum(partial, axis=0)
+    rows = jnp.concatenate(
+        [jnp.broadcast_to(summed, (n_blk, vectors)), partial.reshape(n_blk, wdev * vectors)], axis=1
+    )
+    rows = jnp.pad(rows, ((0, 0), (0, 128 - rows.shape[1])))
+    rows = jnp.broadcast_to(rows[:, None, None], (n_blk, n_walk, 1, 128))
+    rows = exchanged(rows.reshape(n_all, 1, 128), ALL)
+    rows = rows.reshape(n_blk, n_walk, 128)
     bias_shift = jnp.sum(rows, axis=(0, 1))[:vectors] / math.sqrt(wdev * n_all)
-    bias = jnp.sum(exchanged(partial.reshape(n_blk, wdev, vectors), BLK), axis=0)
+    peers = lax.dynamic_index_in_dim(rows, lax.axis_index(WALK), 1, keepdims=False)
+    bias = jnp.sum(peers, axis=0)[vectors : vectors + wdev * vectors].reshape(wdev, vectors)
 
     shifted = 0.1 * (field_noise - bias_shift)
     own = full_chol.shape[0]
-    mine = lax.dynamic_slice_in_dim(shifted, lax.axis_index(WALK) * own, own)
-    part_field = jnp.sum(mine[:, None, None] * full_chol.astype(jnp.float32), axis=0)
-    part_field = part_field.astype(jnp.bfloat16).reshape(n_walk, -1, orbitals)
-    parts = exchanged(part_field, WALK)
-    piece = sum(parts[k].astype(jnp.float32) for k in range(n_walk)).astype(jnp.bfloat16)
+    by_owner = shifted.reshape(2, -1, own)
+    mine = lax.dynamic_index_in_dim(by_owner, lax.axis_index("walk_1"), 1, keepdims=False)
+    near = lax.dynamic_index_in_dim(mine, half, 0, keepdims=False)
+    far = lax.dynamic_index_in_dim(mine, 1 - half, 0, keepdims=False)
+    part_field = sum(
+        scale[k] * rows[k].astype(jnp.float32)
+        for scale, rows in ((near, kept), (far, came))
+        for k in range(own)
+    )
     n_z = lax.axis_size("walk_1")
+    part_field = part_field.astype(jnp.bfloat16).reshape(n_z, -1, orbitals)
+    parts = exchanged(part_field, "walk_1")
+    piece = sum(parts[k].astype(jnp.float32) for k in range(n_z)).astype(jnp.bfloat16)
     pieces = exchanged(jnp.broadcast_to(piece[None], (n_z, *piece.shape)), "walk_1")
     rows = pieces.reshape(-1, orbitals)
     left, right = rows[:, : orbitals // 2], rows[:, orbitals // 2 :]

time: 202 us -> 218 us (1.079)
  blocking collectives: 72.9 us -> 29.7 us
  starting transfers between devices: 45.5 us -> 64.2 us
  local copies, waits for them, and re-layouts: 15 us -> 32.7 us
  waiting for transfers between devices: 38.6 us -> 54.6 us
  Pallas kernels: 26.4 us -> 30.5 us
  other arithmetic: 1.68 us -> 4.63 us
    all_to_all x4 -> x2, blocking collectives: 72.9 us -> 29.7 us  [exchanged(): return lax.all_to_all(blocks, axes, split_axis=0, concat_axis=0, tiled=True)]
    all_to_all x1 -> x2, waiting for transfers between devices: 12.6 us -> 32.4 us  [exchanged(): return lax.all_to_all(blocks, axes, split_axis=0, concat_axis=0, tiled=True)]
    unnamed x35 -> x71, local copies, waits for them, and re-layouts: 11.9 us -> 27.4 us
    all_to_all x1 -> x2, starting transfers between devices: 12.5 us -> 21.4 us  [exchanged(): return lax.all_to_all(blocks, axes, split_axis=0, concat_axis=0, tiled=True)]
    ppermute x14 -> x18, waiting for transfers between devices: 26 us -> 19.9 us  [along(): lax.ppermute(array, names, [(index(v), index(v + steps)) for v in range(4)])]
    ppermute x10 -> x16, starting transfers between devices: 16.8 us -> 21.3 us  [other_core(): return lax.ppermute(array, 'blk_2', [(0, 1), (1, 0)])]
    pallas_call x1, Pallas kernels: 24.3 us -> 28.4 us  [propagate(): pl.pallas_call(product_kernel, out_shape=jax.ShapeDtypeStruct((rows, orbi...]
    ppermute x0 -> x1, starting transfers between devices: none -> 2.86 us  [part(): came = lax.ppermute(given, 'walk_0', [(0, 1), (1, 0)])]
  transfers between devices with their start and end apart: 25 -> 37, of which waited for: 7 -> 11; matrix products, arithmetic and copies ran while one was open for 1% -> 2% of each run, Pallas kernels for 0% -> 0%
where the time goes in v3:
time: 218 us; the launch traced here: 217 us
  starting transfers between devices  64.2 us (29%)
  waiting for transfers between devices  54.6 us (25%)
  local copies, waits for them, and re-layouts  32.7 us (15%)
  Pallas kernels  30.5 us (14%)
  blocking collectives  29.7 us (14%)
  other arithmetic  4.63 us (2%)
    all_to_all x2, waiting for transfers between devices, exchanged(): return lax.all_to_all(blocks, axes, split_axis=0, concat_axis=0, tiled=True)  32.4 us
    all_to_all x2, blocking collectives, exchanged(): return lax.all_to_all(blocks, axes, split_axis=0, concat_axis=0, tiled=True)  29.7 us
    pallas_call x1, Pallas kernels, propagate(): pl.pallas_call(product_kernel, out_shape=jax.ShapeDtypeStruct((rows, orbi...  28.4 us
    unnamed x71, local copies, waits for them, and re-layouts  27.4 us
    all_to_all x2, starting transfers between devices, exchanged(): return lax.all_to_all(blocks, axes, split_axis=0, concat_axis=0, tiled=True)  21.4 us
    ppermute x16, starting transfers between devices, other_core(): return lax.ppermute(array, 'blk_2', [(0, 1), (1, 0)])  21.3 us
    ppermute x18, waiting for transfers between devices, along(): lax.ppermute(array, names, [(index(v), index(v + steps)) for v in range(4)])  19.9 us
    ppermute x18, starting transfers between devices, along(): lax.ppermute(array, names, [(index(v), index(v + steps)) for v in range(4)])  18.6 us
  transfers between devices with their start and end apart: 37, of which 11 were waited for; matrix products, arithmetic and copies ran while one was open for 2% of the time, Pallas kernels for 0%

profile of v3, /device:TPU:1, one launch (start us, length us, event | category | flops | bytes accessed | tf_op | source)
XLA Modules:
  0.0 217.4 jit_solution(1975983509800532811)
XLA Ops:
  5.2 6.9 %all-to-all-start = ((bf16[16,4,112,128]{3,2,1,0:T(8,128)(2,1)}), bf16[16,4,112,128]{3,2,1,0:T(8,128)(2,1)S(1)}, u32[]{:S(2)}, u32[]{:S(2)}) async-start(bf16[16,4,112,128]{3,2,1,0:T(8,128)(2,1)} %copy-done), calls=%async_computation | async-start | bytes 3670016 | tf_op jit(solution)/shard_map/all_to_all | solution.py:223
  12.1 24.5 %all-to-all-done.both_ref = bf16[16,4,112,128]{3,2,1,0:T(8,128)(2,1)S(1)} async-done(((bf16[16,4,112,128]{3,2,1,0:T(8,128)(2,1)}), bf16[16,4,112,128]{3,2,1,0:T(8,128)(2,1)S(1)}, u32[]{:S(2)}, u32[]{:S(2)}) %all-to-all-start) | async-done | bytes 1835040 | tf_op jit(solution)/shard_map/all_to_all | solution.py:223
  38.8 14.5 %all-to-all-start.1 = ((f32[256,1,128]{2,1,0:T(1,128)}), f32[256,1,128]{2,1,0:T(1,128)S(1)}, u32[]{:S(2)}, u32[]{:S(2)}) async-start(f32[256,1,128]{2,1,0:T(1,128)} %bitcast.2), calls=%async_computation.1 | async-start | bytes 262144 | tf_op jit(solution)/shard_map/all_to_all | solution.py:223
  53.4 1.9 constant_dynamic-slice_fusion
  55.3 2.9 %collective-permute-start = (bf16[2,64,2048]{2,1,0:T(8,128)(2,1)}, bf16[2,64,2048]{2,1,0:T(8,128)(2,1)S(1)}, u32[]{:S(2)}, u32[]{:S(2)}) collective-permute-start(bf16[2,64,2048]{2,1,0:T(8,128)(2,1)} %constant_dynamic-slice_fusion), channel_id=1, source_target_pairs={{0,8},{8,0},{1,9},{9,1},{2,10},{10,2},{3,11},{11,3},{4,12},{12,4},... | collective-permute-start | bytes 1572872 | tf_op jit(solution)/shard_map/ppermute | solution.py:237
  58.1 7.9 %all-to-all-done.1 = f32[256,1,128]{2,1,0:T(1,128)S(1)} async-done(((f32[256,1,128]{2,1,0:T(1,128)}), f32[256,1,128]{2,1,0:T(1,128)S(1)}, u32[]{:S(2)}, u32[]{:S(2)}) %all-to-all-start.1) | async-done | bytes 131104 | tf_op jit(solution)/shard_map/all_to_all | solution.py:223
  67.6 2.2 %collective-permute-done = bf16[2,64,2048]{2,1,0:T(8,128)(2,1)S(1)} collective-permute-done((bf16[2,64,2048]{2,1,0:T(8,128)(2,1)}, bf16[2,64,2048]{2,1,0:T(8,128)(2,1)S(1)}, u32[]{:S(2)}, u32[]{:S(2)}) %collective-permute-start) | collective-permute-done | bytes 524320 | tf_op jit(solution)/shard_map/ppermute | solution.py:237
  69.8 2.7 %fusion = bf16[8,8,2048]{2,1,0:T(8,128)(2,1)S(1)} fusion(bf16[2,64,2048]{2,1,0:T(8,128)(2,1)S(1)} %collective-permute-done, bf16[2,128,2048]{2,1,0:T(8,128)(2,1)S(1)} %copy-done.32, s32[]{:T(128)S(6)} %add.98, s32[]{:T(128)S(6)} %select_n.31, f32[]{:T(128)} %bitcast.6, f32[]{:T(128)} %bitcast.5, f32[]{:T(128)} %bitcast.4, f32[]{:T(128)} %bitcast.3), kind=kLoop, calls=%fused_computation.1 | loop fusion | flops 1572864 | bytes 1310744 | tf_op jit(solution)/shard_map/convert_element_type | solution.py:269
  72.6 17.7 %all_to_all.20 = bf16[8,8,2048]{2,1,0:T(8,128)(2,1)S(1)} all-to-all(bf16[8,8,2048]{2,1,0:T(8,128)(2,1)S(1)} %fusion), channel_id=1, replica_groups=mesh['blk_0'=2,'blk_1'=4,'blk_2'=2,'walk_0'=2,'walk_1'=8] {'walk_1'}, dimensions={0} | all-to-all | bytes 524288 | tf_op jit(solution)/shard_map/all_to_all | solution.py:223
  90.3 12.0 %all_to_all.21 = bf16[8,8,2048]{2,1,0:T(8,128)(2,1)S(1)} all-to-all(bf16[8,8,2048]{2,1,0:T(8,128)(2,1)S(1)} %broadcast_in_dim.23), channel_id=1, replica_groups=mesh['blk_0'=2,'blk_1'=4,'blk_2'=2,'walk_0'=2,'walk_1'=8] {'walk_1'}, dimensions={0} | all-to-all | bytes 524288 | tf_op jit(solution)/shard_map/all_to_all | solution.py:223
  102.4 2.5 %collective-permute-start.2 = (bf16[64,1024]{1,0:T(8,128)(2,1)S(1)}, bf16[64,1024]{1,0:T(8,128)(2,1)S(1)}, u32[]{:S(2)}, u32[]{:S(2)}) collective-permute-start(bf16[64,1024]{1,0:T(8,128)(2,1)S(1)} %get-tuple-element.8), channel_id=1, source_target_pairs={{0,136},{128,0},{8,128},{136,8},{1,137},{129,1},{9,129},{137,9},{2... | collective-permute-start | bytes 393224 | tf_op jit(solution)/shard_map/ppermute | solution.py:204
  105.5 2.6 %collective-permute-start.19 = (bf16[64,1024]{1,0:T(8,128)(2,1)S(1)}, bf16[64,1024]{1,0:T(8,128)(2,1)S(1)}, u32[]{:S(2)}, u32[]{:S(2)}) collective-permute-start(bf16[64,1024]{1,0:T(8,128)(2,1)S(1)} %get-tuple-element.7), channel_id=1, source_target_pairs={{0,96},{32,0},{64,32},{96,64},{1,97},{33,1},{65,33},{97,65},{2,98}... | collective-permute-start | bytes 393224 | tf_op jit(solution)/shard_map/ppermute | solution.py:204
  110.3 5.1 %collective-permute-start.11 = (bf16[2,64,1024]{2,1,0:T(8,128)(2,1)S(1)}, bf16[2,64,1024]{2,1,0:T(8,128)(2,1)S(1)}, u32[]{:S(2)}, u32[]{:S(2)}) collective-permute-start(bf16[2,64,1024]{2,1,0:T(8,128)(2,1)S(1)} %pad_maximum_fusion.1.refs_2_), channel_id=1, source_target_pairs={{0,16},{16,0},{1,17},{17,1},{2,18},{18,2},{3,19},{19,3},{4,20},{20... | collective-permute-start | bytes 786440 | tf_op jit(solution)/shard_map/ppermute | solution.py:219
  115.3 2.6 %collective-permute-start.7 = (bf16[2,64,1024]{2,1,0:T(8,128)(2,1)S(1)}, bf16[2,64,1024]{2,1,0:T(8,128)(2,1)S(1)}, u32[]{:S(2)}, u32[]{:S(2)}) collective-permute-start(bf16[2,64,1024]{2,1,0:T(8,128)(2,1)S(1)} %pad_maximum_fusion.1.refs_2_), channel_id=1, source_target_pairs={{0,96},{32,0},{64,32},{96,64},{1,97},{33,1},{65,33},{97,65},{2,98}... | collective-permute-start | bytes 786440 | tf_op jit(solution)/shard_map/ppermute | solution.py:204
  118.0 1.7 collective-permute-start.20
  121.2 7.3 %collective-permute-done.20 = bf16[64,1024]{1,0:T(8,128)(2,1)S(1)} collective-permute-done((bf16[64,1024]{1,0:T(8,128)(2,1)S(1)}, bf16[64,1024]{1,0:T(8,128)(2,1)S(1)}, u32[]{:S(2)}, u32[]{:S(2)}) %collective-permute-start.20) | collective-permute-done | bytes 131104 | tf_op jit(solution)/shard_map/ppermute | solution.py:204
  128.6 2.1 collective-permute-start.10
  133.7 1.8 collective-permute-start.28
  138.9 2.1 collective-permute-start.27
  150.6 2.2 collective-permute-start.12
  160.5 2.1 collective-permute-done.8.refs_7_
  166.1 5.0 %collective-permute-done.25.refs_23_ = bf16[2,64,1024]{2,1,0:T(8,128)(2,1)} collective-permute-done((bf16[2,64,1024]{2,1,0:T(8,128)(2,1)}, bf16[2,64,1024]{2,1,0:T(8,128)(2,1)}, u32[]{:S(2)}, u32[]{:S(2)}) %collective-permute-start.25) | collective-permute-done | bytes 262176 | tf_op jit(solution)/shard_map/ppermute | solution.py:204
  171.2 1.7 collective-permute-start.33
  188.8 28.4 %shard_map.78 = bf16[400,2048]{1,0:T(8,128)(2,1)} custom-call(bf16[400,2048]{1,0:T(8,128)(2,1)S(1)} %bitcast.24, bf16[2,64,1024]{2,1,0:T(8,128)(2,1)S(1)} %pad_maximum_fusion.refs_1_, bf16[2,64,1024]{2,1,0:T(8,128)(2,1)S(1)} %pad_maximum_fusion.1.refs_2_, bf16[2,64,1024]{2,1,0:T(8,128)(2,1)S(1)} %copy-done.7, ...), custom_call_target="tpu_custom_call" | custom-call | flops 13421772800 | bytes 11665408 | tf_op jit(solution)/shard_map/pallas_call | solution.py:179
  (151 shorter events, 55.9 us)
Async XLA Ops:
  5.2 31.4 %all-to-all-start = ((bf16[16,4,112,128]{3,2,1,0:T(8,128)(2,1)}), bf16[16,4,112,128]{3,2,1,0:T(8,128)(2,1)S(1)}, u32[]{:S(2)}, u32[]{:S(2)}) async-start(bf16[16,4,112,128]{3,2,1,0:T(8,128)(2,1)} %copy-done), calls=%async_computation | async-start | bytes 3670016 | tf_op jit(solution)/shard_map/all_to_all | solution.py:223
  38.8 27.2 %all-to-all-start.1 = ((f32[256,1,128]{2,1,0:T(1,128)}), f32[256,1,128]{2,1,0:T(1,128)S(1)}, u32[]{:S(2)}, u32[]{:S(2)}) async-start(f32[256,1,128]{2,1,0:T(1,128)} %bitcast.2), calls=%async_computation.1 | async-start | bytes 262144 | tf_op jit(solution)/shard_map/all_to_all | solution.py:223
  55.3 14.6 %collective-permute-start = (bf16[2,64,2048]{2,1,0:T(8,128)(2,1)}, bf16[2,64,2048]{2,1,0:T(8,128)(2,1)S(1)}, u32[]{:S(2)}, u32[]{:S(2)}) collective-permute-start(bf16[2,64,2048]{2,1,0:T(8,128)(2,1)} %constant_dynamic-slice_fusion), channel_id=1, source_target_pairs={{0,8},{8,0},{1,9},{9,1},{2,10},{10,2},{3,11},{11,3},{4,12},{12,4},... | collective-permute-start | bytes 1572872 | tf_op jit(solution)/shard_map/ppermute | solution.py:237
  105.5 12.5 %collective-permute-start.19 = (bf16[64,1024]{1,0:T(8,128)(2,1)S(1)}, bf16[64,1024]{1,0:T(8,128)(2,1)S(1)}, u32[]{:S(2)}, u32[]{:S(2)}) collective-permute-start(bf16[64,1024]{1,0:T(8,128)(2,1)S(1)} %get-tuple-element.7), channel_id=1, source_target_pairs={{0,96},{32,0},{64,32},{96,64},{1,97},{33,1},{65,33},{97,65},{2,98}... | collective-permute-start | bytes 393224 | tf_op jit(solution)/shard_map/ppermute | solution.py:204
  108.1 11.6 %collective-permute-start.1 = (bf16[64,1024]{1,0:T(8,128)(2,1)S(1)}, bf16[64,1024]{1,0:T(8,128)(2,1)S(1)}, u32[]{:S(2)}, u32[]{:S(2)}) collective-permute-start(bf16[64,1024]{1,0:T(8,128)(2,1)S(1)} %get-tuple-element.8), channel_id=1, source_target_pairs={{0,128},{128,8},{8,136},{136,0},{1,129},{129,9},{9,137},{137,1},{2... | collective-permute-start | bytes 393224 | tf_op jit(solution)/shard_map/ppermute | solution.py:204
  110.3 22.0 %collective-permute-start.11 = (bf16[2,64,1024]{2,1,0:T(8,128)(2,1)S(1)}, bf16[2,64,1024]{2,1,0:T(8,128)(2,1)S(1)}, u32[]{:S(2)}, u32[]{:S(2)}) collective-permute-start(bf16[2,64,1024]{2,1,0:T(8,128)(2,1)S(1)} %pad_maximum_fusion.1.refs_2_), channel_id=1, source_target_pairs={{0,16},{16,0},{1,17},{17,1},{2,18},{18,2},{3,19},{19,3},{4,20},{20... | collective-permute-start | bytes 786440 | tf_op jit(solution)/shard_map/ppermute | solution.py:219
  115.3 18.4 %collective-permute-start.7 = (bf16[2,64,1024]{2,1,0:T(8,128)(2,1)S(1)}, bf16[2,64,1024]{2,1,0:T(8,128)(2,1)S(1)}, u32[]{:S(2)}, u32[]{:S(2)}) collective-permute-start(bf16[2,64,1024]{2,1,0:T(8,128)(2,1)S(1)} %pad_maximum_fusion.1.refs_2_), channel_id=1, source_target_pairs={{0,96},{32,0},{64,32},{96,64},{1,97},{33,1},{65,33},{97,65},{2,98}... | collective-permute-start | bytes 786440 | tf_op jit(solution)/shard_map/ppermute | solution.py:204
  117.9 17.6 %collective-permute-start.5 = (bf16[2,64,1024]{2,1,0:T(8,128)(2,1)S(1)}, bf16[2,64,1024]{2,1,0:T(8,128)(2,1)S(1)}, u32[]{:S(2)}, u32[]{:S(2)}) collective-permute-start(bf16[2,64,1024]{2,1,0:T(8,128)(2,1)S(1)} %pad_maximum_fusion.1.refs_2_), channel_id=1, source_target_pairs={{0,32},{32,64},{64,96},{96,0},{1,33},{33,65},{65,97},{97,1},{2,34}... | collective-permute-start | bytes 786440 | tf_op jit(solution)/shard_map/ppermute | solution.py:204
  118.0 10.6 %collective-permute-start.20 = (bf16[64,1024]{1,0:T(8,128)(2,1)S(1)}, bf16[64,1024]{1,0:T(8,128)(2,1)S(1)}, u32[]{:S(2)}, u32[]{:S(2)}) collective-permute-start(bf16[64,1024]{1,0:T(8,128)(2,1)S(1)} %get-tuple-element.7), channel_id=1, source_target_pairs={{0,64},{32,96},{64,0},{96,32},{1,65},{33,97},{65,1},{97,33},{2,66}... | collective-permute-start | bytes 393224 | tf_op jit(solution)/shard_map/ppermute | solution.py:204
  119.7 12.6 %collective-permute-start.18 = (bf16[64,1024]{1,0:T(8,128)(2,1)S(1)}, bf16[64,1024]{1,0:T(8,128)(2,1)S(1)}, u32[]{:S(2)}, u32[]{:S(2)}) collective-permute-start(bf16[64,1024]{1,0:T(8,128)(2,1)S(1)} %get-tuple-element.7), channel_id=1, source_target_pairs={{0,32},{32,64},{64,96},{96,0},{1,33},{33,65},{65,97},{97,1},{2,34}... | collective-permute-start | bytes 393224 | tf_op jit(solution)/shard_map/ppermute | solution.py:204
  132.3 8.7 %collective-permute-start.4 = (bf16[2,64,1024]{2,1,0:T(8,128)(2,1)S(1)}, bf16[2,64,1024]{2,1,0:T(8,128)(2,1)S(1)}, u32[]{:S(2)}, u32[]{:S(2)}) collective-permute-start(bf16[2,64,1024]{2,1,0:T(8,128)(2,1)S(1)} %pad_maximum_fusion.refs_1_), channel_id=1, source_target_pairs={{0,32},{32,64},{64,96},{96,0},{1,33},{33,65},{65,97},{97,1},{2,34}... | collective-permute-start | bytes 786440 | tf_op jit(solution)/shard_map/ppermute | solution.py:204
  137.1 8.7 %collective-permute-start.22 = (bf16[2,64,1024]{2,1,0:T(8,128)(2,1)S(1)}, bf16[2,64,1024]{2,1,0:T(8,128)(2,1)S(1)}, u32[]{:S(2)}, u32[]{:S(2)}) collective-permute-start(bf16[2,64,1024]{2,1,0:T(8,128)(2,1)S(1)} %pad_maximum_fusion.3.refs_18_), channel_id=1, source_target_pairs={{0,128},{128,8},{8,136},{136,0},{1,129},{129,9},{9,137},{137,1},{2... | collective-permute-start | bytes 786440 | tf_op jit(solution)/shard_map/ppermute | solution.py:204
  143.3 9.4 %collective-permute-start.15 = (bf16[2,64,1024]{2,1,0:T(8,128)(2,1)S(1)}, bf16[2,64,1024]{2,1,0:T(8,128)(2,1)S(1)}, u32[]{:S(2)}, u32[]{:S(2)}) collective-permute-start(bf16[2,64,1024]{2,1,0:T(8,128)(2,1)S(1)} %collective-permute-done.7.refs_6_), channel_id=1, source_target_pairs={{0,16},{16,0},{1,17},{17,1},{2,18},{18,2},{3,19},{19,3},{4,20},{20... | collective-permute-start | bytes 786440 | tf_op jit(solution)/shard_map/ppermute | solution.py:219
  145.8 8.4 %collective-permute-start.9 = (bf16[2,64,1024]{2,1,0:T(8,128)(2,1)S(1)}, bf16[2,64,1024]{2,1,0:T(8,128)(2,1)}, u32[]{:S(2)}, u32[]{:S(2)}) collective-permute-start(bf16[2,64,1024]{2,1,0:T(8,128)(2,1)S(1)} %collective-permute-done.7.refs_6_), channel_id=1, source_target_pairs={{0,96},{32,0},{64,32},{96,64},{1,97},{33,1},{65,33},{97,65},{2,98}... | collective-permute-start | bytes 786440 | tf_op jit(solution)/shard_map/ppermute | solution.py:204
  148.9 8.2 %collective-permute-start.14 = (bf16[2,64,1024]{2,1,0:T(8,128)(2,1)S(1)}, bf16[2,64,1024]{2,1,0:T(8,128)(2,1)S(1)}, u32[]{:S(2)}, u32[]{:S(2)}) collective-permute-start(bf16[2,64,1024]{2,1,0:T(8,128)(2,1)S(1)} %collective-permute-done.6.refs_5_), channel_id=1, source_target_pairs={{0,16},{16,0},{1,17},{17,1},{2,18},{18,2},{3,19},{19,3},{4,20},{20... | collective-permute-start | bytes 786440 | tf_op jit(solution)/shard_map/ppermute | solution.py:219
  150.6 8.3 %collective-permute-start.12 = (bf16[2,64,1024]{2,1,0:T(8,128)(2,1)S(1)}, bf16[2,64,1024]{2,1,0:T(8,128)(2,1)S(1)}, u32[]{:S(2)}, u32[]{:S(2)}) collective-permute-start(bf16[2,64,1024]{2,1,0:T(8,128)(2,1)S(1)} %collective-permute-done.4.refs_3_), channel_id=1, source_target_pairs={{0,16},{16,0},{1,17},{17,1},{2,18},{18,2},{3,19},{19,3},{4,20},{20... | collective-permute-start | bytes 786440 | tf_op jit(solution)/shard_map/ppermute | solution.py:219
  153.5 9.2 %collective-permute-start.8 = (bf16[2,64,1024]{2,1,0:T(8,128)(2,1)S(1)}, bf16[2,64,1024]{2,1,0:T(8,128)(2,1)}, u32[]{:S(2)}, u32[]{:S(2)}) collective-permute-start(bf16[2,64,1024]{2,1,0:T(8,128)(2,1)S(1)} %collective-permute-done.4.refs_3_), channel_id=1, source_target_pairs={{0,32},{32,64},{64,96},{96,0},{1,33},{33,65},{65,97},{97,1},{2,34}... | collective-permute-start | bytes 786440 | tf_op jit(solution)/shard_map/ppermute | solution.py:204
  154.2 8.5 %collective-permute-start.32 = (bf16[2,64,1024]{2,1,0:T(8,128)(2,1)S(1)}, bf16[2,64,1024]{2,1,0:T(8,128)(2,1)S(1)}, u32[]{:S(2)}, u32[]{:S(2)}) collective-permute-start(bf16[2,64,1024]{2,1,0:T(8,128)(2,1)S(1)} %collective-permute-done.24.refs_22_), channel_id=1, source_target_pairs={{0,16},{16,0},{1,17},{17,1},{2,18},{18,2},{3,19},{19,3},{4,20},{20... | collective-permute-start | bytes 786440 | tf_op jit(solution)/shard_map/ppermute | solution.py:219
  155.3 8.9 %collective-permute-start.26 = (bf16[2,64,1024]{2,1,0:T(8,128)(2,1)S(1)}, bf16[2,64,1024]{2,1,0:T(8,128)(2,1)}, u32[]{:S(2)}, u32[]{:S(2)}) collective-permute-start(bf16[2,64,1024]{2,1,0:T(8,128)(2,1)S(1)} %collective-permute-done.24.refs_22_), channel_id=1, source_target_pairs={{0,136},{128,0},{8,128},{136,8},{1,137},{129,1},{9,129},{137,9},{2... | collective-permute-start | bytes 786440 | tf_op jit(solution)/shard_map/ppermute | solution.py:204
  162.6 8.5 %collective-permute-start.25 = (bf16[2,64,1024]{2,1,0:T(8,128)(2,1)}, bf16[2,64,1024]{2,1,0:T(8,128)(2,1)}, u32[]{:S(2)}, u32[]{:S(2)}) collective-permute-start(bf16[2,64,1024]{2,1,0:T(8,128)(2,1)} %collective-permute-done.21.refs_19_), channel_id=1, source_target_pairs={{0,128},{128,8},{8,136},{136,0},{1,129},{129,9},{9,137},{137,1},{2... | collective-permute-start | bytes 786440 | tf_op jit(solution)/shard_map/ppermute | solution.py:204
  163.4 11.1 %collective-permute-start.29 = (bf16[2,64,1024]{2,1,0:T(8,128)(2,1)}, bf16[2,64,1024]{2,1,0:T(8,128)(2,1)}, u32[]{:S(2)}, u32[]{:S(2)}) collective-permute-start(bf16[2,64,1024]{2,1,0:T(8,128)(2,1)} %collective-permute-done.21.refs_19_), channel_id=1, source_target_pairs={{0,16},{16,0},{1,17},{17,1},{2,18},{18,2},{3,19},{19,3},{4,20},{20... | collective-permute-start | bytes 786440 | tf_op jit(solution)/shard_map/ppermute | solution.py:219
  164.2 10.3 %collective-permute-start.17 = (bf16[2,64,1024]{2,1,0:T(8,128)(2,1)}, bf16[2,64,1024]{2,1,0:T(8,128)(2,1)}, u32[]{:S(2)}, u32[]{:S(2)}) collective-permute-start(bf16[2,64,1024]{2,1,0:T(8,128)(2,1)} %collective-permute-done.9.refs_8_), channel_id=1, source_target_pairs={{0,16},{16,0},{1,17},{17,1},{2,18},{18,2},{3,19},{19,3},{4,20},{20... | collective-permute-start | bytes 786440 | tf_op jit(solution)/shard_map/ppermute | solution.py:219
  164.9 9.6 %collective-permute-start.16 = (bf16[2,64,1024]{2,1,0:T(8,128)(2,1)}, bf16[2,64,1024]{2,1,0:T(8,128)(2,1)}, u32[]{:S(2)}, u32[]{:S(2)}) collective-permute-start(bf16[2,64,1024]{2,1,0:T(8,128)(2,1)} %collective-permute-done.8.refs_7_), channel_id=1, source_target_pairs={{0,16},{16,0},{1,17},{17,1},{2,18},{18,2},{3,19},{19,3},{4,20},{20... | collective-permute-start | bytes 786440 | tf_op jit(solution)/shard_map/ppermute | solution.py:219
  166.1 8.4 %collective-permute-start.34 = (bf16[2,64,1024]{2,1,0:T(8,128)(2,1)}, bf16[2,64,1024]{2,1,0:T(8,128)(2,1)}, u32[]{:S(2)}, u32[]{:S(2)}) collective-permute-start(bf16[2,64,1024]{2,1,0:T(8,128)(2,1)} %collective-permute-done.26.refs_24_), channel_id=1, source_target_pairs={{0,16},{16,0},{1,17},{17,1},{2,18},{18,2},{3,19},{19,3},{4,20},{20... | collective-permute-start | bytes 786440 | tf_op jit(solution)/shard_map/ppermute | solution.py:219
  (48 other events, 239.5 us)

commit v4 on v2

v4 whole, which is shorter than its diff:
```python
import functools
import math

import jax
import jax.numpy as jnp
from jax import lax
from jax.experimental import pallas as pl
from jax.experimental.pallas import tpu as pltpu
from jax.sharding import Mesh
from jax.sharding import PartitionSpec as P

BLK = ("blk_0", "blk_1", "blk_2")
WALK = ("walk_0", "walk_1")
ALL = BLK + WALK
ROWS = 16


def theta_kernel(inv_ref, walkers_ref, chol_ref, out_ref):
    blocks, both, padded, width = out_ref.shape
    wdev = walkers_ref.shape[0]
    occupied = chol_ref.shape[1]
    for k in range(blocks):
        columns = slice(k * width, (k + 1) * width)
        for w in range(wdev):
            theta = jnp.dot(
                inv_ref[w], walkers_ref[w, :, columns], preferred_element_type=jnp.float32
            )
            out_ref[k, w] = theta.astype(out_ref.dtype)
        for g in range(both - wdev):
            rows = chol_ref[g, :, columns]
            rest = jnp.zeros((padded - occupied, width), rows.dtype)
            out_ref[k, wdev + g] = jnp.concatenate([rows, rest], axis=0)


def theta_and_chol(inv, walkers, chol, blocks):
    wdev, padded, double_rows = inv.shape
    orbitals = walkers.shape[2]
    shape = (blocks, wdev + chol.shape[0], padded, orbitals // blocks)
    return pl.pallas_call(
        theta_kernel,
        out_shape=jax.ShapeDtypeStruct(shape, jnp.bfloat16),
        in_specs=[pl.BlockSpec(memory_space=pltpu.VMEM)] * 3,
        out_specs=pl.BlockSpec(memory_space=pltpu.VMEM),
        cost_estimate=pl.CostEstimate(
            flops=2 * wdev * padded * double_rows * orbitals,
            bytes_accessed=2 * (walkers.size + chol.size + math.prod(shape)),
            transcendentals=0,
        ),
        compiler_params=pltpu.CompilerParams(vmem_limit_bytes=16 * 1024 * 1024),
    )(inv, walkers, chol)


def bias_kernel(wdev, both_ref, out_ref):
    blocks, both, padded, lanes = both_ref.shape
    vdev = both - wdev
    walkers, vectors = blocks * wdev, blocks * vdev
    m, n = walkers * ROWS, vectors * ROWS
    total = jnp.zeros((m, n), jnp.float32)
    for t in range(padded // ROWS):
        rows = slice(t * ROWS, (t + 1) * ROWS)
        a = both_ref[:, :wdev, rows, :].reshape(m, lanes)
        b = both_ref[:, wdev:, rows, :].reshape(n, lanes)
        total = total + lax.dot_general(
            a, b, (((1,), (1,)), ((), ())), preferred_element_type=jnp.float32
        )
    row = lax.broadcasted_iota(jnp.int32, (m, n), 0) % ROWS
    col = lax.broadcasted_iota(jnp.int32, (m, n), 1) % ROWS
    kept = jnp.where(row == col, total, 0.0)
    by_walker = kept.reshape(walkers, ROWS, n).sum(axis=1)
    group = lax.broadcasted_iota(jnp.int32, (n, vectors), 0) // ROWS
    vector = lax.broadcasted_iota(jnp.int32, (n, vectors), 1)
    pick = (group == vector).astype(jnp.float32)
    out_ref[...] = jnp.dot(
        by_walker, pick, preferred_element_type=jnp.float32, precision=lax.Precision.HIGHEST
    )


def partial_bias(both, wdev):
    blocks, held, padded, lanes = both.shape
    walkers, vectors = blocks * wdev, blocks * (held - wdev)
    return pl.pallas_call(
        functools.partial(bias_kernel, wdev),
        out_shape=jax.ShapeDtypeStruct((walkers, vectors), jnp.float32),
        in_specs=[pl.BlockSpec(memory_space=pltpu.VMEM)],
        out_specs=pl.BlockSpec(memory_space=pltpu.VMEM),
        cost_estimate=pl.CostEstimate(
            flops=2 * walkers * vectors * ROWS * padded * lanes,
            bytes_accessed=2 * both.size,
            transcendentals=0,
        ),
        compiler_params=pltpu.CompilerParams(vmem_limit_bytes=16 * 1024 * 1024),
    )(both)


AROUND = (0, -1, 1, 2)
NEAR, NEXT = AROUND[:2], AROUND[2:]
HELD = ((NEAR, 0), (NEXT, 0), (NEAR, -1), (NEXT, -1), (NEAR, 1), (NEXT, 1), (NEAR, 2), (NEXT, 2))


def assembly_kernel(*refs):
    blocks, out_ref, sems = refs[: 2 * len(HELD)], refs[2 * len(HELD)], refs[2 * len(HELD) + 1]
    height, width = blocks[0].shape[2:]
    x = lax.axis_index("walk_0") * 2 + lax.axis_index("blk_0")
    y, core = lax.axis_index("blk_1"), lax.axis_index("blk_2")
    copies = []
    for other in (0, 1):
        colour = core if other == 0 else 1 - core
        for array, (kept, far) in enumerate(HELD):
            for k, near in enumerate(kept):
                dx = near + colour * (far - near)
                dy = far + colour * (near - far)
                bx, by = (x + dx + 4) % 4, (y + dy + 4) % 4
                for side in (0, 1):
                    bc = colour if side == 0 else 1 - colour
                    row = (((bx % 2) * 4 + by) * 2 + bc) * 2 * height + (bx // 2) * height
                    row = pl.multiple_of(row, height)
                    column = pl.multiple_of(colour * width, width)
                    copy = pltpu.make_async_copy(
                        blocks[other * len(HELD) + array].at[k, side],
                        out_ref.at[pl.ds(row, height), pl.ds(column, width)],
                        sems.at[len(copies)],
                    )
                    copy.start()
                    copies.append(copy)
    for copy in copies:
        copy.wait()


def assembled(blocks, orbitals):
    return pl.pallas_call(
        assembly_kernel,
        out_shape=jax.ShapeDtypeStruct((orbitals, orbitals), jnp.bfloat16),
        in_specs=[pl.BlockSpec(memory_space=pl.ANY)] * len(blocks),
        out_specs=pl.BlockSpec(memory_space=pltpu.VMEM),
        scratch_shapes=[pltpu.SemaphoreType.DMA((4 * len(blocks),))],
        cost_estimate=pl.CostEstimate(
            flops=orbitals * orbitals, bytes_accessed=4 * orbitals * orbitals, transcendentals=0
        ),
        compiler_params=pltpu.CompilerParams(vmem_limit_bytes=16 * 1024 * 1024),
    )(*blocks)


CHIP = ("blk_0", "blk_1", "blk_2", "walk_0")


def stepped(array, first, steps):
    def device(x, y, core):
        return (((x % 2) * 4 + y % 4) * 2 + core) * 2 + x % 4 // 2

    pairs = []
    for x in range(4):
        for y in range(4):
            for core in (0, 1):
                along_x = first == (core == 0)
                to = (x + steps, y) if along_x else (x, y + steps)
                pairs.append((device(x, y, core), device(*to, core)))
    return lax.ppermute(array, CHIP, pairs)


def other_core(array):
    return lax.ppermute(array, "blk_2", [(0, 1), (1, 0)])


def gathered(rows, core):
    width = rows.shape[1] // 2
    own = lax.dynamic_slice_in_dim(rows, core * width, width, 1, allow_negative_indices=False)
    given = lax.dynamic_slice_in_dim(rows, (1 - core) * width, width, 1, allow_negative_indices=False)
    own = jnp.stack([own, other_core(given)])
    came = [own] + [stepped(own, True, -step) for step in AROUND[1:]]
    near, next_ = jnp.stack(came[:2]), jnp.stack(came[2:])
    below, above = stepped(near, False, 1), stepped(next_, False, -1)
    below_next, above_near = stepped(next_, False, 1), stepped(near, False, -1)
    far = [stepped(below, False, 1), stepped(above, False, -1)]
    held = [near, next_, below, below_next, above_near, above] + far
    return held + [other_core(array) for array in held]


def copy_kernel(in_ref, out_ref):
    out_ref[...] = in_ref[...]


def copied(array):
    return pl.pallas_call(
        copy_kernel,
        out_shape=jax.ShapeDtypeStruct(array.shape, array.dtype),
        in_specs=[pl.BlockSpec(memory_space=pltpu.VMEM)],
        out_specs=pl.BlockSpec(memory_space=pltpu.VMEM),
        cost_estimate=pl.CostEstimate(
            flops=array.size, bytes_accessed=4 * array.size, transcendentals=0
        ),
        compiler_params=pltpu.CompilerParams(vmem_limit_bytes=4 * 1024 * 1024),
    )(array)


def at(array, index, dim):
    return lax.dynamic_index_in_dim(array, index, dim, keepdims=False, allow_negative_indices=False)


def exchanged(blocks, axes):
    return lax.all_to_all(blocks, axes, split_axis=0, concat_axis=0, tiled=True)


def part(walkers, inv_intersection, rotated_chol, full_chol, field_noise):
    wdev, double_rows, orbitals = walkers.shape
    occupied = double_rows // 2
    n_blk, n_walk = lax.axis_size(BLK), lax.axis_size(WALK)
    n_all = n_blk * n_walk
    padded = -(-occupied // ROWS) * ROWS

    inv = jnp.moveaxis(inv_intersection, 1, 2).reshape(wdev, occupied, double_rows)
    inv = jnp.pad(inv, ((0, 0), (0, padded - occupied), (0, 0)))
    both = theta_and_chol(inv, walkers, rotated_chol, n_blk)
    both = exchanged(both, BLK)
    own = full_chol.shape[0]
    n_z = lax.axis_size("walk_1")
    half, at_z = lax.axis_index("walk_0"), lax.axis_index("walk_1")
    raw = full_chol.reshape(own, 2, n_z, -1, orbitals)

    def for_z(step):
        return at(raw, lax.rem(at_z + step, n_z), 2)

    slices = [for_z(step) for step in range(n_z)]
    raws = [copied(slices[0])]
    for step, rows in enumerate(slices[1:], 1):
        pairs = [(k, (k + step) % n_z) for k in range(n_z)]
        raws.append(lax.ppermute(rows, "walk_1", pairs))
    partial = partial_bias(both, wdev)
    vectors = partial.shape[1]

    summed = jnp.sum(partial, axis=0)
    rows = jnp.concatenate(
        [jnp.broadcast_to(summed, (n_blk, vectors)), partial.reshape(n_blk, wdev * vectors)], axis=1
    )
    rows = jnp.pad(rows, ((0, 0), (0, 128 - rows.shape[1])))
    rows = jnp.broadcast_to(rows[:, None, None], (n_blk, n_walk, 1, 128))
    core = lax.axis_index("blk_2")
    rows, half, at_z, core = lax.optimization_barrier((rows, half, at_z, core))
    rows = exchanged(rows.reshape(n_all, 1, 128), ALL)
    rows, half, at_z, core = lax.optimization_barrier((rows, half, at_z, core))
    rows = rows.reshape(n_blk, n_walk, 128)
    bias_shift = jnp.sum(rows, axis=(0, 1))[:vectors] / math.sqrt(wdev * n_all)
    peers = at(rows, half * n_z + at_z, 1)
    bias = jnp.sum(peers, axis=0)[vectors : vectors + wdev * vectors].reshape(wdev, vectors)

    shifted = 0.1 * (field_noise - bias_shift)
    entry = lax.broadcasted_iota(jnp.int32, (n_z * own, vectors), 0)
    vector = lax.broadcasted_iota(jnp.int32, (n_z * own, vectors), 1)
    source = at_z - entry // own
    source = jnp.where(source < 0, source + n_z, source)
    wanted = (half * n_z + source) * own + entry % own
    scale = jnp.sum(jnp.where(vector == wanted, shifted[None, :], 0.0), axis=1)
    part_field = sum(
        scale[step * own + k] * raws[step][k].astype(jnp.float32)
        for step in range(n_z)
        for k in range(own)
    )
    kept = at(part_field, half, 0)
    given = at(part_field, 1 - half, 0)
    came = lax.ppermute(given, "walk_0", [(0, 1), (1, 0)])
    piece = (kept + came).astype(jnp.bfloat16)
    pieces = exchanged(jnp.broadcast_to(piece[None], (n_z, *piece.shape)), "walk_1")
    field = assembled(gathered(pieces.reshape(-1, orbitals), core), orbitals)
    current = walkers.reshape(wdev * double_rows, orbitals)
    total = current.astype(jnp.float32)
    for order in range(1, 5):
        current = (jnp.dot(current, field, preferred_element_type=jnp.float32) / order).astype(
            jnp.bfloat16
        )
        total = total + current.astype(jnp.float32)
    propagated = total.astype(jnp.bfloat16).reshape(walkers.shape)
    return propagated, bias, bias_shift


def solution(mesh):
    torus = Mesh(mesh.devices.reshape(2, 4, 2, 2, 8), ALL)
    in_specs = (
        P(ALL, None, None),
        P(ALL, None, None, None),
        P(BLK, None, None),
        P(WALK, BLK, None),
        P(),
    )
    out_specs = (P(ALL, None, None), P(ALL, None), P())
    return jax.shard_map(part, mesh=torus, in_specs=in_specs, out_specs=out_specs, check_vma=False)
```

time: 202 us -> 171 us (0.85)
  blocking collectives: 72.9 us -> 0 us
  waiting for transfers between devices: 38.6 us -> 61 us
  Pallas kernels: 26.4 us -> 5.56 us
  starting transfers between devices: 45.5 us -> 62.6 us
  matrix products: 0 us -> 15.9 us
  other arithmetic: 1.68 us -> 11.4 us
  local copies, waits for them, and re-layouts: 15 us -> 12.6 us
    all_to_all x4 -> x0, blocking collectives: 72.9 us -> none  [exchanged(): return lax.all_to_all(blocks, axes, split_axis=0, concat_axis=0, tiled=True)]
    pallas_call x1 -> x2, Pallas kernels: 24.3 us -> 3.46 us  [the longest x1 3.45 us: assembled(): pl.pallas_call(assembly_kernel, out_shape=jax.ShapeDtypeStruct((orbitals,...]
    all_to_all x1 -> x3, waiting for transfers between devices: 12.6 us -> 31.9 us  [exchanged(): return lax.all_to_all(blocks, axes, split_axis=0, concat_axis=0, tiled=True)]
    dot_general x0 -> x4, matrix products: none -> 15.9 us  [part(): jnp.dot(current, field, preferred_element_type=jnp.float32) / order]
    all_to_all x1 -> x3, starting transfers between devices: 12.5 us -> 25.7 us  [exchanged(): return lax.all_to_all(blocks, axes, split_axis=0, concat_axis=0, tiled=True)]
    add x0 -> x2, other arithmetic: none -> 10.1 us  [the longest x1 10.1 us: part(): sum((scale[step * own + k] * raws[step][k].astype(jnp.float32) for step i...]
    ppermute x14 -> x17, starting transfers between devices: 16.2 us -> 26.2 us  [the longest x7 16.4 us: part(): raws.append(lax.ppermute(rows, 'walk_1', pairs))]
    ppermute x10 -> x9, starting transfers between devices: 16.8 us -> 10.6 us  [other_core(): return lax.ppermute(array, 'blk_2', [(0, 1), (1, 0)])]
  transfers between devices with their start and end apart: 25 -> 29, of which waited for: 7 -> 14; matrix products, arithmetic and copies ran while one was open for 1% -> 3% of each run, Pallas kernels for 0% -> 1%
where the time goes in v4:
time: 171 us; the launch traced here: 170 us
  starting transfers between devices  62.6 us (37%)
  waiting for transfers between devices  61 us (36%)
  matrix products  15.9 us (9%)
  local copies, waits for them, and re-layouts  12.6 us (7%)
  other arithmetic  11.4 us (7%)
  Pallas kernels  5.56 us (3%)
    all_to_all x3, waiting for transfers between devices, exchanged(): return lax.all_to_all(blocks, axes, split_axis=0, concat_axis=0, tiled=True)  31.9 us
    all_to_all x3, starting transfers between devices, exchanged(): return lax.all_to_all(blocks, axes, split_axis=0, concat_axis=0, tiled=True)  25.7 us
    ppermute x9, waiting for transfers between devices, stepped(): return lax.ppermute(array, CHIP, pairs)  23 us
    ppermute x7, starting transfers between devices, part(): raws.append(lax.ppermute(rows, 'walk_1', pairs))  16.4 us
    dot_general x4, matrix products, part(): jnp.dot(current, field, preferred_element_type=jnp.float32) / order  15.9 us
    ppermute x9, starting transfers between devices, other_core(): return lax.ppermute(array, 'blk_2', [(0, 1), (1, 0)])  10.6 us
    add x1, other arithmetic, part(): sum((scale[step * own + k] * raws[step][k].astype(jnp.float32) for step i...  10.1 us
    unnamed x19, local copies, waits for them, and re-layouts  7.76 us
  transfers between devices with their start and end apart: 29, of which 14 were waited for; matrix products, arithmetic and copies ran while one was open for 3% of the time, Pallas kernels for 1%

profile of v4, /device:TPU:1, one launch (start us, length us, event | category | flops | bytes accessed | tf_op | source)
XLA Modules:
  0.0 169.9 jit_solution(7625006918243228531)
XLA Ops:
  6.5 6.9 %all-to-all-start = ((bf16[16,4,112,128]{3,2,1,0:T(8,128)(2,1)}), bf16[16,4,112,128]{3,2,1,0:T(8,128)(2,1)S(1)}, u32[]{:S(2)}, u32[]{:S(2)}) async-start(bf16[16,4,112,128]{3,2,1,0:T(8,128)(2,1)} %copy-done), calls=%async_computation | async-start | bytes 3670016 | tf_op jit(solution)/shard_map/all_to_all | solution.py:200
  14.2 6.0 %collective-permute-start.5 = (bf16[2,2,8,2048]{3,2,1,0:T(8,128)(2,1)}, bf16[2,2,8,2048]{3,2,1,0:T(8,128)(2,1)S(1)}, u32[]{:S(2)}, u32[]{:S(2)}) collective-permute-start(bf16[2,2,8,2048]{3,2,1,0:T(8,128)(2,1)} %get-tuple-element.22), channel_id=1, source_target_pairs={{0,6},{1,7},{2,0},{3,1},{4,2},{5,3},{6,4},{7,5},{8,14},{9,15},{10,... | collective-permute-start | bytes 393224 | tf_op jit(solution)/shard_map/ppermute | solution.py:226
  21.0 4.2 %collective-permute-start.3 = (bf16[2,2,8,2048]{3,2,1,0:T(8,128)(2,1)}, bf16[2,2,8,2048]{3,2,1,0:T(8,128)(2,1)S(1)}, u32[]{:S(2)}, u32[]{:S(2)}) collective-permute-start(bf16[2,2,8,2048]{3,2,1,0:T(8,128)(2,1)} %get-tuple-element.24), channel_id=1, source_target_pairs={{0,4},{1,5},{2,6},{3,7},{4,0},{5,1},{6,2},{7,3},{8,12},{9,13},{10,... | collective-permute-start | bytes 393224 | tf_op jit(solution)/shard_map/ppermute | solution.py:226
  25.2 2.8 %collective-permute-start.1 = (bf16[2,2,8,2048]{3,2,1,0:T(8,128)(2,1)S(1)}, bf16[2,2,8,2048]{3,2,1,0:T(8,128)(2,1)S(1)}, u32[]{:S(2)}, u32[]{:S(2)}) collective-permute-start(bf16[2,2,8,2048]{3,2,1,0:T(8,128)(2,1)S(1)} %get-tuple-element.26), channel_id=1, source_target_pairs={{0,2},{1,3},{2,4},{3,5},{4,6},{5,7},{6,0},{7,1},{8,10},{9,11},{10,... | collective-permute-start | bytes 393224 | tf_op jit(solution)/shard_map/ppermute | solution.py:226
  28.0 9.9 %all-to-all-done.both_ref = bf16[16,4,112,128]{3,2,1,0:T(8,128)(2,1)S(1)} async-done(((bf16[16,4,112,128]{3,2,1,0:T(8,128)(2,1)}), bf16[16,4,112,128]{3,2,1,0:T(8,128)(2,1)S(1)}, u32[]{:S(2)}, u32[]{:S(2)}) %all-to-all-start) | async-done | bytes 1835040 | tf_op jit(solution)/shard_map/all_to_all | solution.py:200
  40.1 14.8 %all-to-all-start.1 = ((f32[256,1,128]{2,1,0:T(1,128)}), f32[256,1,128]{2,1,0:T(1,128)S(1)}, u32[]{:S(2)}, u32[]{:S(2)}) async-start(f32[256,1,128]{2,1,0:T(1,128)} %bitcast.2), calls=%async_computation.1 | async-start | bytes 262144 | tf_op jit(solution)/shard_map/all_to_all | solution.py:200
  55.0 12.6 %all-to-all-done.1 = f32[256,1,128]{2,1,0:T(1,128)S(1)} async-done(((f32[256,1,128]{2,1,0:T(1,128)}), f32[256,1,128]{2,1,0:T(1,128)S(1)}, u32[]{:S(2)}, u32[]{:S(2)}) %all-to-all-start.1) | async-done | bytes 131104 | tf_op jit(solution)/shard_map/all_to_all | solution.py:200
  73.5 10.1 %bitcast_add_fusion.1 = f32[2,8,2048]{2,1,0:T(8,128)S(1)} fusion(bf16[2,2,8,2048]{3,2,1,0:T(8,128)(2,1)S(1)} %collective-permute-done.6, bf16[2,2,8,2048]{3,2,1,0:T(8,128)(2,1)S(1)} %collective-permute-done.5, bf16[2,2,8,2048]{3,2,1,0:T(8,128)(2,1)S(1)} %collective-permute-done.4, bf16[2,2,8,2048]{3,2,1,0:T(8,128)(2,1)S(1)} %collective-permute-done.3, ...), kind=kLoop, calls=%fused_computation.12 | loop fusion | flops 1540096 | bytes 1179712 | tf_op jit(solution)/shard_map/add | solution.py:252
  85.8 2.5 %collective-permute-done.7 = f32[8,2048]{1,0:T(8,128)S(1)} collective-permute-done((f32[8,2048]{1,0:T(8,128)S(1)}, f32[8,2048]{1,0:T(8,128)S(1)}, u32[]{:S(2)}, u32[]{:S(2)}) %collective-permute-start.7) | collective-permute-done | bytes 65568 | tf_op jit(solution)/shard_map/ppermute | solution.py:259
  89.0 4.0 %all-to-all-start.2 = ((bf16[8,8,2048]{2,1,0:T(8,128)(2,1)}), bf16[8,8,2048]{2,1,0:T(8,128)(2,1)S(1)}, u32[]{:S(2)}, u32[]{:S(2)}) async-start(bf16[8,8,2048]{2,1,0:T(8,128)(2,1)} %broadcast_in_dim.32), calls=%async_computation.2 | async-start | bytes 524288 | tf_op jit(solution)/shard_map/all_to_all | solution.py:200
  93.0 9.4 %all-to-all-done.2 = bf16[8,8,2048]{2,1,0:T(8,128)(2,1)S(1)} async-done(((bf16[8,8,2048]{2,1,0:T(8,128)(2,1)}), bf16[8,8,2048]{2,1,0:T(8,128)(2,1)S(1)}, u32[]{:S(2)}, u32[]{:S(2)}) %all-to-all-start.2) | async-done | bytes 262176 | tf_op jit(solution)/shard_map/all_to_all | solution.py:200
  102.4 5.1 %collective-permute-start.8 = (bf16[64,1024]{1,0:T(8,128)(2,1)S(1)}, bf16[64,1024]{1,0:T(8,128)(2,1)S(1)}, u32[]{:S(2)}, u32[]{:S(2)}) collective-permute-start(bf16[64,1024]{1,0:T(8,128)(2,1)S(1)} %get-tuple-element.32), channel_id=1, source_target_pairs={{0,16},{16,0},{1,17},{17,1},{2,18},{18,2},{3,19},{19,3},{4,20},{20... | collective-permute-start | bytes 393224 | tf_op jit(solution)/shard_map/ppermute | solution.py:161
  110.8 3.3 %collective-permute-done.10 = bf16[2,64,1024]{2,1,0:T(8,128)(2,1)S(1)} collective-permute-done((bf16[2,64,1024]{2,1,0:T(8,128)(2,1)S(1)}, bf16[2,64,1024]{2,1,0:T(8,128)(2,1)S(1)}, u32[]{:S(2)}, u32[]{:S(2)}) %collective-permute-start.10) | collective-permute-done | bytes 262176 | tf_op jit(solution)/shard_map/ppermute | solution.py:157
  118.0 2.7 %collective-permute-start.15 = (bf16[2,2,64,1024]{3,2,1,0:T(8,128)(2,1)S(1)}, bf16[2,2,64,1024]{3,2,1,0:T(8,128)(2,1)S(1)}, u32[]{:S(2)}, u32[]{:S(2)}) collective-permute-start(bf16[2,2,64,1024]{3,2,1,0:T(8,128)(2,1)S(1)} %pad_maximum_fusion.1.refs_1_), channel_id=1, source_target_pairs={{0,96},{16,152},{32,0},{48,184},{64,32},{80,216},{96,64},{112,248}... | collective-permute-start | bytes 1572872 | tf_op jit(solution)/shard_map/ppermute | solution.py:157
  121.1 2.6 %collective-permute-start.14 = (bf16[2,2,64,1024]{3,2,1,0:T(8,128)(2,1)S(1)}, bf16[2,2,64,1024]{3,2,1,0:T(8,128)(2,1)}, u32[]{:S(2)}, u32[]{:S(2)}) collective-permute-start(bf16[2,2,64,1024]{3,2,1,0:T(8,128)(2,1)S(1)} %pad_maximum_fusion.refs_0_), channel_id=1, source_target_pairs={{0,96},{16,152},{32,0},{48,184},{64,32},{80,216},{96,64},{112,248}... | collective-permute-start | bytes 1572872 | tf_op jit(solution)/shard_map/ppermute | solution.py:157
  123.7 3.1 %collective-permute-done.15.refs_5_ = bf16[2,2,64,1024]{3,2,1,0:T(8,128)(2,1)S(1)} collective-permute-done((bf16[2,2,64,1024]{3,2,1,0:T(8,128)(2,1)S(1)}, bf16[2,2,64,1024]{3,2,1,0:T(8,128)(2,1)S(1)}, u32[]{:S(2)}, u32[]{:S(2)}) %collective-permute-start.15) | collective-permute-done | bytes 524320 | tf_op jit(solution)/shard_map/ppermute | solution.py:157
  127.3 3.0 %collective-permute-done.13.refs_3_ = bf16[2,2,64,1024]{3,2,1,0:T(8,128)(2,1)S(1)} collective-permute-done((bf16[2,2,64,1024]{3,2,1,0:T(8,128)(2,1)S(1)}, bf16[2,2,64,1024]{3,2,1,0:T(8,128)(2,1)S(1)}, u32[]{:S(2)}, u32[]{:S(2)}) %collective-permute-start.13) | collective-permute-done | bytes 524320 | tf_op jit(solution)/shard_map/ppermute | solution.py:157
  130.2 5.3 %collective-permute-done.12.refs_2_ = bf16[2,2,64,1024]{3,2,1,0:T(8,128)(2,1)S(1)} collective-permute-done((bf16[2,2,64,1024]{3,2,1,0:T(8,128)(2,1)S(1)}, bf16[2,2,64,1024]{3,2,1,0:T(8,128)(2,1)S(1)}, u32[]{:S(2)}, u32[]{:S(2)}) %collective-permute-start.12) | collective-permute-done | bytes 524320 | tf_op jit(solution)/shard_map/ppermute | solution.py:157
  139.7 5.6 %collective-permute-done.16.refs_6_ = bf16[2,2,64,1024]{3,2,1,0:T(8,128)(2,1)} collective-permute-done((bf16[2,2,64,1024]{3,2,1,0:T(8,128)(2,1)S(1)}, bf16[2,2,64,1024]{3,2,1,0:T(8,128)(2,1)}, u32[]{:S(2)}, u32[]{:S(2)}) %collective-permute-start.16) | collective-permute-done | bytes 524320 | tf_op jit(solution)/shard_map/ppermute | solution.py:157
  150.4 3.5 %shard_map.79 = bf16[2048,2048]{1,0:T(8,128)(2,1)S(1)} custom-call(bf16[2,2,64,1024]{3,2,1,0:T(8,128)(2,1)S(1)} %pad_maximum_fusion.refs_0_, bf16[2,2,64,1024]{3,2,1,0:T(8,128)(2,1)S(1)} %pad_maximum_fusion.1.refs_1_, bf16[2,2,64,1024]{3,2,1,0:T(8,128)(2,1)S(1)} %collective-permute-done.12.refs_2_, ...), custom_call_target="tpu_custom_call" | custom-call | flops 4194304 | bytes 16777216 | tf_op jit(solution)/shard_map/pallas_call | solution.py:130
  153.9 3.6 %convolution_convert_fusion = bf16[2048,400]{0,1:T(8,128)(2,1)S(1)} fusion(bf16[400,2048]{1,0:T(8,128)(2,1)S(1)} %bitcast.91, bf16[2048,2048]{1,0:T(8,128)(2,1)S(1)} %shard_map.79), kind=kOutput, calls=%fused_computation.8 | convolution fusion | flops 3356262400 | bytes 11665408 | tf_op jit(solution)/shard_map/dot_general | solution.py:266
  157.5 3.6 %multiply_convert_fusion.2 = bf16[400,2048]{1,0:T(8,128)(2,1)S(1)} fusion(bf16[2048,400]{0,1:T(8,128)(2,1)S(1)} %convolution_convert_fusion, bf16[2048,2048]{1,0:T(8,128)(2,1)S(1)} %shard_map.79), kind=kOutput, calls=%fused_computation.7 | convolution fusion | flops 3357081600 | bytes 11665408 | tf_op jit(solution)/shard_map/dot_general | solution.py:266
  161.2 3.6 %multiply_convert_fusion.1 = bf16[400,2048]{1,0:T(8,128)(2,1)S(1)} fusion(bf16[400,2048]{1,0:T(8,128)(2,1)S(1)} %multiply_convert_fusion.2, bf16[2048,2048]{1,0:T(8,128)(2,1)S(1)} %shard_map.79), kind=kOutput, calls=%fused_computation.6 | convolution fusion | flops 3357081600 | bytes 11665408 | tf_op jit(solution)/shard_map/dot_general | solution.py:266
  164.8 5.1 %fusion.3 = bf16[400,2048]{1,0:T(8,128)(2,1)} fusion(bf16[2048,400]{0,1:T(8,128)(2,1)S(1)} %convolution_convert_fusion, bf16[400,2048]{1,0:T(8,128)(2,1)S(1)} %multiply_convert_fusion.1, bf16[400,2048]{1,0:T(8,128)(2,1)S(1)} %multiply_convert_fusion.2, bf16[400,2048]{1,0:T(8,128)(2,1)S(1)} %bitcast.92, bf16[2048,2048]{1,0:T(8,128)(2,1)S(1)} %shard_map.79), kind=kOutput, calls=%fused_computation.4 | convolution fusion | flops 3365273600 | bytes 16580608 | tf_op jit(solution)/shard_map/dot_general | solution.py:266
  (88 shorter events, 35.6 us)
Async XLA Ops:
  6.5 31.4 %all-to-all-start = ((bf16[16,4,112,128]{3,2,1,0:T(8,128)(2,1)}), bf16[16,4,112,128]{3,2,1,0:T(8,128)(2,1)S(1)}, u32[]{:S(2)}, u32[]{:S(2)}) async-start(bf16[16,4,112,128]{3,2,1,0:T(8,128)(2,1)} %copy-done), calls=%async_computation | async-start | bytes 3670016 | tf_op jit(solution)/shard_map/all_to_all | solution.py:200
  14.2 54.2 %collective-permute-start.5 = (bf16[2,2,8,2048]{3,2,1,0:T(8,128)(2,1)}, bf16[2,2,8,2048]{3,2,1,0:T(8,128)(2,1)S(1)}, u32[]{:S(2)}, u32[]{:S(2)}) collective-permute-start(bf16[2,2,8,2048]{3,2,1,0:T(8,128)(2,1)} %get-tuple-element.22), channel_id=1, source_target_pairs={{0,6},{1,7},{2,0},{3,1},{4,2},{5,3},{6,4},{7,5},{8,14},{9,15},{10,... | collective-permute-start | bytes 393224 | tf_op jit(solution)/shard_map/ppermute | solution.py:226
  20.3 49.0 %collective-permute-start.4 = (bf16[2,2,8,2048]{3,2,1,0:T(8,128)(2,1)}, bf16[2,2,8,2048]{3,2,1,0:T(8,128)(2,1)S(1)}, u32[]{:S(2)}, u32[]{:S(2)}) collective-permute-start(bf16[2,2,8,2048]{3,2,1,0:T(8,128)(2,1)} %get-tuple-element.23), channel_id=1, source_target_pairs={{0,5},{1,6},{2,7},{3,0},{4,1},{5,2},{6,3},{7,4},{8,13},{9,14},{10,... | collective-permute-start | bytes 393224 | tf_op jit(solution)/shard_map/ppermute | solution.py:226
  21.0 51.1 %collective-permute-start.3 = (bf16[2,2,8,2048]{3,2,1,0:T(8,128)(2,1)}, bf16[2,2,8,2048]{3,2,1,0:T(8,128)(2,1)S(1)}, u32[]{:S(2)}, u32[]{:S(2)}) collective-permute-start(bf16[2,2,8,2048]{3,2,1,0:T(8,128)(2,1)} %get-tuple-element.24), channel_id=1, source_target_pairs={{0,4},{1,5},{2,6},{3,7},{4,0},{5,1},{6,2},{7,3},{8,12},{9,13},{10,... | collective-permute-start | bytes 393224 | tf_op jit(solution)/shard_map/ppermute | solution.py:226
  25.2 46.9 %collective-permute-start.2 = (bf16[2,2,8,2048]{3,2,1,0:T(8,128)(2,1)}, bf16[2,2,8,2048]{3,2,1,0:T(8,128)(2,1)S(1)}, u32[]{:S(2)}, u32[]{:S(2)}) collective-permute-start(bf16[2,2,8,2048]{3,2,1,0:T(8,128)(2,1)} %get-tuple-element.25), channel_id=1, source_target_pairs={{0,3},{1,4},{2,5},{3,6},{4,7},{5,0},{6,1},{7,2},{8,11},{9,12},{10,... | collective-permute-start | bytes 393224 | tf_op jit(solution)/shard_map/ppermute | solution.py:226
  25.2 46.9 %collective-permute-start.1 = (bf16[2,2,8,2048]{3,2,1,0:T(8,128)(2,1)S(1)}, bf16[2,2,8,2048]{3,2,1,0:T(8,128)(2,1)S(1)}, u32[]{:S(2)}, u32[]{:S(2)}) collective-permute-start(bf16[2,2,8,2048]{3,2,1,0:T(8,128)(2,1)S(1)} %get-tuple-element.26), channel_id=1, source_target_pairs={{0,2},{1,3},{2,4},{3,5},{4,6},{5,7},{6,0},{7,1},{8,10},{9,11},{10,... | collective-permute-start | bytes 393224 | tf_op jit(solution)/shard_map/ppermute | solution.py:226
  40.1 27.5 %all-to-all-start.1 = ((f32[256,1,128]{2,1,0:T(1,128)}), f32[256,1,128]{2,1,0:T(1,128)S(1)}, u32[]{:S(2)}, u32[]{:S(2)}) async-start(f32[256,1,128]{2,1,0:T(1,128)} %bitcast.2), calls=%async_computation.1 | async-start | bytes 262144 | tf_op jit(solution)/shard_map/all_to_all | solution.py:200
  89.0 13.3 %all-to-all-start.2 = ((bf16[8,8,2048]{2,1,0:T(8,128)(2,1)}), bf16[8,8,2048]{2,1,0:T(8,128)(2,1)S(1)}, u32[]{:S(2)}, u32[]{:S(2)}) async-start(bf16[8,8,2048]{2,1,0:T(8,128)(2,1)} %broadcast_in_dim.32), calls=%async_computation.2 | async-start | bytes 524288 | tf_op jit(solution)/shard_map/all_to_all | solution.py:200
  102.4 6.1 %collective-permute-start.8 = (bf16[64,1024]{1,0:T(8,128)(2,1)S(1)}, bf16[64,1024]{1,0:T(8,128)(2,1)S(1)}, u32[]{:S(2)}, u32[]{:S(2)}) collective-permute-start(bf16[64,1024]{1,0:T(8,128)(2,1)S(1)} %get-tuple-element.32), channel_id=1, source_target_pairs={{0,16},{16,0},{1,17},{17,1},{2,18},{18,2},{3,19},{19,3},{4,20},{20... | collective-permute-start | bytes 393224 | tf_op jit(solution)/shard_map/ppermute | solution.py:161
  108.5 5.6 %collective-permute-start.10 = (bf16[2,64,1024]{2,1,0:T(8,128)(2,1)S(1)}, bf16[2,64,1024]{2,1,0:T(8,128)(2,1)S(1)}, u32[]{:S(2)}, u32[]{:S(2)}) collective-permute-start(bf16[2,64,1024]{2,1,0:T(8,128)(2,1)S(1)} %get-tuple-element.30), channel_id=1, source_target_pairs={{0,136},{16,112},{32,168},{48,16},{64,200},{80,48},{96,232},{112,8... | collective-permute-start | bytes 786440 | tf_op jit(solution)/shard_map/ppermute | solution.py:157
  109.3 7.0 %collective-permute-start.11 = (bf16[2,64,1024]{2,1,0:T(8,128)(2,1)S(1)}, bf16[2,64,1024]{2,1,0:T(8,128)(2,1)S(1)}, u32[]{:S(2)}, u32[]{:S(2)}) collective-permute-start(bf16[2,64,1024]{2,1,0:T(8,128)(2,1)S(1)} %get-tuple-element.30), channel_id=1, source_target_pairs={{0,8},{16,80},{32,40},{48,112},{64,72},{80,16},{96,104},{112,48},{... | collective-permute-start | bytes 786440 | tf_op jit(solution)/shard_map/ppermute | solution.py:157
  110.8 9.9 %collective-permute-start.9 = (bf16[2,64,1024]{2,1,0:T(8,128)(2,1)S(1)}, bf16[2,64,1024]{2,1,0:T(8,128)(2,1)S(1)}, u32[]{:S(2)}, u32[]{:S(2)}) collective-permute-start(bf16[2,64,1024]{2,1,0:T(8,128)(2,1)S(1)} %get-tuple-element.30), channel_id=1, source_target_pairs={{0,128},{16,48},{32,160},{48,80},{64,192},{80,112},{96,224},{112,1... | collective-permute-start | bytes 786440 | tf_op jit(solution)/shard_map/ppermute | solution.py:157
  118.0 8.8 %collective-permute-start.15 = (bf16[2,2,64,1024]{3,2,1,0:T(8,128)(2,1)S(1)}, bf16[2,2,64,1024]{3,2,1,0:T(8,128)(2,1)S(1)}, u32[]{:S(2)}, u32[]{:S(2)}) collective-permute-start(bf16[2,2,64,1024]{3,2,1,0:T(8,128)(2,1)S(1)} %pad_maximum_fusion.1.refs_1_), channel_id=1, source_target_pairs={{0,96},{16,152},{32,0},{48,184},{64,32},{80,216},{96,64},{112,248}... | collective-permute-start | bytes 1572872 | tf_op jit(solution)/shard_map/ppermute | solution.py:157
  120.7 9.5 %collective-permute-start.13 = (bf16[2,2,64,1024]{3,2,1,0:T(8,128)(2,1)S(1)}, bf16[2,2,64,1024]{3,2,1,0:T(8,128)(2,1)S(1)}, u32[]{:S(2)}, u32[]{:S(2)}) collective-permute-start(bf16[2,2,64,1024]{3,2,1,0:T(8,128)(2,1)S(1)} %pad_maximum_fusion.1.refs_1_), channel_id=1, source_target_pairs={{0,32},{16,144},{32,64},{48,176},{64,96},{80,208},{96,0},{112,240}... | collective-permute-start | bytes 1572872 | tf_op jit(solution)/shard_map/ppermute | solution.py:157
  120.8 14.8 %collective-permute-start.12 = (bf16[2,2,64,1024]{3,2,1,0:T(8,128)(2,1)S(1)}, bf16[2,2,64,1024]{3,2,1,0:T(8,128)(2,1)S(1)}, u32[]{:S(2)}, u32[]{:S(2)}) collective-permute-start(bf16[2,2,64,1024]{3,2,1,0:T(8,128)(2,1)S(1)} %pad_maximum_fusion.refs_0_), channel_id=1, source_target_pairs={{0,32},{16,144},{32,64},{48,176},{64,96},{80,208},{96,0},{112,240}... | collective-permute-start | bytes 1572872 | tf_op jit(solution)/shard_map/ppermute | solution.py:157
  120.8 14.7 %collective-permute-start.18 = (bf16[2,2,64,1024]{3,2,1,0:T(8,128)(2,1)S(1)}, bf16[2,2,64,1024]{3,2,1,0:T(8,128)(2,1)S(1)}, u32[]{:S(2)}, u32[]{:S(2)}) collective-permute-start(bf16[2,2,64,1024]{3,2,1,0:T(8,128)(2,1)S(1)} %pad_maximum_fusion.refs_0_), channel_id=1, source_target_pairs={{0,16},{16,0},{1,17},{17,1},{2,18},{18,2},{3,19},{19,3},{4,20},{20... | collective-permute-start | bytes 1572872 | tf_op jit(solution)/shard_map/ppermute | solution.py:161
  121.1 15.7 %collective-permute-start.14 = (bf16[2,2,64,1024]{3,2,1,0:T(8,128)(2,1)S(1)}, bf16[2,2,64,1024]{3,2,1,0:T(8,128)(2,1)}, u32[]{:S(2)}, u32[]{:S(2)}) collective-permute-start(bf16[2,2,64,1024]{3,2,1,0:T(8,128)(2,1)S(1)} %pad_maximum_fusion.refs_0_), channel_id=1, source_target_pairs={{0,96},{16,152},{32,0},{48,184},{64,32},{80,216},{96,64},{112,248}... | collective-permute-start | bytes 1572872 | tf_op jit(solution)/shard_map/ppermute | solution.py:157
  126.8 10.1 %collective-permute-start.23 = (bf16[2,2,64,1024]{3,2,1,0:T(8,128)(2,1)S(1)}, bf16[2,2,64,1024]{3,2,1,0:T(8,128)(2,1)S(1)}, u32[]{:S(2)}, u32[]{:S(2)}) collective-permute-start(bf16[2,2,64,1024]{3,2,1,0:T(8,128)(2,1)S(1)} %collective-permute-done.15.refs_5_), channel_id=1, source_target_pairs={{0,16},{16,0},{1,17},{17,1},{2,18},{18,2},{3,19},{19,3},{4,20},{20... | collective-permute-start | bytes 1572872 | tf_op jit(solution)/shard_map/ppermute | solution.py:161
  130.2 8.4 %collective-permute-start.17 = (bf16[2,2,64,1024]{3,2,1,0:T(8,128)(2,1)S(1)}, bf16[2,2,64,1024]{3,2,1,0:T(8,128)(2,1)}, u32[]{:S(2)}, u32[]{:S(2)}) collective-permute-start(bf16[2,2,64,1024]{3,2,1,0:T(8,128)(2,1)S(1)} %collective-permute-done.15.refs_5_), channel_id=1, source_target_pairs={{0,96},{16,152},{32,0},{48,184},{64,32},{80,216},{96,64},{112,248}... | collective-permute-start | bytes 1572872 | tf_op jit(solution)/shard_map/ppermute | solution.py:157
  135.6 9.6 %collective-permute-start.16 = (bf16[2,2,64,1024]{3,2,1,0:T(8,128)(2,1)S(1)}, bf16[2,2,64,1024]{3,2,1,0:T(8,128)(2,1)}, u32[]{:S(2)}, u32[]{:S(2)}) collective-permute-start(bf16[2,2,64,1024]{3,2,1,0:T(8,128)(2,1)S(1)} %collective-permute-done.12.refs_2_), channel_id=1, source_target_pairs={{0,32},{16,144},{32,64},{48,176},{64,96},{80,208},{96,0},{112,240}... | collective-permute-start | bytes 1572872 | tf_op jit(solution)/shard_map/ppermute | solution.py:157
  136.4 10.9 %collective-permute-start.20 = (bf16[2,2,64,1024]{3,2,1,0:T(8,128)(2,1)S(1)}, bf16[2,2,64,1024]{3,2,1,0:T(8,128)(2,1)}, u32[]{:S(2)}, u32[]{:S(2)}) collective-permute-start(bf16[2,2,64,1024]{3,2,1,0:T(8,128)(2,1)S(1)} %collective-permute-done.12.refs_2_), channel_id=1, source_target_pairs={{0,16},{16,0},{1,17},{17,1},{2,18},{18,2},{3,19},{19,3},{4,20},{20... | collective-permute-start | bytes 1572872 | tf_op jit(solution)/shard_map/ppermute | solution.py:161
  136.8 10.5 %collective-permute-start.21 = (bf16[2,2,64,1024]{3,2,1,0:T(8,128)(2,1)S(1)}, bf16[2,2,64,1024]{3,2,1,0:T(8,128)(2,1)}, u32[]{:S(2)}, u32[]{:S(2)}) collective-permute-start(bf16[2,2,64,1024]{3,2,1,0:T(8,128)(2,1)S(1)} %collective-permute-done.13.refs_3_), channel_id=1, source_target_pairs={{0,16},{16,0},{1,17},{17,1},{2,18},{18,2},{3,19},{19,3},{4,20},{20... | collective-permute-start | bytes 1572872 | tf_op jit(solution)/shard_map/ppermute | solution.py:161
  137.7 9.5 %collective-permute-start.22 = (bf16[2,2,64,1024]{3,2,1,0:T(8,128)(2,1)}, bf16[2,2,64,1024]{3,2,1,0:T(8,128)(2,1)}, u32[]{:S(2)}, u32[]{:S(2)}) collective-permute-start(bf16[2,2,64,1024]{3,2,1,0:T(8,128)(2,1)} %collective-permute-done.14.refs_4_), channel_id=1, source_target_pairs={{0,16},{16,0},{1,17},{17,1},{2,18},{18,2},{3,19},{19,3},{4,20},{20... | collective-permute-start | bytes 1572872 | tf_op jit(solution)/shard_map/ppermute | solution.py:161
  138.7 8.6 %collective-permute-start.25 = (bf16[2,2,64,1024]{3,2,1,0:T(8,128)(2,1)}, bf16[2,2,64,1024]{3,2,1,0:T(8,128)(2,1)}, u32[]{:S(2)}, u32[]{:S(2)}) collective-permute-start(bf16[2,2,64,1024]{3,2,1,0:T(8,128)(2,1)} %collective-permute-done.17.refs_7_), channel_id=1, source_target_pairs={{0,16},{16,0},{1,17},{17,1},{2,18},{18,2},{3,19},{19,3},{4,20},{20... | collective-permute-start | bytes 1572872 | tf_op jit(solution)/shard_map/ppermute | solution.py:161
  (14 other events, 98.3 us)

commit v5 on v4

--- a/solution.py
+++ b/solution.py
@@ -18,7 +18,6 @@
 def theta_kernel(inv_ref, walkers_ref, chol_ref, out_ref):
     blocks, both, padded, width = out_ref.shape
     wdev = walkers_ref.shape[0]
-    occupied = chol_ref.shape[1]
     for k in range(blocks):
         columns = slice(k * width, (k + 1) * width)
         for w in range(wdev):
@@ -28,7 +27,7 @@
             out_ref[k, w] = theta.astype(out_ref.dtype)
         for g in range(both - wdev):
             rows = chol_ref[g, :, columns]
-            rest = jnp.zeros((padded - occupied, width), rows.dtype)
+            rest = jnp.zeros((padded - rows.shape[0], width), rows.dtype)
             out_ref[k, wdev + g] = jnp.concatenate([rows, rest], axis=0)
 
 
@@ -51,15 +50,18 @@
 
 
 def bias_kernel(wdev, both_ref, out_ref):
-    blocks, both, padded, lanes = both_ref.shape
+    blocks, both, occupied, lanes = both_ref.shape
     vdev = both - wdev
     walkers, vectors = blocks * wdev, blocks * vdev
     m, n = walkers * ROWS, vectors * ROWS
     total = jnp.zeros((m, n), jnp.float32)
-    for t in range(padded // ROWS):
-        rows = slice(t * ROWS, (t + 1) * ROWS)
-        a = both_ref[:, :wdev, rows, :].reshape(m, lanes)
-        b = both_ref[:, wdev:, rows, :].reshape(n, lanes)
+    for first in range(0, occupied, ROWS):
+        rows = slice(first, min(first + ROWS, occupied))
+        a, b = both_ref[:, :wdev, rows, :], both_ref[:, wdev:, rows, :]
+        if first + ROWS > occupied:
+            rest = ((0, 0), (0, 0), (0, first + ROWS - occupied), (0, 0))
+            a, b = jnp.pad(a, rest), jnp.pad(b, rest)
+        a, b = a.reshape(m, lanes), b.reshape(n, lanes)
         total = total + lax.dot_general(
             a, b, (((1,), (1,)), ((), ())), preferred_element_type=jnp.float32
         )
@@ -76,7 +78,7 @@
 
 
 def partial_bias(both, wdev):
-    blocks, held, padded, lanes = both.shape
+    blocks, held, occupied, lanes = both.shape
     walkers, vectors = blocks * wdev, blocks * (held - wdev)
     return pl.pallas_call(
         functools.partial(bias_kernel, wdev),
@@ -84,7 +86,7 @@
         in_specs=[pl.BlockSpec(memory_space=pltpu.VMEM)],
         out_specs=pl.BlockSpec(memory_space=pltpu.VMEM),
         cost_estimate=pl.CostEstimate(
-            flops=2 * walkers * vectors * ROWS * padded * lanes,
+            flops=2 * walkers * vectors * ROWS * occupied * lanes,
             bytes_accessed=2 * both.size,
             transcendentals=0,
         ),
@@ -166,11 +168,14 @@
     own = lax.dynamic_slice_in_dim(rows, core * width, width, 1, allow_negative_indices=False)
     given = lax.dynamic_slice_in_dim(rows, (1 - core) * width, width, 1, allow_negative_indices=False)
     own = jnp.stack([own, other_core(given)])
-    came = [own] + [stepped(own, True, -step) for step in AROUND[1:]]
-    near, next_ = jnp.stack(came[:2]), jnp.stack(came[2:])
-    below, above = stepped(near, False, 1), stepped(next_, False, -1)
-    below_next, above_near = stepped(next_, False, 1), stepped(near, False, -1)
-    far = [stepped(below, False, 1), stepped(above, False, -1)]
+    came = [own] + [stepped(own, True, -step) for step in AROUND[1:3]]
+    came.append(stepped(own, True, AROUND[3]))
+    near = jnp.stack(came[:2])
+    below, above_near = stepped(near, False, 1), stepped(near, False, -1)
+    next_ = jnp.stack(came[2:])
+    above, below_next = stepped(next_, False, -1), stepped(next_, False, 1)
+    far = [stepped(below, False, 1)]
+    far.append(stepped(above, False, -1))
     held = [near, next_, below, below_next, above_near, above] + far
     return held + [other_core(array) for array in held]
 
@@ -192,6 +197,32 @@
     )(array)
 
 
+def sum_kernel(scale_ref, *refs):
+    raws, out_ref = refs[:-1], refs[-1]
+    own, halves = raws[0].shape[:2]
+    for h in range(halves):
+        total = None
+        for step, raw in enumerate(raws):
+            for k in range(own):
+                value = scale_ref[step * own + k] * raw[k, h].astype(jnp.float32)
+                total = value if total is None else total + value
+        out_ref[h] = total
+
+
+def scaled_sum(scale, raws):
+    own, *shape = raws[0].shape
+    size = own * math.prod(shape) * len(raws)
+    return pl.pallas_call(
+        sum_kernel,
+        out_shape=jax.ShapeDtypeStruct(tuple(shape), jnp.float32),
+        in_specs=[pl.BlockSpec(memory_space=pltpu.SMEM)]
+        + [pl.BlockSpec(memory_space=pltpu.VMEM)] * len(raws),
+        out_specs=pl.BlockSpec(memory_space=pltpu.VMEM),
+        cost_estimate=pl.CostEstimate(flops=2 * size, bytes_accessed=2 * size, transcendentals=0),
+        compiler_params=pltpu.CompilerParams(vmem_limit_bytes=8 * 1024 * 1024),
+    )(scale, *raws)
+
+
 def at(array, index, dim):
     return lax.dynamic_index_in_dim(array, index, dim, keepdims=False, allow_negative_indices=False)
 
@@ -205,10 +236,9 @@
     occupied = double_rows // 2
     n_blk, n_walk = lax.axis_size(BLK), lax.axis_size(WALK)
     n_all = n_blk * n_walk
-    padded = -(-occupied // ROWS) * ROWS
 
     inv = jnp.moveaxis(inv_intersection, 1, 2).reshape(wdev, occupied, double_rows)
-    inv = jnp.pad(inv, ((0, 0), (0, padded - occupied), (0, 0)))
+    inv = jnp.pad(inv, ((0, 0), (0, -occupied % 8), (0, 0)))
     both = theta_and_chol(inv, walkers, rotated_chol, n_blk)
     both = exchanged(both, BLK)
     own = full_chol.shape[0]
@@ -234,26 +264,24 @@
     rows = jnp.pad(rows, ((0, 0), (0, 128 - rows.shape[1])))
     rows = jnp.broadcast_to(rows[:, None, None], (n_blk, n_walk, 1, 128))
     core = lax.axis_index("blk_2")
-    rows, half, at_z, core = lax.optimization_barrier((rows, half, at_z, core))
-    rows = exchanged(rows.reshape(n_all, 1, 128), ALL)
-    rows, half, at_z, core = lax.optimization_barrier((rows, half, at_z, core))
-    rows = rows.reshape(n_blk, n_walk, 128)
-    bias_shift = jnp.sum(rows, axis=(0, 1))[:vectors] / math.sqrt(wdev * n_all)
-    peers = at(rows, half * n_z + at_z, 1)
-    bias = jnp.sum(peers, axis=0)[vectors : vectors + wdev * vectors].reshape(wdev, vectors)
-
-    shifted = 0.1 * (field_noise - bias_shift)
     entry = lax.broadcasted_iota(jnp.int32, (n_z * own, vectors), 0)
     vector = lax.broadcasted_iota(jnp.int32, (n_z * own, vectors), 1)
     source = at_z - entry // own
     source = jnp.where(source < 0, source + n_z, source)
     wanted = (half * n_z + source) * own + entry % own
-    scale = jnp.sum(jnp.where(vector == wanted, shifted[None, :], 0.0), axis=1)
-    part_field = sum(
-        scale[step * own + k] * raws[step][k].astype(jnp.float32)
-        for step in range(n_z)
-        for k in range(own)
-    )
+    ids = (half, at_z, core, vector == wanted)
+    rows, (half, at_z, core, picked) = lax.optimization_barrier((rows, ids))
+    rows = exchanged(rows.reshape(n_all, 1, 128), ALL)
+    ids = (half, at_z, core, picked)
+    rows, (half, at_z, core, picked) = lax.optimization_barrier((rows, ids))
+    rows = rows.reshape(n_blk, n_walk, 128)
+    bias_shift = jnp.sum(rows, axis=(0, 1))[:vectors] / math.sqrt(wdev * n_all)
+    peers = at(rows, half * n_z + at_z, 1)
+    bias = jnp.sum(peers, axis=0)[vectors : vectors + wdev * vectors].reshape(wdev, vectors)
+
+    shifted = 0.1 * (field_noise - bias_shift)
+    scale = jnp.sum(jnp.where(picked, shifted[None, :], 0.0), axis=1)
+    part_field = scaled_sum(scale, raws)
     kept = at(part_field, half, 0)
     given = at(part_field, 1 - half, 0)
     came = lax.ppermute(given, "walk_0", [(0, 1), (1, 0)])

time: 171 us -> 176 us (1.029)
  waiting for transfers between devices: 61 us -> 77 us
  other arithmetic: 11.4 us -> 1.29 us
  local copies, waits for them, and re-layouts: 12.6 us -> 9.89 us
  Pallas kernels: 5.56 us -> 7.6 us
    ppermute x7, waiting for transfers between devices: 1.44 us -> 19 us  [part(): raws.append(lax.ppermute(rows, 'walk_1', pairs))]
    add x1 -> x0, other arithmetic: 10.1 us -> none  [part(): sum((scale[step * own + k] * raws[step][k].astype(jnp.float32) for step i...]
    ppermute x9, starting transfers between devices: 10.6 us -> 14.7 us  [other_core(): return lax.ppermute(array, 'blk_2', [(0, 1), (1, 0)])]
    ppermute x7, starting transfers between devices: 16.4 us -> 12.9 us  [part(): raws.append(lax.ppermute(rows, 'walk_1', pairs))]
    ppermute x9, waiting for transfers between devices: 23 us -> 20.2 us  [stepped(): return lax.ppermute(array, CHIP, pairs)]
    all_to_all x3, waiting for transfers between devices: 31.9 us -> 33.8 us  [exchanged(): return lax.all_to_all(blocks, axes, split_axis=0, concat_axis=0, tiled=True)]
    unnamed x19 -> x17, local copies, waits for them, and re-layouts: 7.76 us -> 6.53 us
  transfers between devices with their start and end apart: 29 -> 29, of which waited for: 14 -> 16; matrix products, arithmetic and copies ran while one was open for 3% -> 1% of each run, Pallas kernels for 1% -> 0%
where the time goes in v5:
time: 176 us
  waiting for transfers between devices  77 us (44%)
  starting transfers between devices  63 us (36%)
  matrix products  15.9 us (9%)
  local copies, waits for them, and re-layouts  9.89 us (6%)
  Pallas kernels  7.6 us (4%)
    all_to_all x3, waiting for transfers between devices, exchanged(): return lax.all_to_all(blocks, axes, split_axis=0, concat_axis=0, tiled=True)  33.8 us
    all_to_all x3, starting transfers between devices, exchanged(): return lax.all_to_all(blocks, axes, split_axis=0, concat_axis=0, tiled=True)  25 us
    ppermute x9, waiting for transfers between devices, stepped(): return lax.ppermute(array, CHIP, pairs)  20.2 us
    ppermute x7, waiting for transfers between devices, part(): raws.append(lax.ppermute(rows, 'walk_1', pairs))  19 us
    dot_general x4, matrix products, part(): jnp.dot(current, field, preferred_element_type=jnp.float32) / order  15.9 us
    ppermute x9, starting transfers between devices, other_core(): return lax.ppermute(array, 'blk_2', [(0, 1), (1, 0)])  14.7 us
    ppermute x7, starting transfers between devices, part(): raws.append(lax.ppermute(rows, 'walk_1', pairs))  12.9 us
    ppermute x9, starting transfers between devices, stepped(): return lax.ppermute(array, CHIP, pairs)  7.61 us
  transfers between devices with their start and end apart: 29, of which 16 were waited for; matrix products, arithmetic and copies ran while one was open for 1% of the time, Pallas kernels for 0%

profile of v5, /device:TPU:1, one launch (start us, length us, event | category | flops | bytes accessed | tf_op | source)
XLA Modules:
  0.0 175.6 jit_solution(7479217866620339470)
XLA Ops:
  6.5 7.0 %all-to-all-start = ((bf16[16,4,104,128]{3,2,1,0:T(8,128)(2,1)}), bf16[16,4,104,128]{3,2,1,0:T(8,128)(2,1)S(1)}, u32[]{:S(2)}, u32[]{:S(2)}) async-start(bf16[16,4,104,128]{3,2,1,0:T(8,128)(2,1)} %shard_map.76), calls=%async_computation | async-start | bytes 3407872 | tf_op jit(solution)/shard_map/all_to_all | solution.py:231
  13.7 22.8 %all-to-all-done.both_ref = bf16[16,4,104,128]{3,2,1,0:T(8,128)(2,1)S(1)} async-done(((bf16[16,4,104,128]{3,2,1,0:T(8,128)(2,1)}), bf16[16,4,104,128]{3,2,1,0:T(8,128)(2,1)S(1)}, u32[]{:S(2)}, u32[]{:S(2)}) %all-to-all-start) | async-done | bytes 1703968 | tf_op jit(solution)/shard_map/all_to_all | solution.py:231
  38.8 14.2 %all-to-all-start.1 = ((f32[256,1,128]{2,1,0:T(1,128)}), f32[256,1,128]{2,1,0:T(1,128)S(1)}, u32[]{:S(2)}, u32[]{:S(2)}) async-start(f32[256,1,128]{2,1,0:T(1,128)} %bitcast.2), calls=%async_computation.1 | async-start | bytes 262144 | tf_op jit(solution)/shard_map/all_to_all | solution.py:231
  53.1 4.4 %collective-permute-start.6 = (bf16[2,2,8,2048]{3,2,1,0:T(8,128)(2,1)S(1)}, bf16[2,2,8,2048]{3,2,1,0:T(8,128)(2,1)S(1)}, u32[]{:S(2)}, u32[]{:S(2)}) collective-permute-start(bf16[2,2,8,2048]{3,2,1,0:T(8,128)(2,1)S(1)} %get-tuple-element.25), channel_id=1, source_target_pairs={{0,7},{1,0},{2,1},{3,2},{4,3},{5,4},{6,5},{7,6},{8,15},{9,8},{10,9... | collective-permute-start | bytes 393224 | tf_op jit(solution)/shard_map/ppermute | solution.py:256
  59.7 4.1 %collective-permute-start.3 = (bf16[2,2,8,2048]{3,2,1,0:T(8,128)(2,1)S(1)}, bf16[2,2,8,2048]{3,2,1,0:T(8,128)(2,1)S(1)}, u32[]{:S(2)}, u32[]{:S(2)}) collective-permute-start(bf16[2,2,8,2048]{3,2,1,0:T(8,128)(2,1)S(1)} %get-tuple-element.28), channel_id=1, source_target_pairs={{0,4},{1,5},{2,6},{3,7},{4,0},{5,1},{6,2},{7,3},{8,12},{9,13},{10,... | collective-permute-start | bytes 393224 | tf_op jit(solution)/shard_map/ppermute | solution.py:256
  68.7 4.8 %collective-permute-done.4.refs_5_ = bf16[2,2,8,2048]{3,2,1,0:T(8,128)(2,1)S(1)} collective-permute-done((bf16[2,2,8,2048]{3,2,1,0:T(8,128)(2,1)S(1)}, bf16[2,2,8,2048]{3,2,1,0:T(8,128)(2,1)S(1)}, u32[]{:S(2)}, u32[]{:S(2)}) %collective-permute-start.4) | collective-permute-done | bytes 131104 | tf_op jit(solution)/shard_map/ppermute | solution.py:256
  73.6 6.3 %collective-permute-done.2.refs_3_ = bf16[2,2,8,2048]{3,2,1,0:T(8,128)(2,1)S(1)} collective-permute-done((bf16[2,2,8,2048]{3,2,1,0:T(8,128)(2,1)S(1)}, bf16[2,2,8,2048]{3,2,1,0:T(8,128)(2,1)S(1)}, u32[]{:S(2)}, u32[]{:S(2)}) %collective-permute-start.2) | collective-permute-done | bytes 131104 | tf_op jit(solution)/shard_map/ppermute | solution.py:256
  79.9 2.4 %collective-permute-done.1.refs_2_ = bf16[2,2,8,2048]{3,2,1,0:T(8,128)(2,1)S(1)} collective-permute-done((bf16[2,2,8,2048]{3,2,1,0:T(8,128)(2,1)S(1)}, bf16[2,2,8,2048]{3,2,1,0:T(8,128)(2,1)S(1)}, u32[]{:S(2)}, u32[]{:S(2)}) %collective-permute-start.1) | collective-permute-done | bytes 131104 | tf_op jit(solution)/shard_map/ppermute | solution.py:256
  82.3 5.4 %collective-permute-done.refs_1_ = bf16[2,2,8,2048]{3,2,1,0:T(8,128)(2,1)S(1)} collective-permute-done((bf16[2,2,8,2048]{3,2,1,0:T(8,128)(2,1)S(1)}, bf16[2,2,8,2048]{3,2,1,0:T(8,128)(2,1)S(1)}, u32[]{:S(2)}, u32[]{:S(2)}) %collective-permute-start) | collective-permute-done | bytes 131104 | tf_op jit(solution)/shard_map/ppermute | solution.py:256
  88.5 2.9 %collective-permute-start.7 = (f32[8,2048]{1,0:T(8,128)S(1)}, f32[8,2048]{1,0:T(8,128)S(1)}, u32[]{:S(2)}, u32[]{:S(2)}) collective-permute-start(f32[8,2048]{1,0:T(8,128)S(1)} %dynamic-slice_bitcast_fusion.9), channel_id=1, source_target_pairs={{0,8},{8,0},{1,9},{9,1},{2,10},{10,2},{3,11},{11,3},{4,12},{12,4},... | collective-permute-start | bytes 196616 | tf_op jit(solution)/shard_map/ppermute | solution.py:287
  94.0 3.7 %all-to-all-start.2 = ((bf16[8,8,2048]{2,1,0:T(8,128)(2,1)}), bf16[8,8,2048]{2,1,0:T(8,128)(2,1)S(1)}, u32[]{:S(2)}, u32[]{:S(2)}) async-start(bf16[8,8,2048]{2,1,0:T(8,128)(2,1)} %broadcast_in_dim.32), calls=%async_computation.2 | async-start | bytes 524288 | tf_op jit(solution)/shard_map/all_to_all | solution.py:231
  97.7 9.3 %all-to-all-done.2 = bf16[8,8,2048]{2,1,0:T(8,128)(2,1)S(1)} async-done(((bf16[8,8,2048]{2,1,0:T(8,128)(2,1)}), bf16[8,8,2048]{2,1,0:T(8,128)(2,1)S(1)}, u32[]{:S(2)}, u32[]{:S(2)}) %all-to-all-start.2) | async-done | bytes 262176 | tf_op jit(solution)/shard_map/all_to_all | solution.py:231
  107.0 3.7 %collective-permute-start.8 = (bf16[64,1024]{1,0:T(8,128)(2,1)S(1)}, bf16[64,1024]{1,0:T(8,128)(2,1)S(1)}, u32[]{:S(2)}, u32[]{:S(2)}) collective-permute-start(bf16[64,1024]{1,0:T(8,128)(2,1)S(1)} %get-tuple-element.36), channel_id=1, source_target_pairs={{0,16},{16,0},{1,17},{17,1},{2,18},{18,2},{3,19},{19,3},{4,20},{20... | collective-permute-start | bytes 393224 | tf_op jit(solution)/shard_map/ppermute | solution.py:163
  111.7 2.5 %collective-permute-start.10 = (bf16[2,64,1024]{2,1,0:T(8,128)(2,1)S(1)}, bf16[2,64,1024]{2,1,0:T(8,128)(2,1)S(1)}, u32[]{:S(2)}, u32[]{:S(2)}) collective-permute-start(bf16[2,64,1024]{2,1,0:T(8,128)(2,1)S(1)} %get-tuple-element.34), channel_id=1, source_target_pairs={{0,136},{16,112},{32,168},{48,16},{64,200},{80,48},{96,232},{112,8... | collective-permute-start | bytes 786440 | tf_op jit(solution)/shard_map/ppermute | solution.py:159
  115.2 5.0 %collective-permute-done.10 = bf16[2,64,1024]{2,1,0:T(8,128)(2,1)S(1)} collective-permute-done((bf16[2,64,1024]{2,1,0:T(8,128)(2,1)S(1)}, bf16[2,64,1024]{2,1,0:T(8,128)(2,1)S(1)}, u32[]{:S(2)}, u32[]{:S(2)}) %collective-permute-start.10) | collective-permute-done | bytes 262176 | tf_op jit(solution)/shard_map/ppermute | solution.py:159
  128.7 2.4 %collective-permute-done.15.refs_5_ = bf16[2,2,64,1024]{3,2,1,0:T(8,128)(2,1)S(1)} collective-permute-done((bf16[2,2,64,1024]{3,2,1,0:T(8,128)(2,1)S(1)}, bf16[2,2,64,1024]{3,2,1,0:T(8,128)(2,1)S(1)}, u32[]{:S(2)}, u32[]{:S(2)}) %collective-permute-start.15) | collective-permute-done | bytes 524320 | tf_op jit(solution)/shard_map/ppermute | solution.py:159
  134.5 5.5 %collective-permute-done.12.refs_2_ = bf16[2,2,64,1024]{3,2,1,0:T(8,128)(2,1)S(1)} collective-permute-done((bf16[2,2,64,1024]{3,2,1,0:T(8,128)(2,1)S(1)}, bf16[2,2,64,1024]{3,2,1,0:T(8,128)(2,1)S(1)}, u32[]{:S(2)}, u32[]{:S(2)}) %collective-permute-start.12) | collective-permute-done | bytes 524320 | tf_op jit(solution)/shard_map/ppermute | solution.py:159
  145.4 4.3 %collective-permute-done.16.refs_6_ = bf16[2,2,64,1024]{3,2,1,0:T(8,128)(2,1)} collective-permute-done((bf16[2,2,64,1024]{3,2,1,0:T(8,128)(2,1)S(1)}, bf16[2,2,64,1024]{3,2,1,0:T(8,128)(2,1)}, u32[]{:S(2)}, u32[]{:S(2)}) %collective-permute-start.16) | collective-permute-done | bytes 524320 | tf_op jit(solution)/shard_map/ppermute | solution.py:159
  149.7 2.5 %collective-permute-start.24 = (bf16[2,2,64,1024]{3,2,1,0:T(8,128)(2,1)}, bf16[2,2,64,1024]{3,2,1,0:T(8,128)(2,1)}, u32[]{:S(2)}, u32[]{:S(2)}) collective-permute-start(bf16[2,2,64,1024]{3,2,1,0:T(8,128)(2,1)} %collective-permute-done.16.refs_6_), channel_id=1, source_target_pairs={{0,16},{16,0},{1,17},{17,1},{2,18},{18,2},{3,19},{19,3},{4,20},{20... | collective-permute-start | bytes 1572872 | tf_op jit(solution)/shard_map/ppermute | solution.py:163
  156.2 3.5 %shard_map.80 = bf16[2048,2048]{1,0:T(8,128)(2,1)S(1)} custom-call(bf16[2,2,64,1024]{3,2,1,0:T(8,128)(2,1)S(1)} %pad_maximum_fusion.refs_0_, bf16[2,2,64,1024]{3,2,1,0:T(8,128)(2,1)S(1)} %pad_maximum_fusion.1.refs_1_, bf16[2,2,64,1024]{3,2,1,0:T(8,128)(2,1)S(1)} %collective-permute-done.12.refs_2_, ...), custom_call_target="tpu_custom_call" | custom-call | flops 4194304 | bytes 16777216 | tf_op jit(solution)/shard_map/pallas_call | solution.py:132
  159.6 3.6 %convolution_convert_fusion = bf16[2048,400]{0,1:T(8,128)(2,1)S(1)} fusion(bf16[400,2048]{1,0:T(8,128)(2,1)S(1)} %bitcast.71, bf16[2048,2048]{1,0:T(8,128)(2,1)S(1)} %shard_map.80), kind=kOutput, calls=%fused_computation.8 | convolution fusion | flops 3356262400 | bytes 11665408 | tf_op jit(solution)/shard_map/dot_general | solution.py:294
  163.3 3.6 %multiply_convert_fusion.2 = bf16[400,2048]{1,0:T(8,128)(2,1)S(1)} fusion(bf16[2048,400]{0,1:T(8,128)(2,1)S(1)} %convolution_convert_fusion, bf16[2048,2048]{1,0:T(8,128)(2,1)S(1)} %shard_map.80), kind=kOutput, calls=%fused_computation.7 | convolution fusion | flops 3357081600 | bytes 11665408 | tf_op jit(solution)/shard_map/dot_general | solution.py:294
  166.9 3.6 %multiply_convert_fusion.1 = bf16[400,2048]{1,0:T(8,128)(2,1)S(1)} fusion(bf16[400,2048]{1,0:T(8,128)(2,1)S(1)} %multiply_convert_fusion.2, bf16[2048,2048]{1,0:T(8,128)(2,1)S(1)} %shard_map.80), kind=kOutput, calls=%fused_computation.6 | convolution fusion | flops 3357081600 | bytes 11665408 | tf_op jit(solution)/shard_map/dot_general | solution.py:294
  170.5 5.1 %fusion.3 = bf16[400,2048]{1,0:T(8,128)(2,1)} fusion(bf16[2048,400]{0,1:T(8,128)(2,1)S(1)} %convolution_convert_fusion, bf16[400,2048]{1,0:T(8,128)(2,1)S(1)} %multiply_convert_fusion.1, bf16[400,2048]{1,0:T(8,128)(2,1)S(1)} %multiply_convert_fusion.2, bf16[400,2048]{1,0:T(8,128)(2,1)S(1)} %bitcast.72, bf16[2048,2048]{1,0:T(8,128)(2,1)S(1)} %shard_map.80), kind=kOutput, calls=%fused_computation.4 | convolution fusion | flops 3365273600 | bytes 16580608 | tf_op jit(solution)/shard_map/dot_general | solution.py:294
  (86 shorter events, 42.1 us)
Async XLA Ops:
  6.5 30.0 %all-to-all-start = ((bf16[16,4,104,128]{3,2,1,0:T(8,128)(2,1)}), bf16[16,4,104,128]{3,2,1,0:T(8,128)(2,1)S(1)}, u32[]{:S(2)}, u32[]{:S(2)}) async-start(bf16[16,4,104,128]{3,2,1,0:T(8,128)(2,1)} %shard_map.76), calls=%async_computation | async-start | bytes 3407872 | tf_op jit(solution)/shard_map/all_to_all | solution.py:231
  38.8 26.9 %all-to-all-start.1 = ((f32[256,1,128]{2,1,0:T(1,128)}), f32[256,1,128]{2,1,0:T(1,128)S(1)}, u32[]{:S(2)}, u32[]{:S(2)}) async-start(f32[256,1,128]{2,1,0:T(1,128)} %bitcast.2), calls=%async_computation.1 | async-start | bytes 262144 | tf_op jit(solution)/shard_map/all_to_all | solution.py:231
  53.1 12.8 %collective-permute-start.6 = (bf16[2,2,8,2048]{3,2,1,0:T(8,128)(2,1)S(1)}, bf16[2,2,8,2048]{3,2,1,0:T(8,128)(2,1)S(1)}, u32[]{:S(2)}, u32[]{:S(2)}) collective-permute-start(bf16[2,2,8,2048]{3,2,1,0:T(8,128)(2,1)S(1)} %get-tuple-element.25), channel_id=1, source_target_pairs={{0,7},{1,0},{2,1},{3,2},{4,3},{5,4},{6,5},{7,6},{8,15},{9,8},{10,9... | collective-permute-start | bytes 393224 | tf_op jit(solution)/shard_map/ppermute | solution.py:256
  57.5 9.7 %collective-permute-start.5 = (bf16[2,2,8,2048]{3,2,1,0:T(8,128)(2,1)S(1)}, bf16[2,2,8,2048]{3,2,1,0:T(8,128)(2,1)S(1)}, u32[]{:S(2)}, u32[]{:S(2)}) collective-permute-start(bf16[2,2,8,2048]{3,2,1,0:T(8,128)(2,1)S(1)} %get-tuple-element.26), channel_id=1, source_target_pairs={{0,6},{1,7},{2,0},{3,1},{4,2},{5,3},{6,4},{7,5},{8,14},{9,15},{10,... | collective-permute-start | bytes 393224 | tf_op jit(solution)/shard_map/ppermute | solution.py:256
  59.1 14.5 %collective-permute-start.4 = (bf16[2,2,8,2048]{3,2,1,0:T(8,128)(2,1)S(1)}, bf16[2,2,8,2048]{3,2,1,0:T(8,128)(2,1)S(1)}, u32[]{:S(2)}, u32[]{:S(2)}) collective-permute-start(bf16[2,2,8,2048]{3,2,1,0:T(8,128)(2,1)S(1)} %get-tuple-element.27), channel_id=1, source_target_pairs={{0,5},{1,6},{2,7},{3,0},{4,1},{5,2},{6,3},{7,4},{8,13},{9,14},{10,... | collective-permute-start | bytes 393224 | tf_op jit(solution)/shard_map/ppermute | solution.py:256
  59.7 13.9 %collective-permute-start.3 = (bf16[2,2,8,2048]{3,2,1,0:T(8,128)(2,1)S(1)}, bf16[2,2,8,2048]{3,2,1,0:T(8,128)(2,1)S(1)}, u32[]{:S(2)}, u32[]{:S(2)}) collective-permute-start(bf16[2,2,8,2048]{3,2,1,0:T(8,128)(2,1)S(1)} %get-tuple-element.28), channel_id=1, source_target_pairs={{0,4},{1,5},{2,6},{3,7},{4,0},{5,1},{6,2},{7,3},{8,12},{9,13},{10,... | collective-permute-start | bytes 393224 | tf_op jit(solution)/shard_map/ppermute | solution.py:256
  63.8 16.0 %collective-permute-start.2 = (bf16[2,2,8,2048]{3,2,1,0:T(8,128)(2,1)S(1)}, bf16[2,2,8,2048]{3,2,1,0:T(8,128)(2,1)S(1)}, u32[]{:S(2)}, u32[]{:S(2)}) collective-permute-start(bf16[2,2,8,2048]{3,2,1,0:T(8,128)(2,1)S(1)} %get-tuple-element.29), channel_id=1, source_target_pairs={{0,3},{1,4},{2,5},{3,6},{4,7},{5,0},{6,1},{7,2},{8,11},{9,12},{10,... | collective-permute-start | bytes 393224 | tf_op jit(solution)/shard_map/ppermute | solution.py:256
  65.9 16.4 %collective-permute-start.1 = (bf16[2,2,8,2048]{3,2,1,0:T(8,128)(2,1)S(1)}, bf16[2,2,8,2048]{3,2,1,0:T(8,128)(2,1)S(1)}, u32[]{:S(2)}, u32[]{:S(2)}) collective-permute-start(bf16[2,2,8,2048]{3,2,1,0:T(8,128)(2,1)S(1)} %get-tuple-element.30), channel_id=1, source_target_pairs={{0,2},{1,3},{2,4},{3,5},{4,6},{5,7},{6,0},{7,1},{8,10},{9,11},{10,... | collective-permute-start | bytes 393224 | tf_op jit(solution)/shard_map/ppermute | solution.py:256
  67.2 20.5 %collective-permute-start = (bf16[2,2,8,2048]{3,2,1,0:T(8,128)(2,1)S(1)}, bf16[2,2,8,2048]{3,2,1,0:T(8,128)(2,1)S(1)}, u32[]{:S(2)}, u32[]{:S(2)}) collective-permute-start(bf16[2,2,8,2048]{3,2,1,0:T(8,128)(2,1)S(1)} %get-tuple-element.31), channel_id=1, source_target_pairs={{0,1},{1,2},{2,3},{3,4},{4,5},{5,6},{6,7},{7,0},{8,9},{9,10},{10,1... | collective-permute-start | bytes 393224 | tf_op jit(solution)/shard_map/ppermute | solution.py:256
  94.0 13.0 %all-to-all-start.2 = ((bf16[8,8,2048]{2,1,0:T(8,128)(2,1)}), bf16[8,8,2048]{2,1,0:T(8,128)(2,1)S(1)}, u32[]{:S(2)}, u32[]{:S(2)}) async-start(bf16[8,8,2048]{2,1,0:T(8,128)(2,1)} %broadcast_in_dim.32), calls=%async_computation.2 | async-start | bytes 524288 | tf_op jit(solution)/shard_map/all_to_all | solution.py:231
  111.7 8.6 %collective-permute-start.10 = (bf16[2,64,1024]{2,1,0:T(8,128)(2,1)S(1)}, bf16[2,64,1024]{2,1,0:T(8,128)(2,1)S(1)}, u32[]{:S(2)}, u32[]{:S(2)}) collective-permute-start(bf16[2,64,1024]{2,1,0:T(8,128)(2,1)S(1)} %get-tuple-element.34), channel_id=1, source_target_pairs={{0,136},{16,112},{32,168},{48,16},{64,200},{80,48},{96,232},{112,8... | collective-permute-start | bytes 786440 | tf_op jit(solution)/shard_map/ppermute | solution.py:159
  114.6 10.2 %collective-permute-start.9 = (bf16[2,64,1024]{2,1,0:T(8,128)(2,1)S(1)}, bf16[2,64,1024]{2,1,0:T(8,128)(2,1)S(1)}, u32[]{:S(2)}, u32[]{:S(2)}) collective-permute-start(bf16[2,64,1024]{2,1,0:T(8,128)(2,1)S(1)} %get-tuple-element.34), channel_id=1, source_target_pairs={{0,128},{16,48},{32,160},{48,80},{64,192},{80,112},{96,224},{112,1... | collective-permute-start | bytes 786440 | tf_op jit(solution)/shard_map/ppermute | solution.py:159
  122.7 8.3 %collective-permute-start.15 = (bf16[2,2,64,1024]{3,2,1,0:T(8,128)(2,1)S(1)}, bf16[2,2,64,1024]{3,2,1,0:T(8,128)(2,1)S(1)}, u32[]{:S(2)}, u32[]{:S(2)}) collective-permute-start(bf16[2,2,64,1024]{3,2,1,0:T(8,128)(2,1)S(1)} %pad_maximum_fusion.1.refs_1_), channel_id=1, source_target_pairs={{0,96},{16,152},{32,0},{48,184},{64,32},{80,216},{96,64},{112,248}... | collective-permute-start | bytes 1572872 | tf_op jit(solution)/shard_map/ppermute | solution.py:159
  124.9 9.5 %collective-permute-start.13 = (bf16[2,2,64,1024]{3,2,1,0:T(8,128)(2,1)S(1)}, bf16[2,2,64,1024]{3,2,1,0:T(8,128)(2,1)S(1)}, u32[]{:S(2)}, u32[]{:S(2)}) collective-permute-start(bf16[2,2,64,1024]{3,2,1,0:T(8,128)(2,1)S(1)} %pad_maximum_fusion.1.refs_1_), channel_id=1, source_target_pairs={{0,32},{16,144},{32,64},{48,176},{64,96},{80,208},{96,0},{112,240}... | collective-permute-start | bytes 1572872 | tf_op jit(solution)/shard_map/ppermute | solution.py:159
  124.9 15.1 %collective-permute-start.12 = (bf16[2,2,64,1024]{3,2,1,0:T(8,128)(2,1)S(1)}, bf16[2,2,64,1024]{3,2,1,0:T(8,128)(2,1)S(1)}, u32[]{:S(2)}, u32[]{:S(2)}) collective-permute-start(bf16[2,2,64,1024]{3,2,1,0:T(8,128)(2,1)S(1)} %pad_maximum_fusion.refs_0_), channel_id=1, source_target_pairs={{0,32},{16,144},{32,64},{48,176},{64,96},{80,208},{96,0},{112,240}... | collective-permute-start | bytes 1572872 | tf_op jit(solution)/shard_map/ppermute | solution.py:159
  125.0 15.0 %collective-permute-start.18 = (bf16[2,2,64,1024]{3,2,1,0:T(8,128)(2,1)S(1)}, bf16[2,2,64,1024]{3,2,1,0:T(8,128)(2,1)S(1)}, u32[]{:S(2)}, u32[]{:S(2)}) collective-permute-start(bf16[2,2,64,1024]{3,2,1,0:T(8,128)(2,1)S(1)} %pad_maximum_fusion.refs_0_), channel_id=1, source_target_pairs={{0,16},{16,0},{1,17},{17,1},{2,18},{18,2},{3,19},{19,3},{4,20},{20... | collective-permute-start | bytes 1572872 | tf_op jit(solution)/shard_map/ppermute | solution.py:163
  127.0 15.5 %collective-permute-start.14 = (bf16[2,2,64,1024]{3,2,1,0:T(8,128)(2,1)S(1)}, bf16[2,2,64,1024]{3,2,1,0:T(8,128)(2,1)}, u32[]{:S(2)}, u32[]{:S(2)}) collective-permute-start(bf16[2,2,64,1024]{3,2,1,0:T(8,128)(2,1)S(1)} %pad_maximum_fusion.refs_0_), channel_id=1, source_target_pairs={{0,96},{16,152},{32,0},{48,184},{64,32},{80,216},{96,64},{112,248}... | collective-permute-start | bytes 1572872 | tf_op jit(solution)/shard_map/ppermute | solution.py:159
  131.1 11.5 %collective-permute-start.23 = (bf16[2,2,64,1024]{3,2,1,0:T(8,128)(2,1)S(1)}, bf16[2,2,64,1024]{3,2,1,0:T(8,128)(2,1)S(1)}, u32[]{:S(2)}, u32[]{:S(2)}) collective-permute-start(bf16[2,2,64,1024]{3,2,1,0:T(8,128)(2,1)S(1)} %collective-permute-done.15.refs_5_), channel_id=1, source_target_pairs={{0,16},{16,0},{1,17},{17,1},{2,18},{18,2},{3,19},{19,3},{4,20},{20... | collective-permute-start | bytes 1572872 | tf_op jit(solution)/shard_map/ppermute | solution.py:163
  134.4 9.4 %collective-permute-start.17 = (bf16[2,2,64,1024]{3,2,1,0:T(8,128)(2,1)S(1)}, bf16[2,2,64,1024]{3,2,1,0:T(8,128)(2,1)}, u32[]{:S(2)}, u32[]{:S(2)}) collective-permute-start(bf16[2,2,64,1024]{3,2,1,0:T(8,128)(2,1)S(1)} %collective-permute-done.15.refs_5_), channel_id=1, source_target_pairs={{0,96},{16,152},{32,0},{48,184},{64,32},{80,216},{96,64},{112,248}... | collective-permute-start | bytes 1572872 | tf_op jit(solution)/shard_map/ppermute | solution.py:159
  140.0 9.6 %collective-permute-start.16 = (bf16[2,2,64,1024]{3,2,1,0:T(8,128)(2,1)S(1)}, bf16[2,2,64,1024]{3,2,1,0:T(8,128)(2,1)}, u32[]{:S(2)}, u32[]{:S(2)}) collective-permute-start(bf16[2,2,64,1024]{3,2,1,0:T(8,128)(2,1)S(1)} %collective-permute-done.12.refs_2_), channel_id=1, source_target_pairs={{0,32},{16,144},{32,64},{48,176},{64,96},{80,208},{96,0},{112,240}... | collective-permute-start | bytes 1572872 | tf_op jit(solution)/shard_map/ppermute | solution.py:159
  140.8 12.1 %collective-permute-start.20 = (bf16[2,2,64,1024]{3,2,1,0:T(8,128)(2,1)S(1)}, bf16[2,2,64,1024]{3,2,1,0:T(8,128)(2,1)}, u32[]{:S(2)}, u32[]{:S(2)}) collective-permute-start(bf16[2,2,64,1024]{3,2,1,0:T(8,128)(2,1)S(1)} %collective-permute-done.12.refs_2_), channel_id=1, source_target_pairs={{0,16},{16,0},{1,17},{17,1},{2,18},{18,2},{3,19},{19,3},{4,20},{20... | collective-permute-start | bytes 1572872 | tf_op jit(solution)/shard_map/ppermute | solution.py:163
  142.5 10.5 %collective-permute-start.21 = (bf16[2,2,64,1024]{3,2,1,0:T(8,128)(2,1)S(1)}, bf16[2,2,64,1024]{3,2,1,0:T(8,128)(2,1)}, u32[]{:S(2)}, u32[]{:S(2)}) collective-permute-start(bf16[2,2,64,1024]{3,2,1,0:T(8,128)(2,1)S(1)} %collective-permute-done.13.refs_3_), channel_id=1, source_target_pairs={{0,16},{16,0},{1,17},{17,1},{2,18},{18,2},{3,19},{19,3},{4,20},{20... | collective-permute-start | bytes 1572872 | tf_op jit(solution)/shard_map/ppermute | solution.py:163
  143.3 9.6 %collective-permute-start.22 = (bf16[2,2,64,1024]{3,2,1,0:T(8,128)(2,1)}, bf16[2,2,64,1024]{3,2,1,0:T(8,128)(2,1)}, u32[]{:S(2)}, u32[]{:S(2)}) collective-permute-start(bf16[2,2,64,1024]{3,2,1,0:T(8,128)(2,1)} %collective-permute-done.14.refs_4_), channel_id=1, source_target_pairs={{0,16},{16,0},{1,17},{17,1},{2,18},{18,2},{3,19},{19,3},{4,20},{20... | collective-permute-start | bytes 1572872 | tf_op jit(solution)/shard_map/ppermute | solution.py:163
  143.8 9.1 %collective-permute-start.25 = (bf16[2,2,64,1024]{3,2,1,0:T(8,128)(2,1)}, bf16[2,2,64,1024]{3,2,1,0:T(8,128)(2,1)}, u32[]{:S(2)}, u32[]{:S(2)}) collective-permute-start(bf16[2,2,64,1024]{3,2,1,0:T(8,128)(2,1)} %collective-permute-done.17.refs_7_), channel_id=1, source_target_pairs={{0,16},{16,0},{1,17},{17,1},{2,18},{18,2},{3,19},{19,3},{4,20},{20... | collective-permute-start | bytes 1572872 | tf_op jit(solution)/shard_map/ppermute | solution.py:163
  (13 other events, 139.5 us)
